TPU v7x, 32 devices: a whole 2x2x4 slice. The times are simulated.
32 devices in a mesh: grp: 4 (over y, x), blk: 8 (over z, core).
Axes of the slice: x: 2, y: 2, z: 4, core: 2. Of those that a mesh axis runs over, the one named last changes fastest.
Arguments:
- data: bfloat16 [256, 65536], P('blk'), may hold values from -8 to 8
- labels: int32 [256], P('blk'), may hold values from -1 to 1, as said below
- order: int32 [8, 4], P('blk'), may hold values from 0 to 3, each once within a row
- reg_index: int32 [4], P('grp'), parts along dimension 0, may hold values from 0 to 5
Outputs:
- dual: float32 [1024], P(('grp', 'blk')), parts along dimension 0
- margins: float32 [1024], P(('grp', 'blk')), parts along dimension 0
- gap: float32 [4], P('grp'), parts along dimension 0
There are 4 independent parts, one for each index of `grp`. A program takes and returns all parts, laid end to end along the dimension named above; an argument that names none is the same for every part. Nothing has to cross between parts.
Inputs may be any that keep to these rules, and one draw needn't show every extreme that they name: `labels`: each entry is -1 or 1.
All inputs are finite; a program needn't handle non-finite values.
Results may differ from a plain program's by a relative error of at most 0.00055.
Values sent between devices are 32-bit elements; how exact they have to be, the bound alone decides.
No kernel may reach another device: no remote copies, remote signals or barrier semaphores. Data moves between devices by JAX's collectives and lax.ppermute only.
A program may use at most 64 MiB of HBM per device.

v0:
```python
import math

import jax
import jax.numpy as jnp
from jax import lax
from jax.sharding import PartitionSpec as P

NBLOCKS = 4
ROUNDS = 2


def local_round(shard_data, signs, dual, order_row, weights, reg_total, sigma_prime, squared):
    block_rows = shard_data.shape[0] // NBLOCKS
    feature_scale = 1.0 / math.sqrt(shard_data.shape[1])
    local_weights = weights
    dual_change = jnp.zeros_like(dual)
    for position in range(NBLOCKS):
        offset = order_row[position] * block_rows
        block_data = lax.dynamic_slice_in_dim(shard_data, offset, block_rows, 0)
        block_signs = lax.dynamic_slice_in_dim(signs, offset, block_rows, 0)
        block_dual = lax.dynamic_slice_in_dim(dual, offset, block_rows, 0)
        block_change = lax.dynamic_slice_in_dim(dual_change, offset, block_rows, 0)
        block_norms = lax.dynamic_slice_in_dim(squared, offset, block_rows, 0)
        rounded = local_weights.astype(jnp.bfloat16)
        score = feature_scale * jnp.dot(block_data, rounded, preferred_element_type=jnp.float32)
        current = block_dual + block_change
        updated = jnp.clip(
            current + reg_total * (1.0 - block_signs * score) / (sigma_prime * block_norms),
            0.0,
            1.0,
        )
        change = updated - current
        dual_change = lax.dynamic_update_slice_in_dim(dual_change, block_change + change, offset, 0)
        coefficient = (block_signs * change).astype(jnp.bfloat16)
        local_weights = local_weights + sigma_prime * feature_scale / reg_total * jnp.dot(
            coefficient, block_data, preferred_element_type=jnp.float32
        )
    return dual_change


def shards(data, labels, order, reg_index):
    group_size = lax.axis_size("blk")
    row_count = data.shape[0]
    feature_count = data.shape[1]
    samples_all = row_count * group_size
    feature_scale = 1.0 / math.sqrt(feature_count)
    reg_strength = 0.04 * jnp.exp(0.5 * math.log(2.0) * reg_index[0].astype(jnp.float32))
    reg_total = reg_strength * samples_all
    sigma_prime = jnp.float32(group_size)
    signs = labels.astype(jnp.float32)
    squared = (
        jnp.einsum("rf,rf->r", data, data, preferred_element_type=jnp.float32) / feature_count
        + 1e-06
    )
    weights = jnp.zeros((feature_count,), jnp.float32)
    dual = jnp.zeros((row_count,), jnp.float32)
    for round_index in range(ROUNDS):
        dual_change = local_round(
            data, signs, dual, order[0], weights, reg_total, sigma_prime, squared
        )
        coefficient = (signs * dual_change).astype(jnp.bfloat16)
        delta = (
            feature_scale
            / reg_total
            * jnp.dot(coefficient, data, preferred_element_type=jnp.float32)
        )
        weights = weights + lax.psum(delta, "blk")
        dual = dual + dual_change
    margins = feature_scale * jnp.dot(
        data, weights.astype(jnp.bfloat16), preferred_element_type=jnp.float32
    )
    hinge = jnp.maximum(0.0, 1.0 - signs * margins)
    hinge_total, dual_total = lax.psum((jnp.sum(hinge), jnp.sum(dual)), "blk")
    gap = reg_strength * jnp.sum(weights * weights) + (hinge_total - dual_total) / samples_all
    return (dual, margins, gap.reshape(1))


def solution(mesh):
    placed = (P("blk", None), P("blk"), P("blk", None), P("grp"))
    return jax.shard_map(
        shards,
        mesh=mesh,
        in_specs=placed,
        out_specs=(P(("grp", "blk")), P(("grp", "blk")), P("grp")),
        check_vma=False,
    )
```

profile of v0, /device:TPU:0, one launch (start us, length us, event | category | flops | bytes accessed | tf_op | source)
XLA Modules:
  0.0 192.1 jit_solution(11065774794570149796)
XLA Ops:
  7.2 0.0 all-reduce.4.cloned.1.call-start
  7.2 1.4 fusion.134
  11.8 0.7 convert_element_type.59
  12.5 3.1 %fusion = f32[32]{0:T(128)S(1)} fusion(bf16[32,65536]{1,0:T(8,128)(2,1)} %param.4), kind=kLoop, calls=%fused_computation.1 | loop fusion | flops 6291424 | bytes 4194432 | tf_op jit(solution)/shard_map/rf,rf->r/dot_general | solution.py:52
  15.7 0.1 fusion.135
  15.7 2.1 %fusion.6 = f32[8]{0:T(128)S(1)} fusion(f32[8]{0:T(128)S(1)} %get-tuple-element.15, bf16[32,65536]{1,0:T(8,128)(2,1)} %param.4, s32[]{:T(128)S(6)} %select_n.8, f32[32]{0:T(128)S(1)} %multiply_add_fusion.3, f32[]{:T(128)} %bitcast), kind=kOutput, calls=%fused_computation.15 | convolution fusion | flops 1048632 | bytes 1050208 | tf_op jit(solution)/shard_map/dot_general | solution.py:25
  17.8 1.7 fusion.83
  19.5 0.2 dynamic_update_slice.24
  19.7 0.0 copy-start
  19.7 0.1 reshape.40
  19.9 2.2 %fusion.14 = f32[8]{0:T(128)S(1)} fusion(f32[8]{0:T(128)S(1)} %get-tuple-element.14, bf16[65536,1]{0,1:T(2,128)(2,1)S(1)} %reshape.40, bf16[32,65536]{1,0:T(8,128)(2,1)} %param.4, s32[]{:T(128)S(6)} %select_n.9, f32[32]{0:T(128)S(1)} %multiply_add_fusion.3, f32[]{:T(128)} %bitcast, f32[32]{0:T(128)S(1)} %dynamic_update_slice.24), kind=kOutput, calls=%fused_computation.23 | convolution fusion | flops 1048648 | bytes 1181312 | tf_op jit(solution)/shard_map/dot_general | solution.py:25
  22.1 0.0 copy-start.3
  22.1 0.2 add_dynamic-update-slice_fusion.3
  22.3 1.6 fusion.77
  24.0 0.1 reshape.44
  24.1 0.0 copy-done
  24.1 0.9 fusion.22
  25.0 0.2 add_dynamic-update-slice_fusion.2
  25.1 0.4 fusion.71
  25.6 0.1 add_convert_fusion.1
  25.7 0.1 reshape.48
  25.8 2.1 %fusion.31 = f32[8]{0:T(128)S(1)} fusion(bf16[65536,1]{0,1:T(2,128)(2,1)S(1)} %reshape.48, bf16[32,65536]{1,0:T(8,128)(2,1)} %param.4, s32[]{:T(128)S(6)} %select_n.11, f32[32]{0:T(128)S(1)} %add_dynamic-update-slice_fusion.2, f32[32]{0:T(128)S(1)} %multiply_add_fusion.3, f32[]{:T(128)} %bitcast, f32[32]{0:T(128)S(1)} %convert_element_type.59), kind=kOutput, calls=%fused_computation.40 | convolution fusion | flops 1048656 | bytes 1181312 | tf_op jit(solution)/shard_map/dot_general | solution.py:25
  27.9 0.2 dynamic_update_slice.27
  28.1 0.0 copy-done.3
  28.1 2.8 %fusion.108 = f32[1,65536]{1,0:T(1,128)S(1)} fusion(bf16[32,65536]{1,0:T(8,128)(2,1)} %param.4, f32[32]{0:T(128)S(1)} %dynamic_update_slice.27, s32[32]{0:T(128)S(1)} %copy-done.3), kind=kOutput, calls=%fused_computation.128 | convolution fusion | flops 4194400 | bytes 4456704 | tf_op jit(solution)/shard_map/dot_general | solution.py:65
  31.0 0.7 broadcast_multiply_fusion.1
  31.7 0.0 all-reduce.4.cloned.1.call-update
  31.7 0.0 all-reduce.6.cloned.1.call-start
  31.8 58.2 %all-reduce.4.cloned.1.call-done = f32[65536]{0:T(1024)} async-done(((f32[65536]{0:T(1024)}), f32[65536]{0:T(1024)}) %all-reduce.4.cloned.1.call-update) | async-done | bytes 262160 | tf_op jit(solution)/shard_map/psum | solution.py:67
  90.0 0.0 copy-start.2
  90.0 1.0 convert_element_type.68
  91.1 0.1 reshape.52
  91.2 2.1 %fusion.39 = f32[8]{0:T(128)S(1)} fusion(f32[8]{0:T(128)S(1)} %get-tuple-element.15, bf16[65536,1]{0,1:T(2,128)(2,1)S(1)} %reshape.52, bf16[32,65536]{1,0:T(8,128)(2,1)} %param.4, s32[]{:T(128)S(6)} %select_n.8, f32[32]{0:T(128)S(1)} %dynamic_update_slice.27, f32[32]{0:T(128)S(1)} %multiply_add_fusion.3, f32[]{:T(128)} %bitcast), kind=kOutput, calls=%fused_computation.48 | convolution fusion | flops 1048648 | bytes 1181312 | tf_op jit(solution)/shard_map/dot_general | solution.py:25
  93.3 1.7 fusion.80
  95.0 0.2 dynamic_update_slice.28
  95.2 0.0 copy-start.1
  95.2 1.1 fusion.87
  96.3 0.1 reshape.56
  96.5 2.1 %fusion.47 = f32[8]{0:T(128)S(1)} fusion(f32[8]{0:T(128)S(1)} %get-tuple-element.14, bf16[65536,1]{0,1:T(2,128)(2,1)S(1)} %reshape.56, bf16[32,65536]{1,0:T(8,128)(2,1)} %param.4, s32[]{:T(128)S(6)} %select_n.9, f32[32]{0:T(128)S(1)} %dynamic_update_slice.27, f32[32]{0:T(128)S(1)} %multiply_add_fusion.3, f32[]{:T(128)} %bitcast, f32[32]{0:T(128)S(1)} %dynamic_update_slice.28), kind=kOutput, calls=%fused_computation.56 | convolution fusion | flops 1048656 | bytes 1181344 | tf_op jit(solution)/shard_map/dot_general | solution.py:25
  98.6 0.2 add_dynamic-update-slice_fusion.1
  98.8 1.7 fusion.74
  100.4 0.0 copy-done.2
  100.5 0.1 reshape.60
  100.6 0.0 copy-done.1
  100.6 0.9 fusion.55
  101.5 0.2 add_dynamic-update-slice_fusion
  101.7 0.4 fusion.68
  102.1 0.1 add_convert_fusion
  102.2 0.1 reshape.64
  102.4 0.9 fusion.64
  103.2 0.2 dynamic_update_slice.31
  103.4 2.8 %fusion.103 = f32[1,65536]{1,0:T(1,128)S(1)} fusion(bf16[32,65536]{1,0:T(8,128)(2,1)} %param.4, f32[32]{0:T(128)S(1)} %dynamic_update_slice.31, s32[32]{0:T(128)S(1)} %copy-done.3), kind=kOutput, calls=%fused_computation.123 | convolution fusion | flops 4194400 | bytes 4456704 | tf_op jit(solution)/shard_map/dot_general | solution.py:65
  106.3 0.7 broadcast_multiply_fusion
  107.0 0.0 all-reduce.6.cloned.1.call-update
  107.0 1.1 fusion.133
  108.1 53.5 %all-reduce.6.cloned.1.call-done = f32[65536]{0:T(1024)} async-done(((f32[65536]{0:T(1024)}), f32[65536]{0:T(1024)}) %all-reduce.6.cloned.1.call-update) | async-done | bytes 262160 | tf_op jit(solution)/shard_map/psum | solution.py:67
  161.6 1.7 multiply_reduce_fusion
  163.3 0.1 reshape.68
  163.5 4.5 %maximum_reduce_fusion = (f32[]{:T(128)}, f32[32]{0:T(128)}) fusion(s32[32]{0:T(128)S(1)} %copy-done.3, bf16[65536,1]{0,1:T(2,128)(2,1)S(1)} %reshape.68, bf16[32,65536]{1,0:T(8,128)(2,1)} %param.4), kind=kOutput, calls=%fused_computation.133 | convolution fusion | flops 4194495 | bytes 4325636 | tf_op jit(solution)/shard_map/dot_general | solution.py:69
  168.0 14.3 %all-reduce = (f32[]{:T(128)}, f32[]{:T(128)}) all-reduce(f32[]{:T(128)} %get-tuple-element.16, f32[]{:T(128)} %get-tuple-element.5), channel_id=1, replica_groups=mesh['grp'=4,'blk'=8] {'blk'}, use_global_device_ids=true, to_apply=%region_4.5 | all-reduce | flops 2 | bytes 16 | tf_op jit(solution)/shard_map/psum | solution.py:73
  (6 shorter events, 0.1 us)
Async XLA Ops:
  7.2 82.9 %all-reduce.4.cloned.1.call-start = ((), (), s32[]{:S(2)}) async-start(), calls=%async_computation | async-start | bytes 524288 | tf_op jit(solution)/shard_map/psum | solution.py:67
  19.7 4.4 %copy-start = (bf16[32,65536]{1,0:T(8,128)(2,1)S(1)}, bf16[32,65536]{1,0:T(8,128)(2,1)}, u32[]{:S(2)}) copy-start(bf16[32,65536]{1,0:T(8,128)(2,1)} %param.4) | copy-start | bytes 12582916
  22.1 6.0 %copy-start.3 = (s32[32]{0:T(128)S(1)}, s32[32]{0:T(128)}, u32[]{:S(2)}) copy-start(s32[32]{0:T(128)} %param.5) | copy-start | bytes 388
  31.7 129.9 %all-reduce.6.cloned.1.call-start = ((), (), s32[]{:S(2)}) async-start(), calls=%async_computation.1 | async-start | bytes 524288 | tf_op jit(solution)/shard_map/psum | solution.py:67
  90.0 10.4 %copy-start.2 = (f32[65536]{0:T(1024)S(1)}, f32[65536]{0:T(1024)}, u32[]{:S(2)}) copy-start(f32[65536]{0:T(1024)} %all-reduce.4.cloned.1.call-done) | copy-start | bytes 786436
  95.2 5.4 %copy-start.1 = (bf16[32,65536]{1,0:T(8,128)(2,1)S(1)}, bf16[32,65536]{1,0:T(8,128)(2,1)}, u32[]{:S(2)}) copy-start(bf16[32,65536]{1,0:T(8,128)(2,1)} %param.4) | copy-start | bytes 12582916
Sparse Core Ops, SparseCore 0:
  31.8 58.1 all-reduce.3
  107.1 54.4 all-reduce.5
where the time goes:
time: 193 us; the launch traced here: 192 us
  waiting for transfers between devices  112 us (58%)
  matrix products  30.8 us (16%)
  between operations  20.5 us (11%)
  blocking collectives  14.3 us (7%)
  other arithmetic  11.1 us (6%)
  local copies, waits for them, and re-layouts  3.5 us (2%)
    psum x2, waiting for transfers between devices, shards(): weights = weights + lax.psum(delta, 'blk')  112 us
    psum x1, blocking collectives, shards(): hinge_total, dual_total = lax.psum((jnp.sum(hinge), jnp.sum(dual)), 'blk')  14.3 us
    dot_general x8, matrix products, local_round(): jnp.dot(block_data, rounded, preferred_element_type=jnp.float32)  13.1 us
    dot_general x6, matrix products, local_round(): jnp.dot(coefficient, block_data, preferred_element_type=jnp.float32)  7.46 us
    dot_general x2, matrix products, shards(): jnp.dot(coefficient, data, preferred_element_type=jnp.float32)  5.69 us
    dot_general x1, matrix products, shards(): jnp.dot(data, weights.astype(jnp.bfloat16), preferred_element_type=jnp.fl...  4.52 us
  transfers between devices with their start and end apart: 2, of which 2 were waited for; matrix products, arithmetic and copies ran while one was open for 1% of the time, Pallas kernels for 0%

commit v1 on v0

v1 whole, which is shorter than its diff:
```python
import functools
import math

import jax
import jax.numpy as jnp
from jax import lax
from jax.experimental import pallas as pl
from jax.experimental.pallas import tpu as pltpu
from jax.sharding import PartitionSpec as P

ROUNDS = 2
HALF = 8
LOADS = 8

F32 = jnp.float32
BF16 = jnp.bfloat16
NT = (((1,), (1,)), ((), ()))
NN = (((1,), (0,)), ((), ()))


def regularization(reg_ref, samples):
    index = jnp.full((1, 1), reg_ref[0], jnp.int32).astype(F32)
    lam = 0.04 * jnp.exp(0.5 * math.log(2.0) * index)
    return lam, lam * samples


def ascend(gram, order_ref, signs, dual, score, reg_total, sigma, features):
    rows = gram.shape[0]
    blocks = order_ref.shape[1]
    eye = lax.broadcasted_iota(jnp.int32, (rows, rows), 0) == lax.broadcasted_iota(
        jnp.int32, (rows, rows), 1
    )
    block_of = lax.broadcasted_iota(jnp.int32, (1, rows), 1) // (rows // blocks)
    squared = jnp.sum(jnp.where(eye, gram, 0.0), axis=0, keepdims=True) / features + 1e-06
    rate = reg_total / (sigma * squared)
    couple = gram * (sigma / features / reg_total)
    change = jnp.zeros_like(dual)
    for position in range(blocks):
        current = dual + change
        updated = jnp.clip(current + rate * (1.0 - signs * score), 0.0, 1.0)
        step = jnp.where(block_of == order_ref[0, position], updated - current, 0.0)
        change = change + step
        if position < blocks - 1:
            coefficient = (signs * step).astype(BF16).astype(F32)
            column = jnp.sum(jnp.where(eye, coefficient, 0.0), axis=1, keepdims=True)
            score = score + jnp.sum(couple * column, axis=0, keepdims=True)
    return change


def weight_change(full, x_ref, keep_ref, send_ref, core, scale):
    rows, features = x_ref.shape
    segments = 2 * HALF
    length = features // segments
    depth = segments * rows
    spread = (
        lax.broadcasted_iota(jnp.int32, (rows, depth), 1) % rows
        == lax.broadcasted_iota(jnp.int32, (rows, depth), 0)
    )
    left = jnp.broadcast_to(full, (segments, rows)).astype(BF16)
    wide = lax.dot_general(
        left, jnp.where(spread, 1.0, 0.0).astype(BF16), NN, preferred_element_type=F32
    )
    segment_of = lax.broadcasted_iota(jnp.int32, (segments, depth), 1) // rows
    wanted = (lax.broadcasted_iota(jnp.int32, (segments, depth), 0) + core * HALF) % segments
    wide = jnp.where(segment_of == wanted, wide, 0.0).astype(BF16)
    width = min(length, 512)
    for begin in range(0, length, width):
        stacked = jnp.concatenate(
            [x_ref[:, g * length + begin : g * length + begin + width] for g in range(segments)],
            axis=0,
        )
        part = scale * lax.dot_general(wide, stacked, NN, preferred_element_type=F32)
        keep_ref[:, begin : begin + width] = part[:HALF]
        send_ref[:, begin : begin + width] = part[HALF:]


def scores(x_ref, low, high):
    rows, features = x_ref.shape
    segments = 2 * HALF
    length = features // segments
    total = jnp.zeros((HALF, rows), F32)
    row = lax.broadcasted_iota(jnp.int32, (HALF, rows), 0)
    for g in range(segments):
        half = low if g < HALF else high
        part = lax.dot_general(
            half, x_ref[:, g * length : (g + 1) * length], NT, preferred_element_type=F32
        )
        total = total + jnp.where(row == g % HALF, part, 0.0)
    return jnp.sum(total, axis=0, keepdims=True)


def first_kernel(samples, sigma, order_ref, reg_ref, core_ref, label_ref, data_ref,
                 keep_ref, send_ref, gram_ref, dual_ref, x_ref, arrived):
    rows, features = x_ref.shape
    width = features // LOADS
    copies = [
        pltpu.make_async_copy(
            data_ref.at[:, pl.ds(k * width, width)],
            x_ref.at[:, pl.ds(k * width, width)],
            arrived.at[k],
        )
        for k in range(LOADS)
    ]
    for copy in copies:
        copy.start()
    gram = jnp.zeros((rows, rows), F32)
    for k in range(LOADS):
        copies[k].wait()
        piece = x_ref[:, k * width : (k + 1) * width]
        gram = gram + lax.dot_general(piece, piece, NT, preferred_element_type=F32)
    gram_ref[...] = gram
    signs = label_ref[...].astype(F32)
    _, reg_total = regularization(reg_ref, samples)
    none = jnp.zeros((1, rows), F32)
    change = ascend(gram, order_ref, signs, none, none, reg_total, sigma, features)
    dual_ref[...] = change
    scale = 1.0 / math.sqrt(features) / reg_total
    weight_change((signs * change).astype(BF16), x_ref, keep_ref, send_ref, core_ref[0], scale)


def halves(own, other, core):
    low = jnp.where(core == 0, own, other)
    high = jnp.where(core == 0, other, own)
    return low, high


def next_kernel(samples, sigma, order_ref, reg_ref, core_ref, label_ref, own_ref, other_ref,
                gram_ref, old_dual_ref, x_ref, keep_ref, send_ref, dual_ref):
    rows, features = x_ref.shape
    signs = label_ref[...].astype(F32)
    _, reg_total = regularization(reg_ref, samples)
    low, high = halves(own_ref[...], other_ref[...], core_ref[0])
    score = 1.0 / math.sqrt(features) * scores(x_ref, low.astype(BF16), high.astype(BF16))
    dual = old_dual_ref[...]
    change = ascend(
        gram_ref[...], order_ref, signs, dual, score, reg_total, sigma, features
    )
    dual_ref[...] = dual + change
    scale = 1.0 / math.sqrt(features) / reg_total
    weight_change((signs * change).astype(BF16), x_ref, keep_ref, send_ref, core_ref[0], scale)


def last_kernel(samples, reg_ref, core_ref, label_ref, own_ref, other_ref, dual_ref, x_ref,
                margin_ref, share_ref, norm_ref):
    rows, features = x_ref.shape
    signs = label_ref[...].astype(F32)
    lam, _ = regularization(reg_ref, samples)
    low, high = halves(own_ref[...], other_ref[...], core_ref[0])
    margins = 1.0 / math.sqrt(features) * scores(x_ref, low.astype(BF16), high.astype(BF16))
    margin_ref[...] = margins
    hinge = jnp.maximum(0.0, 1.0 - signs * margins)
    share = jnp.sum(hinge - dual_ref[...], axis=1, keepdims=True)
    share_ref[...] = jnp.broadcast_to(share, share_ref.shape)
    norm = jnp.sum(low * low + high * high, axis=0, keepdims=True)
    norm_ref[...] = lam * jnp.sum(norm, axis=1, keepdims=True)


def gap_kernel(samples, peers, share_ref, norm_ref, gap_ref):
    total = share_ref[0:1, 0:1]
    step = share_ref.shape[0] // peers
    for k in range(1, peers):
        total = total + share_ref[k * step : k * step + 1, 0:1]
    gap_ref[...] = norm_ref[...] + total / samples


def swap(value, peers, partner):
    return lax.ppermute(value, "blk", [(i, partner(i)) for i in range(peers)])


def all_reduce(keep, send, peers):
    chips = peers // 2
    own = keep + swap(send, peers, lambda i: i ^ 1)
    mask = 1
    while mask < chips:
        own = own + swap(own, peers, lambda i: i ^ (2 * mask))
        mask = 2 * mask + 1
    return own, swap(own, peers, lambda i: i ^ 1)


def call(body, outs, spaces, scratch=()):
    return pl.pallas_call(
        body,
        out_shape=[jax.ShapeDtypeStruct(shape, F32) for shape in outs],
        in_specs=[pl.BlockSpec(memory_space=space) for space in spaces],
        out_specs=[pl.BlockSpec(memory_space=pltpu.VMEM) for _ in outs],
        scratch_shapes=list(scratch),
    )


def shards(data, labels, order, reg_index):
    peers = lax.axis_size("blk")
    rows, features = data.shape
    samples = rows * peers
    sigma = float(peers)
    half = (HALF, features // 2 // HALF)
    core = (lax.axis_index("blk") % 2).astype(jnp.int32).reshape(1)
    label_row = labels.reshape(1, rows)
    S, V, A = pltpu.SMEM, pltpu.VMEM, pl.ANY
    keep, send, gram, dual = call(
        functools.partial(first_kernel, samples, sigma),
        [half, half, (rows, rows), (1, rows)],
        [S, S, S, V, A],
        [pltpu.VMEM((rows, features), BF16), pltpu.SemaphoreType.DMA((LOADS,))],
    )(order, reg_index, core, label_row, data)
    own, other = all_reduce(keep, send, peers)
    for _ in range(ROUNDS - 1):
        keep, send, dual = call(
            functools.partial(next_kernel, samples, sigma),
            [half, half, (1, rows)],
            [S, S, S, V, V, V, V, V, V],
        )(order, reg_index, core, label_row, own, other, gram, dual, data)
        more, rest = all_reduce(keep, send, peers)
        own, other = own + more, other + rest
    margins, share, norm = call(
        functools.partial(last_kernel, samples),
        [(1, rows), (8 * peers, 128), (1, 1)],
        [S, S, V, V, V, V, V],
    )(reg_index, core, label_row, own, other, dual, data)
    share = lax.all_to_all(share, "blk", 0, 0, tiled=True)
    (gap,) = call(functools.partial(gap_kernel, samples, peers), [(1, 1)], [V, V])(share, norm)
    return dual.reshape(rows), margins.reshape(rows), gap.reshape(1)


def solution(mesh):
    placed = (P("blk", None), P("blk"), P("blk", None), P("grp"))
    return jax.shard_map(
        shards,
        mesh=mesh,
        in_specs=placed,
        out_specs=(P(("grp", "blk")), P(("grp", "blk")), P("grp")),
        check_vma=False,
    )
```

time: 193 us -> 69.8 us (0.36)
  waiting for transfers between devices: 112 us -> 19.9 us
  matrix products: 30.8 us -> 0 us
  between operations: 20.5 us -> 1.33 us
  Pallas kernels: 0 us -> 18.7 us
  starting transfers between devices: 0.08 us -> 13.1 us
  other arithmetic: 11.1 us -> 5.04 us
  blocking collectives: 14.3 us -> 10.8 us
  local copies, waits for them, and re-layouts: 3.5 us -> 0.65 us
    psum x2 -> x0, waiting for transfers between devices: 112 us -> none  [shards(): weights = weights + lax.psum(delta, 'blk')]
    dot_general x17 -> x0, matrix products: 30.8 us -> none  [the longest x8 13.1 us: local_round(): jnp.dot(block_data, rounded, preferred_element_type=jnp.float32)]
    ppermute x0 -> x8, waiting for transfers between devices: none -> 19.9 us  [swap(): return lax.ppermute(value, 'blk', [(i, partner(i)) for i in range(peers)])]
    pallas_call x0 -> x4, Pallas kernels: none -> 18.7 us  [the longest x1 7.19 us: shards(): call(functools.partial(first_kernel, samples, sigma), [half, half, (rows,...]
    psum x1 -> x0, blocking collectives: 14.3 us -> none  [shards(): hinge_total, dual_total = lax.psum((jnp.sum(hinge), jnp.sum(dual)), 'blk')]
    ppermute x0 -> x8, starting transfers between devices: none -> 13.1 us  [swap(): return lax.ppermute(value, 'blk', [(i, partner(i)) for i in range(peers)])]
    all_to_all x0 -> x1, blocking collectives: none -> 10.8 us  [shards(): share = lax.all_to_all(share, 'blk', 0, 0, tiled=True)]
    add x1 -> x7, other arithmetic: 0.01 us -> 5.04 us  [the longest x2 3.14 us: shards(): own, other = (own + more, other + rest)]
  transfers between devices with their start and end apart: 2 -> 8, of which waited for: 2 -> 8; matrix products, arithmetic and copies ran while one was open for 1% -> 0% of each run, Pallas kernels for 0% -> 0%
where the time goes in v1:
time: 69.8 us; the launch traced here: 69.4 us
  waiting for transfers between devices  19.9 us (29%)
  Pallas kernels  18.7 us (27%)
  starting transfers between devices  13.1 us (19%)
  blocking collectives  10.8 us (15%)
  other arithmetic  5.04 us (7%)
  between operations  1.33 us (2%)
    ppermute x8, waiting for transfers between devices, swap(): return lax.ppermute(value, 'blk', [(i, partner(i)) for i in range(peers)])  19.9 us
    ppermute x8, starting transfers between devices, swap(): return lax.ppermute(value, 'blk', [(i, partner(i)) for i in range(peers)])  13.1 us
    all_to_all x1, blocking collectives, shards(): share = lax.all_to_all(share, 'blk', 0, 0, tiled=True)  10.8 us
    pallas_call x1, Pallas kernels, shards(): call(functools.partial(first_kernel, samples, sigma), [half, half, (rows,...  7.19 us
    pallas_call x1, Pallas kernels, shards(): call(functools.partial(next_kernel, samples, sigma), [half, half, (1, row...  5.37 us
    pallas_call x1, Pallas kernels, shards(): call(functools.partial(last_kernel, samples), [(1, rows), (8 * peers, 128...  4.27 us
    add x2, other arithmetic, shards(): own, other = (own + more, other + rest)  3.14 us
    add x2, other arithmetic, all_reduce(): own = keep + swap(send, peers, lambda i: i ^ 1)  1.85 us
  transfers between devices with their start and end apart: 8, of which 8 were waited for; matrix products, arithmetic and copies ran while one was open for 0% of the time, Pallas kernels for 0%

profile of v1, /device:TPU:0, one launch (start us, length us, event | category | flops | bytes accessed | tf_op | source)
XLA Modules:
  0.0 69.4 jit_solution(14283000505169067920)
XLA Ops:
  1.3 7.2 %shard_map.67 = (f32[8,4096]{1,0:T(8,128)}, f32[8,4096]{1,0:T(8,128)}, f32[32,32]{1,0:T(8,128)}, f32[1,32]{1,0:T(1,128)}) custom-call(s32[1,4]{1,0:T(1,128)} %order_ref.3, s32[1]{0:T(128)S(6)} %copy.7.reg_ref, s32[1]{0:T(128)} %bitcast.core_ref, s32[1,32]{1,0:T(1,128)} %bitcast.9, bf16[32,65536]{1,0:T(8,128)(2,1)} %x_ref.3), custom_call_target="tpu_custom_call" | custom-call | tf_op jit(solution)/shard_map/pallas_call | solution.py:199
  8.5 0.6 collective-permute-start
  9.0 1.2 %collective-permute-done = f32[8,4096]{1,0:T(8,128)S(1)} collective-permute-done((f32[8,4096]{1,0:T(8,128)}, f32[8,4096]{1,0:T(8,128)S(1)}, u32[]{:S(2)}, u32[]{:S(2)}) %collective-permute-start) | collective-permute-done | bytes 131104 | tf_op jit(solution)/shard_map/ppermute | solution.py:167
  10.2 0.9 %add.29 = f32[8,4096]{1,0:T(8,128)S(1)} add(f32[8,4096]{1,0:T(8,128)} %get-tuple-element.13, f32[8,4096]{1,0:T(8,128)S(1)} %collective-permute-done) | non-fusion elementwise | flops 32768 | bytes 393216 | tf_op jit(solution)/shard_map/add | solution.py:172
  11.2 3.0 %collective-permute-start.1 = (f32[8,4096]{1,0:T(8,128)S(1)}, f32[8,4096]{1,0:T(8,128)S(1)}, u32[]{:S(2)}, u32[]{:S(2)}) collective-permute-start(f32[8,4096]{1,0:T(8,128)S(1)} %add.29), channel_id=1, source_target_pairs={{0,2},{1,3},{2,0},{3,1},{4,6},{5,7},{6,4},{7,5},{8,10},{9,11},{10,... | collective-permute-start | bytes 393224 | tf_op jit(solution)/shard_map/ppermute | solution.py:167
  14.2 3.8 %collective-permute-done.1 = f32[8,4096]{1,0:T(8,128)S(1)} collective-permute-done((f32[8,4096]{1,0:T(8,128)S(1)}, f32[8,4096]{1,0:T(8,128)S(1)}, u32[]{:S(2)}, u32[]{:S(2)}) %collective-permute-start.1) | collective-permute-done | bytes 131104 | tf_op jit(solution)/shard_map/ppermute | solution.py:167
  18.0 3.8 %collective-permute-start.2 = (f32[8,4096]{1,0:T(8,128)S(1)}, f32[8,4096]{1,0:T(8,128)S(1)}, u32[]{:S(2)}, u32[]{:S(2)}) collective-permute-start(f32[8,4096]{1,0:T(8,128)S(1)} %add.30), channel_id=1, source_target_pairs={{0,6},{1,7},{2,4},{3,5},{4,2},{5,3},{6,0},{7,1},{8,14},{9,15},{10,... | collective-permute-start | bytes 393224 | tf_op jit(solution)/shard_map/ppermute | solution.py:167
  21.8 3.1 %collective-permute-done.2 = f32[8,4096]{1,0:T(8,128)S(1)} collective-permute-done((f32[8,4096]{1,0:T(8,128)S(1)}, f32[8,4096]{1,0:T(8,128)S(1)}, u32[]{:S(2)}, u32[]{:S(2)}) %collective-permute-start.2) | collective-permute-done | bytes 131104 | tf_op jit(solution)/shard_map/ppermute | solution.py:167
  24.9 0.0 copy-start
  25.0 0.1 collective-permute-start.3
  25.0 1.3 %collective-permute-done.3.other_ref = f32[8,4096]{1,0:T(8,128)S(1)} collective-permute-done((f32[8,4096]{1,0:T(8,128)S(1)}, f32[8,4096]{1,0:T(8,128)S(1)}, u32[]{:S(2)}, u32[]{:S(2)}) %collective-permute-start.3) | collective-permute-done | bytes 131104 | tf_op jit(solution)/shard_map/ppermute | solution.py:167
  26.4 0.0 copy-start.1
  26.4 0.0 copy-done
  26.4 0.6 copy-done.1
  27.0 5.4 %shard_map.68 = (f32[8,4096]{1,0:T(8,128)}, f32[8,4096]{1,0:T(8,128)}, f32[1,32]{1,0:T(1,128)}) custom-call(s32[1,4]{1,0:T(1,128)} %order_ref.3, s32[1]{0:T(128)S(6)} %copy.7.reg_ref, s32[1]{0:T(128)} %bitcast.core_ref, s32[1,32]{1,0:T(1,128)} %bitcast.10, f32[8,4096]{1,0:T(8,128)} %copy-done, f32[8,4096]{1,0:T(8,128)} %copy-done.1, ...), custom_call_target="tpu_custom_call" | custom-call | tf_op jit(solution)/shard_map/pallas_call | solution.py:207
  32.4 0.1 collective-permute-start.4
  32.5 1.4 %collective-permute-done.4 = f32[8,4096]{1,0:T(8,128)S(1)} collective-permute-done((f32[8,4096]{1,0:T(8,128)}, f32[8,4096]{1,0:T(8,128)S(1)}, u32[]{:S(2)}, u32[]{:S(2)}) %collective-permute-start.4) | collective-permute-done | bytes 131104 | tf_op jit(solution)/shard_map/ppermute | solution.py:167
  33.9 0.9 %add.32 = f32[8,4096]{1,0:T(8,128)S(1)} add(f32[8,4096]{1,0:T(8,128)} %get-tuple-element.18, f32[8,4096]{1,0:T(8,128)S(1)} %collective-permute-done.4) | non-fusion elementwise | flops 32768 | bytes 393216 | tf_op jit(solution)/shard_map/add | solution.py:172
  34.9 2.4 %collective-permute-start.5 = (f32[8,4096]{1,0:T(8,128)S(1)}, f32[8,4096]{1,0:T(8,128)S(1)}, u32[]{:S(2)}, u32[]{:S(2)}) collective-permute-start(f32[8,4096]{1,0:T(8,128)S(1)} %add.32), channel_id=1, source_target_pairs={{0,2},{1,3},{2,0},{3,1},{4,6},{5,7},{6,4},{7,5},{8,10},{9,11},{10,... | collective-permute-start | bytes 393224 | tf_op jit(solution)/shard_map/ppermute | solution.py:167
  37.3 3.8 %collective-permute-done.5 = f32[8,4096]{1,0:T(8,128)S(1)} collective-permute-done((f32[8,4096]{1,0:T(8,128)S(1)}, f32[8,4096]{1,0:T(8,128)S(1)}, u32[]{:S(2)}, u32[]{:S(2)}) %collective-permute-start.5) | collective-permute-done | bytes 131104 | tf_op jit(solution)/shard_map/ppermute | solution.py:167
  41.1 3.1 %collective-permute-start.6 = (f32[8,4096]{1,0:T(8,128)S(1)}, f32[8,4096]{1,0:T(8,128)S(1)}, u32[]{:S(2)}, u32[]{:S(2)}) collective-permute-start(f32[8,4096]{1,0:T(8,128)S(1)} %add.33), channel_id=1, source_target_pairs={{0,6},{1,7},{2,4},{3,5},{4,2},{5,3},{6,0},{7,1},{8,14},{9,15},{10,... | collective-permute-start | bytes 393224 | tf_op jit(solution)/shard_map/ppermute | solution.py:167
  44.2 3.8 %collective-permute-done.6 = f32[8,4096]{1,0:T(8,128)S(1)} collective-permute-done((f32[8,4096]{1,0:T(8,128)S(1)}, f32[8,4096]{1,0:T(8,128)S(1)}, u32[]{:S(2)}, u32[]{:S(2)}) %collective-permute-start.6) | collective-permute-done | bytes 131104 | tf_op jit(solution)/shard_map/ppermute | solution.py:167
  48.1 1.6 %fusion = (f32[8,4096]{1,0:T(8,128)}, f32[8,4096]{1,0:T(8,128)S(1)}) fusion(f32[8,4096]{1,0:T(8,128)} %copy-done, f32[8,4096]{1,0:T(8,128)S(1)} %add.33, f32[8,4096]{1,0:T(8,128)S(1)} %collective-permute-done.6), kind=kLoop, calls=%fused_computation | loop fusion | flops 65536 | bytes 655360 | tf_op jit(solution)/shard_map/add | solution.py:213
  49.6 0.0 collective-permute-start.7
  49.7 1.3 %collective-permute-done.7 = f32[8,4096]{1,0:T(8,128)S(1)} collective-permute-done((f32[8,4096]{1,0:T(8,128)S(1)}, f32[8,4096]{1,0:T(8,128)S(1)}, u32[]{:S(2)}, u32[]{:S(2)}) %collective-permute-start.7) | collective-permute-done | bytes 131104 | tf_op jit(solution)/shard_map/ppermute | solution.py:167
  51.0 1.6 %add.36.other_ref = f32[8,4096]{1,0:T(8,128)} add(f32[8,4096]{1,0:T(8,128)} %copy-done.1, f32[8,4096]{1,0:T(8,128)S(1)} %collective-permute-done.7) | non-fusion elementwise | flops 32768 | bytes 393216 | tf_op jit(solution)/shard_map/add | solution.py:213
  52.6 4.3 %shard_map.69 = (f32[1,32]{1,0:T(1,128)}, f32[64,128]{1,0:T(8,128)}, f32[1,1]{1,0:T(1,128)}) custom-call(s32[1]{0:T(128)S(6)} %copy.7.reg_ref, s32[1]{0:T(128)} %bitcast.core_ref, s32[1,32]{1,0:T(1,128)} %bitcast.11, f32[8,4096]{1,0:T(8,128)} %get-tuple-element.23.own_ref, f32[8,4096]{1,0:T(8,128)} %add.36.other_ref, f32[1,32]{1,0:T(1,128)} %get-tuple-element.17.dual_ref, ...), custom_call_target="tpu_custom_call" | custom-call | tf_op jit(solution)/shard_map/pallas_call | solution.py:214
  56.8 10.8 %all_to_all.11 = f32[8,8,128]{2,1,0:T(8,128)} all-to-all(f32[8,8,128]{2,1,0:T(8,128)} %bitcast.8), channel_id=1, replica_groups=mesh['grp'=4,'blk'=8] {'blk'}, dimensions={0} | all-to-all | bytes 65536 | tf_op jit(solution)/shard_map/all_to_all | solution.py:219
  67.6 1.8 %shard_map.70 = f32[1,1]{1,0:T(1,128)} custom-call(f32[64,128]{1,0:T(8,128)} %bitcast.7, f32[1,1]{1,0:T(1,128)} %get-tuple-element.22.norm_ref), custom_call_target="tpu_custom_call" | custom-call | tf_op jit(solution)/shard_map/pallas_call | solution.py:220
  (3 shorter events, 0.0 us)
Async XLA Ops:
  8.5 1.8 %collective-permute-start = (f32[8,4096]{1,0:T(8,128)}, f32[8,4096]{1,0:T(8,128)S(1)}, u32[]{:S(2)}, u32[]{:S(2)}) collective-permute-start(f32[8,4096]{1,0:T(8,128)} %get-tuple-element.14), channel_id=1, source_target_pairs={{0,1},{1,0},{2,3},{3,2},{4,5},{5,4},{6,7},{7,6},{8,9},{9,8},{10,11... | collective-permute-start | bytes 393224 | tf_op jit(solution)/shard_map/ppermute | solution.py:167
  11.2 6.8 %collective-permute-start.1 = (f32[8,4096]{1,0:T(8,128)S(1)}, f32[8,4096]{1,0:T(8,128)S(1)}, u32[]{:S(2)}, u32[]{:S(2)}) collective-permute-start(f32[8,4096]{1,0:T(8,128)S(1)} %add.29), channel_id=1, source_target_pairs={{0,2},{1,3},{2,0},{3,1},{4,6},{5,7},{6,4},{7,5},{8,10},{9,11},{10,... | collective-permute-start | bytes 393224 | tf_op jit(solution)/shard_map/ppermute | solution.py:167
  18.0 6.9 %collective-permute-start.2 = (f32[8,4096]{1,0:T(8,128)S(1)}, f32[8,4096]{1,0:T(8,128)S(1)}, u32[]{:S(2)}, u32[]{:S(2)}) collective-permute-start(f32[8,4096]{1,0:T(8,128)S(1)} %add.30), channel_id=1, source_target_pairs={{0,6},{1,7},{2,4},{3,5},{4,2},{5,3},{6,0},{7,1},{8,14},{9,15},{10,... | collective-permute-start | bytes 393224 | tf_op jit(solution)/shard_map/ppermute | solution.py:167
  24.9 1.4 %copy-start = (f32[8,4096]{1,0:T(8,128)}, f32[8,4096]{1,0:T(8,128)S(1)}, u32[]{:S(2)}) copy-start(f32[8,4096]{1,0:T(8,128)S(1)} %add.31.own_ref) | copy-start | bytes 393220
  25.0 1.4 %collective-permute-start.3 = (f32[8,4096]{1,0:T(8,128)S(1)}, f32[8,4096]{1,0:T(8,128)S(1)}, u32[]{:S(2)}, u32[]{:S(2)}) collective-permute-start(f32[8,4096]{1,0:T(8,128)S(1)} %add.31.own_ref), channel_id=1, source_target_pairs={{0,1},{1,0},{2,3},{3,2},{4,5},{5,4},{6,7},{7,6},{8,9},{9,8},{10,11... | collective-permute-start | bytes 393224 | tf_op jit(solution)/shard_map/ppermute | solution.py:167
  26.4 0.7 copy-start.1
  32.4 1.6 %collective-permute-start.4 = (f32[8,4096]{1,0:T(8,128)}, f32[8,4096]{1,0:T(8,128)S(1)}, u32[]{:S(2)}, u32[]{:S(2)}) collective-permute-start(f32[8,4096]{1,0:T(8,128)} %get-tuple-element.19), channel_id=1, source_target_pairs={{0,1},{1,0},{2,3},{3,2},{4,5},{5,4},{6,7},{7,6},{8,9},{9,8},{10,11... | collective-permute-start | bytes 393224 | tf_op jit(solution)/shard_map/ppermute | solution.py:167
  34.9 6.2 %collective-permute-start.5 = (f32[8,4096]{1,0:T(8,128)S(1)}, f32[8,4096]{1,0:T(8,128)S(1)}, u32[]{:S(2)}, u32[]{:S(2)}) collective-permute-start(f32[8,4096]{1,0:T(8,128)S(1)} %add.32), channel_id=1, source_target_pairs={{0,2},{1,3},{2,0},{3,1},{4,6},{5,7},{6,4},{7,5},{8,10},{9,11},{10,... | collective-permute-start | bytes 393224 | tf_op jit(solution)/shard_map/ppermute | solution.py:167
  41.1 6.9 %collective-permute-start.6 = (f32[8,4096]{1,0:T(8,128)S(1)}, f32[8,4096]{1,0:T(8,128)S(1)}, u32[]{:S(2)}, u32[]{:S(2)}) collective-permute-start(f32[8,4096]{1,0:T(8,128)S(1)} %add.33), channel_id=1, source_target_pairs={{0,6},{1,7},{2,4},{3,5},{4,2},{5,3},{6,0},{7,1},{8,14},{9,15},{10,... | collective-permute-start | bytes 393224 | tf_op jit(solution)/shard_map/ppermute | solution.py:167
  49.6 1.3 %collective-permute-start.7 = (f32[8,4096]{1,0:T(8,128)S(1)}, f32[8,4096]{1,0:T(8,128)S(1)}, u32[]{:S(2)}, u32[]{:S(2)}) collective-permute-start(f32[8,4096]{1,0:T(8,128)S(1)} %get-tuple-element.24), channel_id=1, source_target_pairs={{0,1},{1,0},{2,3},{3,2},{4,5},{5,4},{6,7},{7,6},{8,9},{9,8},{10,11... | collective-permute-start | bytes 393224 | tf_op jit(solution)/shard_map/ppermute | solution.py:167

commit v2 on v1

--- a/solution.py
+++ b/solution.py
@@ -11,6 +11,7 @@
 ROUNDS = 2
 HALF = 8
 LOADS = 8
+VMEM_LIMIT = 12 * 1024 * 1024
 
 F32 = jnp.float32
 BF16 = jnp.bfloat16
@@ -180,10 +181,11 @@
 def call(body, outs, spaces, scratch=()):
     return pl.pallas_call(
         body,
-        out_shape=[jax.ShapeDtypeStruct(shape, F32) for shape in outs],
+        out_shape=[jax.ShapeDtypeStruct(shape, dtype) for shape, dtype in outs],
         in_specs=[pl.BlockSpec(memory_space=space) for space in spaces],
         out_specs=[pl.BlockSpec(memory_space=pltpu.VMEM) for _ in outs],
         scratch_shapes=list(scratch),
+        compiler_params=pltpu.CompilerParams(vmem_limit_bytes=VMEM_LIMIT),
     )
 
 
@@ -192,32 +194,32 @@
     rows, features = data.shape
     samples = rows * peers
     sigma = float(peers)
-    half = (HALF, features // 2 // HALF)
+    half = ((HALF, features // 2 // HALF), F32)
     core = (lax.axis_index("blk") % 2).astype(jnp.int32).reshape(1)
     label_row = labels.reshape(1, rows)
-    S, V, A = pltpu.SMEM, pltpu.VMEM, pl.ANY
-    keep, send, gram, dual = call(
+    S, V = pltpu.SMEM, pltpu.VMEM
+    keep, send, gram, dual, near = call(
         functools.partial(first_kernel, samples, sigma),
-        [half, half, (rows, rows), (1, rows)],
-        [S, S, S, V, A],
-        [pltpu.VMEM((rows, features), BF16), pltpu.SemaphoreType.DMA((LOADS,))],
-    )(order, reg_index, core, label_row, data)
+        [half, half, ((rows, rows), F32), ((1, rows), F32), ((rows, features), BF16)],
+        [S, S, S, V, pltpu.HBM],
+        [pltpu.SemaphoreType.DMA((LOADS,))],
+    )(order, reg_index, core, label_row, pltpu.with_memory_space_constraint(data, pltpu.HBM))
     own, other = all_reduce(keep, send, peers)
     for _ in range(ROUNDS - 1):
         keep, send, dual = call(
             functools.partial(next_kernel, samples, sigma),
-            [half, half, (1, rows)],
+            [half, half, ((1, rows), F32)],
             [S, S, S, V, V, V, V, V, V],
-        )(order, reg_index, core, label_row, own, other, gram, dual, data)
+        )(order, reg_index, core, label_row, own, other, gram, dual, near)
         more, rest = all_reduce(keep, send, peers)
         own, other = own + more, other + rest
     margins, share, norm = call(
         functools.partial(last_kernel, samples),
-        [(1, rows), (8 * peers, 128), (1, 1)],
+        [((1, rows), F32), ((8 * peers, 128), F32), ((1, 1), F32)],
         [S, S, V, V, V, V, V],
-    )(reg_index, core, label_row, own, other, dual, data)
+    )(reg_index, core, label_row, own, other, dual, near)
     share = lax.all_to_all(share, "blk", 0, 0, tiled=True)
-    (gap,) = call(functools.partial(gap_kernel, samples, peers), [(1, 1)], [V, V])(share, norm)
+    (gap,) = call(functools.partial(gap_kernel, samples, peers), [((1, 1), F32)], [V, V])(share, norm)
     return dual.reshape(rows), margins.reshape(rows), gap.reshape(1)
 
 

time: 69.8 us -> 58.8 us (0.84)
  Pallas kernels: 18.7 us -> 12.1 us
  other arithmetic: 5.04 us -> 0.13 us
  local copies, waits for them, and re-layouts: 0.65 us -> 1.95 us
    pallas_call x4, Pallas kernels: 18.7 us -> 12.1 us  [the longest x1 6.36 us: shards(): call(functools.partial(first_kernel, samples, sigma), [half, half, ((rows...]
    add x2, other arithmetic: 3.14 us -> 0.05 us  [shards(): own, other = (own + more, other + rest)]
    add x2, other arithmetic: 1.85 us -> 0.03 us  [all_reduce(): own = keep + swap(send, peers, lambda i: i ^ 1)]
    unnamed x4 -> x6, local copies, waits for them, and re-layouts: 0.65 us -> 1.95 us
where the time goes in v2:
time: 58.8 us; the launch traced here: 58.6 us
  waiting for transfers between devices  19.4 us (33%)
  starting transfers between devices  13.2 us (22%)
  Pallas kernels  12.1 us (21%)
  blocking collectives  10.5 us (18%)
  local copies, waits for them, and re-layouts  1.95 us (3%)
  between operations  1.35 us (2%)
    ppermute x8, waiting for transfers between devices, swap(): return lax.ppermute(value, 'blk', [(i, partner(i)) for i in range(peers)])  19.4 us
    ppermute x8, starting transfers between devices, swap(): return lax.ppermute(value, 'blk', [(i, partner(i)) for i in range(peers)])  13.2 us
    all_to_all x1, blocking collectives, shards(): share = lax.all_to_all(share, 'blk', 0, 0, tiled=True)  10.5 us
    pallas_call x1, Pallas kernels, shards(): call(functools.partial(first_kernel, samples, sigma), [half, half, ((rows...  6.36 us
    pallas_call x1, Pallas kernels, shards(): call(functools.partial(next_kernel, samples, sigma), [half, half, ((1, ro...  2.81 us
    unnamed x6, local copies, waits for them, and re-layouts  1.95 us
    pallas_call x1, Pallas kernels, shards(): call(functools.partial(last_kernel, samples), [((1, rows), F32), ((8 * pe...  1.75 us
  transfers between devices with their start and end apart: 8, of which 8 were waited for; matrix products, arithmetic and copies ran while one was open for 0% of the time, Pallas kernels for 0%

profile of v2, /device:TPU:0, one launch (start us, length us, event | category | flops | bytes accessed | tf_op | source)
XLA Modules:
  0.0 58.6 jit_solution(3880526656638870222)
XLA Ops:
  1.3 0.0 copy-start
  1.3 0.6 %copy-done = s32[32]{0:T(128)S(1)} copy-done((s32[32]{0:T(128)S(1)}, s32[32]{0:T(128)}, u32[]{:S(2)}) %copy-start) | copy-done | bytes 152
  1.9 0.0 copy-start.1
  1.9 0.7 %copy-done.1 = s32[1,4]{1,0:T(1,128)S(1)} copy-done((s32[1,4]{1,0:T(1,128)S(1)}, s32[1,4]{1,0:T(1,128)}, u32[]{:S(2)}) %copy-start.1) | copy-done | bytes 40
  2.6 6.4 %shard_map.67 = (f32[8,4096]{1,0:T(8,128)S(1)}, f32[8,4096]{1,0:T(8,128)S(1)}, f32[32,32]{1,0:T(8,128)S(1)}, f32[1,32]{1,0:T(1,128)S(1)}, bf16[32,65536]{1,0:T(8,128)(2,1)S(1)}) custom-call(s32[1,4]{1,0:T(1,128)S(1)} %copy-done.1, s32[1]{0:T(128)S(6)} %copy.7.reg_ref, s32[1]{0:T(128)} %bitcast.core_ref, s32[1,32]{1,0:T(1,128)S(1)} %bitcast.9, ...), custom_call_target="tpu_custom_call" | custom-call | tf_op jit(solution)/shard_map/pallas_call | solution.py:201
  9.0 0.6 collective-permute-start
  9.5 1.0 %collective-permute-done = f32[8,4096]{1,0:T(8,128)S(1)} collective-permute-done((f32[8,4096]{1,0:T(8,128)S(1)}, f32[8,4096]{1,0:T(8,128)S(1)}, u32[]{:S(2)}, u32[]{:S(2)}) %collective-permute-start) | collective-permute-done | bytes 131104 | tf_op jit(solution)/shard_map/ppermute | solution.py:168
  10.5 3.0 %collective-permute-start.1 = (f32[8,4096]{1,0:T(8,128)S(1)}, f32[8,4096]{1,0:T(8,128)S(1)}, u32[]{:S(2)}, u32[]{:S(2)}) collective-permute-start(f32[8,4096]{1,0:T(8,128)S(1)} %add.29), channel_id=1, source_target_pairs={{0,2},{1,3},{2,0},{3,1},{4,6},{5,7},{6,4},{7,5},{8,10},{9,11},{10,... | collective-permute-start | bytes 393224 | tf_op jit(solution)/shard_map/ppermute | solution.py:168
  13.5 3.8 %collective-permute-done.1 = f32[8,4096]{1,0:T(8,128)S(1)} collective-permute-done((f32[8,4096]{1,0:T(8,128)S(1)}, f32[8,4096]{1,0:T(8,128)S(1)}, u32[]{:S(2)}, u32[]{:S(2)}) %collective-permute-start.1) | collective-permute-done | bytes 131104 | tf_op jit(solution)/shard_map/ppermute | solution.py:168
  17.3 3.8 %collective-permute-start.2 = (f32[8,4096]{1,0:T(8,128)S(1)}, f32[8,4096]{1,0:T(8,128)S(1)}, u32[]{:S(2)}, u32[]{:S(2)}) collective-permute-start(f32[8,4096]{1,0:T(8,128)S(1)} %add.30), channel_id=1, source_target_pairs={{0,6},{1,7},{2,4},{3,5},{4,2},{5,3},{6,0},{7,1},{8,14},{9,15},{10,... | collective-permute-start | bytes 393224 | tf_op jit(solution)/shard_map/ppermute | solution.py:168
  21.2 3.1 %collective-permute-done.2 = f32[8,4096]{1,0:T(8,128)S(1)} collective-permute-done((f32[8,4096]{1,0:T(8,128)S(1)}, f32[8,4096]{1,0:T(8,128)S(1)}, u32[]{:S(2)}, u32[]{:S(2)}) %collective-permute-start.2) | collective-permute-done | bytes 131104 | tf_op jit(solution)/shard_map/ppermute | solution.py:168
  24.3 0.1 collective-permute-start.3
  24.4 1.3 %collective-permute-done.3.other_ref = f32[8,4096]{1,0:T(8,128)S(1)} collective-permute-done((f32[8,4096]{1,0:T(8,128)S(1)}, f32[8,4096]{1,0:T(8,128)S(1)}, u32[]{:S(2)}, u32[]{:S(2)}) %collective-permute-start.3) | collective-permute-done | bytes 131104 | tf_op jit(solution)/shard_map/ppermute | solution.py:168
  25.7 2.8 %shard_map.68 = (f32[8,4096]{1,0:T(8,128)S(1)}, f32[8,4096]{1,0:T(8,128)S(1)}, f32[1,32]{1,0:T(1,128)}) custom-call(s32[1,4]{1,0:T(1,128)S(1)} %copy-done.1, s32[1]{0:T(128)S(6)} %copy.7.reg_ref, s32[1]{0:T(128)} %bitcast.core_ref, s32[1,32]{1,0:T(1,128)S(1)} %bitcast.10, f32[8,4096]{1,0:T(8,128)S(1)} %add.31.own_ref, ...), custom_call_target="tpu_custom_call" | custom-call | tf_op jit(solution)/shard_map/pallas_call | solution.py:209
  28.5 0.2 collective-permute-start.4
  28.7 1.2 %collective-permute-done.4 = f32[8,4096]{1,0:T(8,128)S(1)} collective-permute-done((f32[8,4096]{1,0:T(8,128)S(1)}, f32[8,4096]{1,0:T(8,128)S(1)}, u32[]{:S(2)}, u32[]{:S(2)}) %collective-permute-start.4) | collective-permute-done | bytes 131104 | tf_op jit(solution)/shard_map/ppermute | solution.py:168
  29.9 2.4 %collective-permute-start.5 = (f32[8,4096]{1,0:T(8,128)S(1)}, f32[8,4096]{1,0:T(8,128)S(1)}, u32[]{:S(2)}, u32[]{:S(2)}) collective-permute-start(f32[8,4096]{1,0:T(8,128)S(1)} %add.32), channel_id=1, source_target_pairs={{0,2},{1,3},{2,0},{3,1},{4,6},{5,7},{6,4},{7,5},{8,10},{9,11},{10,... | collective-permute-start | bytes 393224 | tf_op jit(solution)/shard_map/ppermute | solution.py:168
  32.3 3.8 %collective-permute-done.5 = f32[8,4096]{1,0:T(8,128)S(1)} collective-permute-done((f32[8,4096]{1,0:T(8,128)S(1)}, f32[8,4096]{1,0:T(8,128)S(1)}, u32[]{:S(2)}, u32[]{:S(2)}) %collective-permute-start.5) | collective-permute-done | bytes 131104 | tf_op jit(solution)/shard_map/ppermute | solution.py:168
  36.2 3.1 %collective-permute-start.6 = (f32[8,4096]{1,0:T(8,128)S(1)}, f32[8,4096]{1,0:T(8,128)S(1)}, u32[]{:S(2)}, u32[]{:S(2)}) collective-permute-start(f32[8,4096]{1,0:T(8,128)S(1)} %add.33), channel_id=1, source_target_pairs={{0,6},{1,7},{2,4},{3,5},{4,2},{5,3},{6,0},{7,1},{8,14},{9,15},{10,... | collective-permute-start | bytes 393224 | tf_op jit(solution)/shard_map/ppermute | solution.py:168
  39.3 3.8 %collective-permute-done.6 = f32[8,4096]{1,0:T(8,128)S(1)} collective-permute-done((f32[8,4096]{1,0:T(8,128)S(1)}, f32[8,4096]{1,0:T(8,128)S(1)}, u32[]{:S(2)}, u32[]{:S(2)}) %collective-permute-start.6) | collective-permute-done | bytes 131104 | tf_op jit(solution)/shard_map/ppermute | solution.py:168
  43.1 0.1 collective-permute-start.7
  43.2 1.3 %collective-permute-done.7 = f32[8,4096]{1,0:T(8,128)S(1)} collective-permute-done((f32[8,4096]{1,0:T(8,128)S(1)}, f32[8,4096]{1,0:T(8,128)S(1)}, u32[]{:S(2)}, u32[]{:S(2)}) %collective-permute-start.7) | collective-permute-done | bytes 131104 | tf_op jit(solution)/shard_map/ppermute | solution.py:168
  44.6 0.0 copy-start.2
  44.6 0.6 %copy-done.2 = f32[1,32]{1,0:T(1,128)S(1)} copy-done((f32[1,32]{1,0:T(1,128)S(1)}, f32[1,32]{1,0:T(1,128)}, u32[]{:S(2)}) %copy-start.2) | copy-done | bytes 152
  45.2 1.8 %shard_map.69 = (f32[1,32]{1,0:T(1,128)}, f32[64,128]{1,0:T(8,128)S(1)}, f32[1,1]{1,0:T(1,128)}) custom-call(s32[1]{0:T(128)S(6)} %copy.7.reg_ref, s32[1]{0:T(128)} %bitcast.core_ref, s32[1,32]{1,0:T(1,128)S(1)} %bitcast.11, f32[8,4096]{1,0:T(8,128)S(1)} %get-tuple-element.25.own_ref, f32[8,4096]{1,0:T(8,128)S(1)} %add.36.other_ref, f32[1,32]{1,0:T(1,128)S(1)} %copy-done.2, ...), custom_call_target="tpu_custom_call" | custom-call | tf_op jit(solution)/shard_map/pallas_call | solution.py:216
  47.0 10.5 %all_to_all.11 = f32[8,8,128]{2,1,0:T(8,128)S(1)} all-to-all(f32[8,8,128]{2,1,0:T(8,128)S(1)} %bitcast.8), channel_id=1, replica_groups=mesh['grp'=4,'blk'=8] {'blk'}, dimensions={0} | all-to-all | bytes 65536 | tf_op jit(solution)/shard_map/all_to_all | solution.py:221
  57.4 1.2 %shard_map.70 = f32[1,1]{1,0:T(1,128)} custom-call(f32[64,128]{1,0:T(8,128)S(1)} %bitcast.7, f32[1,1]{1,0:T(1,128)} %get-tuple-element.24.norm_ref), custom_call_target="tpu_custom_call" | custom-call | tf_op jit(solution)/shard_map/pallas_call | solution.py:222
  (7 shorter events, 0.1 us)
Async XLA Ops:
  1.3 0.7 %copy-start = (s32[32]{0:T(128)S(1)}, s32[32]{0:T(128)}, u32[]{:S(2)}) copy-start(s32[32]{0:T(128)} %param.5) | copy-start | bytes 388
  1.9 0.7 %copy-start.1 = (s32[1,4]{1,0:T(1,128)S(1)}, s32[1,4]{1,0:T(1,128)}, u32[]{:S(2)}) copy-start(s32[1,4]{1,0:T(1,128)} %order_ref.3) | copy-start | bytes 52
  9.0 1.5 %collective-permute-start = (f32[8,4096]{1,0:T(8,128)S(1)}, f32[8,4096]{1,0:T(8,128)S(1)}, u32[]{:S(2)}, u32[]{:S(2)}) collective-permute-start(f32[8,4096]{1,0:T(8,128)S(1)} %get-tuple-element.15), channel_id=1, source_target_pairs={{0,1},{1,0},{2,3},{3,2},{4,5},{5,4},{6,7},{7,6},{8,9},{9,8},{10,11... | collective-permute-start | bytes 393224 | tf_op jit(solution)/shard_map/ppermute | solution.py:168
  10.5 6.8 %collective-permute-start.1 = (f32[8,4096]{1,0:T(8,128)S(1)}, f32[8,4096]{1,0:T(8,128)S(1)}, u32[]{:S(2)}, u32[]{:S(2)}) collective-permute-start(f32[8,4096]{1,0:T(8,128)S(1)} %add.29), channel_id=1, source_target_pairs={{0,2},{1,3},{2,0},{3,1},{4,6},{5,7},{6,4},{7,5},{8,10},{9,11},{10,... | collective-permute-start | bytes 393224 | tf_op jit(solution)/shard_map/ppermute | solution.py:168
  17.3 6.9 %collective-permute-start.2 = (f32[8,4096]{1,0:T(8,128)S(1)}, f32[8,4096]{1,0:T(8,128)S(1)}, u32[]{:S(2)}, u32[]{:S(2)}) collective-permute-start(f32[8,4096]{1,0:T(8,128)S(1)} %add.30), channel_id=1, source_target_pairs={{0,6},{1,7},{2,4},{3,5},{4,2},{5,3},{6,0},{7,1},{8,14},{9,15},{10,... | collective-permute-start | bytes 393224 | tf_op jit(solution)/shard_map/ppermute | solution.py:168
  24.3 1.4 %collective-permute-start.3 = (f32[8,4096]{1,0:T(8,128)S(1)}, f32[8,4096]{1,0:T(8,128)S(1)}, u32[]{:S(2)}, u32[]{:S(2)}) collective-permute-start(f32[8,4096]{1,0:T(8,128)S(1)} %add.31.own_ref), channel_id=1, source_target_pairs={{0,1},{1,0},{2,3},{3,2},{4,5},{5,4},{6,7},{7,6},{8,9},{9,8},{10,11... | collective-permute-start | bytes 393224 | tf_op jit(solution)/shard_map/ppermute | solution.py:168
  28.5 1.4 %collective-permute-start.4 = (f32[8,4096]{1,0:T(8,128)S(1)}, f32[8,4096]{1,0:T(8,128)S(1)}, u32[]{:S(2)}, u32[]{:S(2)}) collective-permute-start(f32[8,4096]{1,0:T(8,128)S(1)} %get-tuple-element.21), channel_id=1, source_target_pairs={{0,1},{1,0},{2,3},{3,2},{4,5},{5,4},{6,7},{7,6},{8,9},{9,8},{10,11... | collective-permute-start | bytes 393224 | tf_op jit(solution)/shard_map/ppermute | solution.py:168
  29.9 6.2 %collective-permute-start.5 = (f32[8,4096]{1,0:T(8,128)S(1)}, f32[8,4096]{1,0:T(8,128)S(1)}, u32[]{:S(2)}, u32[]{:S(2)}) collective-permute-start(f32[8,4096]{1,0:T(8,128)S(1)} %add.32), channel_id=1, source_target_pairs={{0,2},{1,3},{2,0},{3,1},{4,6},{5,7},{6,4},{7,5},{8,10},{9,11},{10,... | collective-permute-start | bytes 393224 | tf_op jit(solution)/shard_map/ppermute | solution.py:168
  36.2 6.9 %collective-permute-start.6 = (f32[8,4096]{1,0:T(8,128)S(1)}, f32[8,4096]{1,0:T(8,128)S(1)}, u32[]{:S(2)}, u32[]{:S(2)}) collective-permute-start(f32[8,4096]{1,0:T(8,128)S(1)} %add.33), channel_id=1, source_target_pairs={{0,6},{1,7},{2,4},{3,5},{4,2},{5,3},{6,0},{7,1},{8,14},{9,15},{10,... | collective-permute-start | bytes 393224 | tf_op jit(solution)/shard_map/ppermute | solution.py:168
  43.1 1.4 %collective-permute-start.7 = (f32[8,4096]{1,0:T(8,128)S(1)}, f32[8,4096]{1,0:T(8,128)S(1)}, u32[]{:S(2)}, u32[]{:S(2)}) collective-permute-start(f32[8,4096]{1,0:T(8,128)S(1)} %get-tuple-element.26), channel_id=1, source_target_pairs={{0,1},{1,0},{2,3},{3,2},{4,5},{5,4},{6,7},{7,6},{8,9},{9,8},{10,11... | collective-permute-start | bytes 393224 | tf_op jit(solution)/shard_map/ppermute | solution.py:168
  44.6 0.7 %copy-start.2 = (f32[1,32]{1,0:T(1,128)S(1)}, f32[1,32]{1,0:T(1,128)}, u32[]{:S(2)}) copy-start(f32[1,32]{1,0:T(1,128)} %get-tuple-element.19.dual_ref) | copy-start | bytes 388

commit v3 on v2

v3 whole, which is shorter than its diff:
```python
import functools
import math

import jax
import jax.numpy as jnp
from jax import lax
from jax.experimental import pallas as pl
from jax.experimental.pallas import tpu as pltpu
from jax.sharding import PartitionSpec as P

ROUNDS = 2
SEGMENTS = 8
LOADS = 8
LANES = 128
VMEM_LIMIT = 12 * 1024 * 1024

F32 = jnp.float32
BF16 = jnp.bfloat16
NT = (((1,), (1,)), ((), ()))
NN = (((1,), (0,)), ((), ()))

SIGNS, VISIT, RATE, DUAL, FULL, TOTAL, STRENGTH = range(7)


def row_of(state_ref, row, count):
    return state_ref[row : row + 1, 0:count]


def ascend(couple, visit, blocks, signs, dual, rate, score):
    rows = couple.shape[0]
    eye = lax.broadcasted_iota(jnp.int32, (rows, rows), 0) == lax.broadcasted_iota(
        jnp.int32, (rows, rows), 1
    )
    change = jnp.zeros_like(dual)
    for position in range(blocks):
        current = dual + change
        updated = jnp.clip(current + rate * (1.0 - signs * score), 0.0, 1.0)
        step = jnp.where(visit == float(position), updated - current, 0.0)
        change = change + step
        if position < blocks - 1:
            coefficient = (signs * step).astype(BF16).astype(F32)
            column = jnp.sum(jnp.where(eye, coefficient, 0.0), axis=1, keepdims=True)
            score = score + jnp.sum(couple * column, axis=0, keepdims=True)
    return change


def weight_change(full, x_ref, out_ref, half, scale):
    rows, features = x_ref.shape
    length = features // 2 // SEGMENTS
    depth = SEGMENTS * rows
    spread = (
        lax.broadcasted_iota(jnp.int32, (rows, depth), 1) % rows
        == lax.broadcasted_iota(jnp.int32, (rows, depth), 0)
    )
    left = jnp.broadcast_to(full, (SEGMENTS, rows)).astype(BF16)
    wide = lax.dot_general(
        left, jnp.where(spread, 1.0, 0.0).astype(BF16), NN, preferred_element_type=F32
    )
    segment_of = lax.broadcasted_iota(jnp.int32, (SEGMENTS, depth), 1) // rows
    wanted = lax.broadcasted_iota(jnp.int32, (SEGMENTS, depth), 0)
    wide = jnp.where(segment_of == wanted, wide, 0.0).astype(BF16)
    width = min(length, 512)
    base = half * (features // 2)
    for begin in range(0, length, width):
        stacked = jnp.concatenate(
            [
                x_ref[:, pl.ds(pl.multiple_of(base + g * length + begin, LANES), width)]
                for g in range(SEGMENTS)
            ],
            axis=0,
        )
        out_ref[:, begin : begin + width] = scale * lax.dot_general(
            wide, stacked, NN, preferred_element_type=F32
        )


def scores(x_ref, weights, half):
    rows, features = x_ref.shape
    length = features // 2 // SEGMENTS
    base = half * (features // 2)
    weights = weights.astype(BF16)
    total = jnp.zeros((SEGMENTS, rows), F32)
    row = lax.broadcasted_iota(jnp.int32, (SEGMENTS, rows), 0)
    for g in range(SEGMENTS):
        part = lax.dot_general(
            weights,
            x_ref[:, pl.ds(pl.multiple_of(base + g * length, LANES), length)],
            NT,
            preferred_element_type=F32,
        )
        total = total + jnp.where(row == g, part, 0.0)
    return jnp.sum(total, axis=0, keepdims=True)


def core_index():
    return lax.rem(lax.axis_index("blk"), 2)


def first_kernel(samples, sigma, reg_ref, order_hbm, label_hbm, data_hbm,
                 send_ref, couple_ref, state_ref, x_ref,
                 order_ref, label_ref, arrived, small):
    rows, features = x_ref.shape
    blocks = order_ref.shape[1]
    width = features // LOADS
    copies = [
        pltpu.make_async_copy(
            data_hbm.at[:, pl.ds(k * width, width)],
            x_ref.at[:, pl.ds(k * width, width)],
            arrived.at[k],
        )
        for k in range(LOADS)
    ]
    for copy in copies:
        copy.start()
    fetches = [
        pltpu.make_async_copy(order_hbm, order_ref, small.at[0]),
        pltpu.make_async_copy(label_hbm, label_ref, small.at[1]),
    ]
    for fetch in fetches:
        fetch.start()
    gram = jnp.zeros((rows, rows), F32)
    for k in range(LOADS):
        copies[k].wait()
        piece = x_ref[:, k * width : (k + 1) * width]
        gram = gram + lax.dot_general(piece, piece, NT, preferred_element_type=F32)
    for fetch in fetches:
        fetch.wait()
    signs = label_ref[...].astype(F32)
    index = jnp.full((1, rows), reg_ref[0], jnp.int32).astype(F32)
    strength = 0.04 * jnp.exp(0.5 * math.log(2.0) * index)
    total = strength * samples
    block_of = lax.broadcasted_iota(jnp.int32, (1, rows), 1) // (rows // blocks)
    visit = jnp.zeros((1, rows), F32)
    for position in range(1, blocks):
        visit = jnp.where(block_of == order_ref[0, position], float(position), visit)
    eye = lax.broadcasted_iota(jnp.int32, (rows, rows), 0) == lax.broadcasted_iota(
        jnp.int32, (rows, rows), 1
    )
    squared = jnp.sum(jnp.where(eye, gram, 0.0), axis=0, keepdims=True) / features + 1e-06
    rate = total / (sigma * squared)
    couple = gram * (sigma / features / total)
    none = jnp.zeros((1, rows), F32)
    change = ascend(couple, visit, blocks, signs, none, rate, none)
    full = (signs * change).astype(BF16).astype(F32)
    couple_ref[...] = couple
    state_ref[...] = jnp.zeros_like(state_ref)
    for row, value in (
        (SIGNS, signs), (VISIT, visit), (RATE, rate), (DUAL, change),
        (FULL, full), (TOTAL, total), (STRENGTH, strength),
    ):
        state_ref[row : row + 1, 0:rows] = value
    scale = 1.0 / math.sqrt(features) / total[:, 0:1]
    weight_change(full, x_ref, send_ref, 1 - core_index(), scale)


def change_kernel(state_ref, x_ref, keep_ref):
    rows, features = x_ref.shape
    scale = 1.0 / math.sqrt(features) / row_of(state_ref, TOTAL, 1)
    weight_change(row_of(state_ref, FULL, rows), x_ref, keep_ref, core_index(), scale)


def score_kernel(own_ref, x_ref, part_ref):
    part_ref[...] = scores(x_ref, own_ref[...], core_index())


def next_kernel(blocks, part_ref, other_ref, couple_ref, state_ref, x_ref, send_ref, new_ref):
    rows, features = x_ref.shape
    signs = row_of(state_ref, SIGNS, rows)
    dual = row_of(state_ref, DUAL, rows)
    score = part_ref[...] + scores(x_ref, other_ref[...], 1 - core_index())
    score = 1.0 / math.sqrt(features) * score
    change = ascend(
        couple_ref[...], row_of(state_ref, VISIT, rows), blocks, signs, dual,
        row_of(state_ref, RATE, rows), score,
    )
    full = (signs * change).astype(BF16).astype(F32)
    new_ref[...] = state_ref[...]
    new_ref[DUAL : DUAL + 1, 0:rows] = dual + change
    new_ref[FULL : FULL + 1, 0:rows] = full
    scale = 1.0 / math.sqrt(features) / row_of(state_ref, TOTAL, 1)
    weight_change(full, x_ref, send_ref, 1 - core_index(), scale)


def last_kernel(part_ref, own_ref, other_ref, state_ref, x_ref, dual_ref, margin_ref, share_ref, norm_ref):
    rows, features = x_ref.shape
    signs = row_of(state_ref, SIGNS, rows)
    dual = row_of(state_ref, DUAL, rows)
    margins = part_ref[...] + scores(x_ref, other_ref[...], 1 - core_index())
    margins = 1.0 / math.sqrt(features) * margins
    hinge = jnp.maximum(0.0, 1.0 - signs * margins)
    share = jnp.sum(hinge - dual, axis=1, keepdims=True)
    share_ref[...] = jnp.broadcast_to(share, share_ref.shape)
    own, other = own_ref[...], other_ref[...]
    low = jnp.sum(jnp.sum(own * own, axis=0, keepdims=True), axis=1, keepdims=True)
    high = jnp.sum(jnp.sum(other * other, axis=0, keepdims=True), axis=1, keepdims=True)
    norm = row_of(state_ref, STRENGTH, 1) * (low + high)
    norm_ref[...] = jnp.broadcast_to(norm, norm_ref.shape)
    dual_ref[...] = dual
    margin_ref[...] = margins


def swap(value, peers, mask):
    return lax.ppermute(value, "blk", [(i, i ^ mask) for i in range(peers)])


def reduce_half(keep, arrived, peers):
    own = keep + arrived
    mask = 1
    while mask < peers // 2:
        own = own + swap(own, peers, 2 * mask)
        mask = 2 * mask + 1
    return own


def call(body, outs, spaces, scratch=(), work=0):
    return pl.pallas_call(
        body,
        out_shape=[jax.ShapeDtypeStruct(shape, dtype) for shape, dtype in outs],
        in_specs=[pl.BlockSpec(memory_space=space) for space in spaces],
        out_specs=[pl.BlockSpec(memory_space=pltpu.VMEM) for _ in outs],
        scratch_shapes=list(scratch),
        compiler_params=pltpu.CompilerParams(vmem_limit_bytes=VMEM_LIMIT),
        cost_estimate=pl.CostEstimate(flops=work, bytes_accessed=work // 64, transcendentals=0),
    )


def shards(data, labels, order, reg_index):
    peers = lax.axis_size("blk")
    rows, features = data.shape
    blocks = order.shape[1]
    samples = rows * peers
    work = 32 * rows * features
    half = ((SEGMENTS, features // 2 // SEGMENTS), F32)
    line = ((1, rows), F32)
    state_shape = ((8, LANES), F32)
    V, H = pltpu.VMEM, pltpu.HBM
    pinned = [
        pltpu.with_memory_space_constraint(a, H)
        for a in (order, labels.reshape(1, rows), data)
    ]
    send, couple, state, x = call(
        functools.partial(first_kernel, samples, float(peers)),
        [half, ((rows, rows), F32), state_shape, ((rows, features), BF16)],
        [pltpu.SMEM, H, H, H],
        [
            pltpu.SMEM(order.shape, jnp.int32),
            pltpu.VMEM((1, rows), jnp.int32),
            pltpu.SemaphoreType.DMA((LOADS,)),
            pltpu.SemaphoreType.DMA((2,)),
        ],
        work,
    )(reg_index, *pinned)
    own = None
    for index in range(ROUNDS):
        arrived = swap(send, peers, 1)
        (keep,) = call(change_kernel, [half], [V, V], work=work)(state, x)
        more = reduce_half(keep, arrived, peers)
        own = more if own is None else own + more
        other = swap(own, peers, 1)
        (part,) = call(score_kernel, [line], [V, V], work=work)(own, x)
        if index < ROUNDS - 1:
            send, state = call(
                functools.partial(next_kernel, blocks), [half, state_shape], [V] * 5, work=work
            )(part, other, couple, state, x)
    dual, margins, share, norm = call(
        last_kernel,
        [line, line, ((1, LANES), F32), ((1, LANES), F32)],
        [V] * 5,
        work=work,
    )(part, own, other, state, x)
    mask = 1
    while mask < peers:
        share = share + swap(share, peers, mask)
        mask *= 2
    gap = norm[0:1, 0:1] + share[0:1, 0:1] / samples
    return dual.reshape(rows), margins.reshape(rows), gap.reshape(1)


def solution(mesh):
    placed = (P("blk", None), P("blk"), P("blk", None), P("grp"))
    return jax.shard_map(
        shards,
        mesh=mesh,
        in_specs=placed,
        out_specs=(P(("grp", "blk")), P(("grp", "blk")), P("grp")),
        check_vma=False,
    )
```

time: 58.8 us -> 53.4 us (0.908)
  blocking collectives: 10.5 us -> 0 us
  starting transfers between devices: 13.2 us -> 19 us
  local copies, waits for them, and re-layouts: 1.95 us -> 0 us
  waiting for transfers between devices: 19.4 us -> 21.2 us
  Pallas kernels: 12.1 us -> 10.3 us
  between operations: 1.35 us -> 2.54 us
    all_to_all x1 -> x0, blocking collectives: 10.5 us -> none  [shards(): share = lax.all_to_all(share, 'blk', 0, 0, tiled=True)]
    ppermute x8 -> x11, starting transfers between devices: 13.2 us -> 19 us  [swap(): return lax.ppermute(value, 'blk', [(i, i ^ mask) for i in range(peers)])]
    unnamed x6 -> x0, local copies, waits for them, and re-layouts: 1.95 us -> none
    ppermute x8 -> x11, waiting for transfers between devices: 19.4 us -> 21.2 us  [swap(): return lax.ppermute(value, 'blk', [(i, i ^ mask) for i in range(peers)])]
    pallas_call x4 -> x7, Pallas kernels: 12.1 us -> 10.3 us  [the longest x1 5.33 us: shards(): call(functools.partial(first_kernel, samples, float(peers)), [half, ((row...]
  transfers between devices with their start and end apart: 8 -> 11, of which waited for: 8 -> 11; matrix products, arithmetic and copies ran while one was open for 0% -> 0% of each run, Pallas kernels for 0% -> 4%
where the time goes in v3:
time: 53.4 us; the launch traced here: 53.2 us
  waiting for transfers between devices  21.2 us (40%)
  starting transfers between devices  19 us (36%)
  Pallas kernels  10.3 us (19%)
  between operations  2.54 us (5%)
    ppermute x11, waiting for transfers between devices, swap(): return lax.ppermute(value, 'blk', [(i, i ^ mask) for i in range(peers)])  21.2 us
    ppermute x11, starting transfers between devices, swap(): return lax.ppermute(value, 'blk', [(i, i ^ mask) for i in range(peers)])  19 us
    pallas_call x1, Pallas kernels, shards(): call(functools.partial(first_kernel, samples, float(peers)), [half, ((row...  5.33 us
    pallas_call x1, Pallas kernels, shards(): call(functools.partial(next_kernel, blocks), [half, state_shape], [V] * 5...  1.46 us
    pallas_call x2, Pallas kernels, shards(): part, = call(score_kernel, [line], [V, V], work=work)(own, x)  1.35 us
    pallas_call x1, Pallas kernels, shards(): call(last_kernel, [line, line, ((1, LANES), F32), ((1, LANES), F32)], [V]...  1.19 us
  transfers between devices with their start and end apart: 11, of which 11 were waited for; matrix products, arithmetic and copies ran while one was open for 0% of the time, Pallas kernels for 4%

profile of v3, /device:TPU:0, one launch (start us, length us, event | category | flops | bytes accessed | tf_op | source)
XLA Modules:
  0.0 53.2 jit_solution(6190413887549012325)
XLA Ops:
  1.3 5.3 %shard_map.67 = (f32[8,4096]{1,0:T(8,128)S(1)}, f32[32,32]{1,0:T(8,128)S(1)}, f32[8,128]{1,0:T(8,128)S(1)}, bf16[32,65536]{1,0:T(8,128)(2,1)S(1)}) custom-call(s32[1]{0:T(128)S(6)} %copy.7.reg_ref, s32[1,4]{1,0:T(1,128)} %order_hbm.1, s32[1,32]{1,0:T(1,128)} %bitcast.7, bf16[32,65536]{1,0:T(8,128)(2,1)} %data_hbm.1), custom_call_target="tpu_custom_call" | custom-call | flops 67108864 | bytes 1048576 | tf_op jit(solution)/shard_map/pallas_call | solution.py:241
  6.6 0.6 %collective-permute-start = (f32[8,4096]{1,0:T(8,128)S(1)}, f32[8,4096]{1,0:T(8,128)S(1)}, u32[]{:S(2)}, u32[]{:S(2)}) collective-permute-start(f32[8,4096]{1,0:T(8,128)S(1)} %get-tuple-element.15), channel_id=1, source_target_pairs={{0,1},{1,0},{2,3},{3,2},{4,5},{5,4},{6,7},{7,6},{8,9},{9,8},{10,11... | collective-permute-start | bytes 393224 | tf_op jit(solution)/shard_map/ppermute | solution.py:203
  7.2 0.5 shard_map.68
  7.7 0.5 collective-permute-done
  8.2 3.0 %collective-permute-start.1 = (f32[8,4096]{1,0:T(8,128)S(1)}, f32[8,4096]{1,0:T(8,128)S(1)}, u32[]{:S(2)}, u32[]{:S(2)}) collective-permute-start(f32[8,4096]{1,0:T(8,128)S(1)} %add.33), channel_id=1, source_target_pairs={{0,2},{1,3},{2,0},{3,1},{4,6},{5,7},{6,4},{7,5},{8,10},{9,11},{10,... | collective-permute-start | bytes 393224 | tf_op jit(solution)/shard_map/ppermute | solution.py:203
  11.2 3.8 %collective-permute-done.1 = f32[8,4096]{1,0:T(8,128)S(1)} collective-permute-done((f32[8,4096]{1,0:T(8,128)S(1)}, f32[8,4096]{1,0:T(8,128)S(1)}, u32[]{:S(2)}, u32[]{:S(2)}) %collective-permute-start.1) | collective-permute-done | bytes 131104 | tf_op jit(solution)/shard_map/ppermute | solution.py:203
  15.0 3.8 %collective-permute-start.2 = (f32[8,4096]{1,0:T(8,128)S(1)}, f32[8,4096]{1,0:T(8,128)S(1)}, u32[]{:S(2)}, u32[]{:S(2)}) collective-permute-start(f32[8,4096]{1,0:T(8,128)S(1)} %add.34), channel_id=1, source_target_pairs={{0,6},{1,7},{2,4},{3,5},{4,2},{5,3},{6,0},{7,1},{8,14},{9,15},{10,... | collective-permute-start | bytes 393224 | tf_op jit(solution)/shard_map/ppermute | solution.py:203
  18.8 3.1 %collective-permute-done.2 = f32[8,4096]{1,0:T(8,128)S(1)} collective-permute-done((f32[8,4096]{1,0:T(8,128)S(1)}, f32[8,4096]{1,0:T(8,128)S(1)}, u32[]{:S(2)}, u32[]{:S(2)}) %collective-permute-start.2) | collective-permute-done | bytes 131104 | tf_op jit(solution)/shard_map/ppermute | solution.py:203
  22.0 0.1 collective-permute-start.3
  22.0 0.7 %shard_map.69.part_ref = f32[1,32]{1,0:T(1,128)S(1)} custom-call(f32[8,4096]{1,0:T(8,128)S(1)} %add.35.own_ref, bf16[32,65536]{1,0:T(8,128)(2,1)S(1)} %get-tuple-element.14.x_ref), custom_call_target="tpu_custom_call" | custom-call | flops 67108864 | bytes 1048576 | tf_op jit(solution)/shard_map/pallas_call | solution.py:260
  22.7 0.7 %collective-permute-done.3.other_ref = f32[8,4096]{1,0:T(8,128)S(1)} collective-permute-done((f32[8,4096]{1,0:T(8,128)S(1)}, f32[8,4096]{1,0:T(8,128)S(1)}, u32[]{:S(2)}, u32[]{:S(2)}) %collective-permute-start.3) | collective-permute-done | bytes 131104 | tf_op jit(solution)/shard_map/ppermute | solution.py:203
  23.4 1.5 %shard_map.70 = (f32[8,4096]{1,0:T(8,128)S(1)}, f32[8,128]{1,0:T(8,128)S(1)}) custom-call(f32[1,32]{1,0:T(1,128)S(1)} %shard_map.69.part_ref, f32[8,4096]{1,0:T(8,128)S(1)} %collective-permute-done.3.other_ref, f32[32,32]{1,0:T(8,128)S(1)} %get-tuple-element.16.couple_ref, f32[8,128]{1,0:T(8,128)S(1)} %get-tuple-element.13.state_ref, ...), custom_call_target="tpu_custom_call" | custom-call | flops 67108864 | bytes 1048576 | tf_op jit(solution)/shard_map/pallas_call | solution.py:262
  24.8 0.2 collective-permute-start.4
  25.0 0.5 shard_map.71
  25.5 0.7 %collective-permute-done.4 = f32[8,4096]{1,0:T(8,128)S(1)} collective-permute-done((f32[8,4096]{1,0:T(8,128)S(1)}, f32[8,4096]{1,0:T(8,128)S(1)}, u32[]{:S(2)}, u32[]{:S(2)}) %collective-permute-start.4) | collective-permute-done | bytes 131104 | tf_op jit(solution)/shard_map/ppermute | solution.py:203
  26.2 2.4 %collective-permute-start.5 = (f32[8,4096]{1,0:T(8,128)S(1)}, f32[8,4096]{1,0:T(8,128)S(1)}, u32[]{:S(2)}, u32[]{:S(2)}) collective-permute-start(f32[8,4096]{1,0:T(8,128)S(1)} %add.36), channel_id=1, source_target_pairs={{0,2},{1,3},{2,0},{3,1},{4,6},{5,7},{6,4},{7,5},{8,10},{9,11},{10,... | collective-permute-start | bytes 393224 | tf_op jit(solution)/shard_map/ppermute | solution.py:203
  28.6 3.8 %collective-permute-done.5 = f32[8,4096]{1,0:T(8,128)S(1)} collective-permute-done((f32[8,4096]{1,0:T(8,128)S(1)}, f32[8,4096]{1,0:T(8,128)S(1)}, u32[]{:S(2)}, u32[]{:S(2)}) %collective-permute-start.5) | collective-permute-done | bytes 131104 | tf_op jit(solution)/shard_map/ppermute | solution.py:203
  32.5 3.1 %collective-permute-start.6 = (f32[8,4096]{1,0:T(8,128)S(1)}, f32[8,4096]{1,0:T(8,128)S(1)}, u32[]{:S(2)}, u32[]{:S(2)}) collective-permute-start(f32[8,4096]{1,0:T(8,128)S(1)} %add.37), channel_id=1, source_target_pairs={{0,6},{1,7},{2,4},{3,5},{4,2},{5,3},{6,0},{7,1},{8,14},{9,15},{10,... | collective-permute-start | bytes 393224 | tf_op jit(solution)/shard_map/ppermute | solution.py:203
  35.6 3.8 %collective-permute-done.6 = f32[8,4096]{1,0:T(8,128)S(1)} collective-permute-done((f32[8,4096]{1,0:T(8,128)S(1)}, f32[8,4096]{1,0:T(8,128)S(1)}, u32[]{:S(2)}, u32[]{:S(2)}) %collective-permute-start.6) | collective-permute-done | bytes 131104 | tf_op jit(solution)/shard_map/ppermute | solution.py:203
  39.4 0.1 collective-permute-start.7
  39.5 0.7 %shard_map.72.part_ref = f32[1,32]{1,0:T(1,128)S(1)} custom-call(f32[8,4096]{1,0:T(8,128)S(1)} %add_add_fusion.own_ref, bf16[32,65536]{1,0:T(8,128)(2,1)S(1)} %get-tuple-element.14.x_ref), custom_call_target="tpu_custom_call" | custom-call | flops 67108864 | bytes 1048576 | tf_op jit(solution)/shard_map/pallas_call | solution.py:260
  40.2 0.7 %collective-permute-done.7.other_ref = f32[8,4096]{1,0:T(8,128)S(1)} collective-permute-done((f32[8,4096]{1,0:T(8,128)S(1)}, f32[8,4096]{1,0:T(8,128)S(1)}, u32[]{:S(2)}, u32[]{:S(2)}) %collective-permute-start.7) | collective-permute-done | bytes 131104 | tf_op jit(solution)/shard_map/ppermute | solution.py:203
  40.9 1.2 %shard_map.73 = (f32[1,32]{1,0:T(1,128)}, f32[1,32]{1,0:T(1,128)}, f32[1,128]{1,0:T(1,128)S(1)}, f32[1,128]{1,0:T(1,128)S(1)}) custom-call(f32[1,32]{1,0:T(1,128)S(1)} %shard_map.72.part_ref, f32[8,4096]{1,0:T(8,128)S(1)} %add_add_fusion.own_ref, f32[8,4096]{1,0:T(8,128)S(1)} %collective-permute-done.7.other_ref, f32[8,128]{1,0:T(8,128)S(1)} %get-tuple-element.17.state_ref, ...), custom_call_target="tpu_custom_call" | custom-call | flops 67108864 | bytes 1048576 | tf_op jit(solution)/shard_map/pallas_call | solution.py:265
  42.0 0.1 collective-permute-start.8
  42.2 1.0 %collective-permute-done.8 = f32[1,128]{1,0:T(1,128)S(1)} collective-permute-done((f32[1,128]{1,0:T(1,128)S(1)}, f32[1,128]{1,0:T(1,128)S(1)}, u32[]{:S(2)}, u32[]{:S(2)}) %collective-permute-start.8) | collective-permute-done | bytes 544 | tf_op jit(solution)/shard_map/ppermute | solution.py:203
  43.2 2.5 %collective-permute-start.9 = (f32[1,128]{1,0:T(1,128)S(1)}, f32[1,128]{1,0:T(1,128)S(1)}, u32[]{:S(2)}, u32[]{:S(2)}) collective-permute-start(f32[1,128]{1,0:T(1,128)S(1)} %add.40), channel_id=1, source_target_pairs={{0,2},{1,3},{2,0},{3,1},{4,6},{5,7},{6,4},{7,5},{8,10},{9,11},{10,... | collective-permute-start | bytes 1544 | tf_op jit(solution)/shard_map/ppermute | solution.py:203
  45.7 1.5 %collective-permute-done.9 = f32[1,128]{1,0:T(1,128)S(1)} collective-permute-done((f32[1,128]{1,0:T(1,128)S(1)}, f32[1,128]{1,0:T(1,128)S(1)}, u32[]{:S(2)}, u32[]{:S(2)}) %collective-permute-start.9) | collective-permute-done | bytes 544 | tf_op jit(solution)/shard_map/ppermute | solution.py:203
  47.2 3.2 %collective-permute-start.10 = (f32[1,128]{1,0:T(1,128)S(1)}, f32[1,128]{1,0:T(1,128)S(1)}, u32[]{:S(2)}, u32[]{:S(2)}) collective-permute-start(f32[1,128]{1,0:T(1,128)S(1)} %add.41), channel_id=1, source_target_pairs={{0,4},{1,5},{2,6},{3,7},{4,0},{5,1},{6,2},{7,3},{8,12},{9,13},{10,... | collective-permute-start | bytes 1544 | tf_op jit(solution)/shard_map/ppermute | solution.py:203
  50.4 1.5 %collective-permute-done.10 = f32[1,128]{1,0:T(1,128)S(1)} collective-permute-done((f32[1,128]{1,0:T(1,128)S(1)}, f32[1,128]{1,0:T(1,128)S(1)}, u32[]{:S(2)}, u32[]{:S(2)}) %collective-permute-start.10) | collective-permute-done | bytes 544 | tf_op jit(solution)/shard_map/ppermute | solution.py:203
  (9 shorter events, 0.1 us)
Async XLA Ops:
  6.6 1.5 %collective-permute-start = (f32[8,4096]{1,0:T(8,128)S(1)}, f32[8,4096]{1,0:T(8,128)S(1)}, u32[]{:S(2)}, u32[]{:S(2)}) collective-permute-start(f32[8,4096]{1,0:T(8,128)S(1)} %get-tuple-element.15), channel_id=1, source_target_pairs={{0,1},{1,0},{2,3},{3,2},{4,5},{5,4},{6,7},{7,6},{8,9},{9,8},{10,11... | collective-permute-start | bytes 393224 | tf_op jit(solution)/shard_map/ppermute | solution.py:203
  8.2 6.8 %collective-permute-start.1 = (f32[8,4096]{1,0:T(8,128)S(1)}, f32[8,4096]{1,0:T(8,128)S(1)}, u32[]{:S(2)}, u32[]{:S(2)}) collective-permute-start(f32[8,4096]{1,0:T(8,128)S(1)} %add.33), channel_id=1, source_target_pairs={{0,2},{1,3},{2,0},{3,1},{4,6},{5,7},{6,4},{7,5},{8,10},{9,11},{10,... | collective-permute-start | bytes 393224 | tf_op jit(solution)/shard_map/ppermute | solution.py:203
  15.0 6.9 %collective-permute-start.2 = (f32[8,4096]{1,0:T(8,128)S(1)}, f32[8,4096]{1,0:T(8,128)S(1)}, u32[]{:S(2)}, u32[]{:S(2)}) collective-permute-start(f32[8,4096]{1,0:T(8,128)S(1)} %add.34), channel_id=1, source_target_pairs={{0,6},{1,7},{2,4},{3,5},{4,2},{5,3},{6,0},{7,1},{8,14},{9,15},{10,... | collective-permute-start | bytes 393224 | tf_op jit(solution)/shard_map/ppermute | solution.py:203
  22.0 1.4 %collective-permute-start.3 = (f32[8,4096]{1,0:T(8,128)S(1)}, f32[8,4096]{1,0:T(8,128)S(1)}, u32[]{:S(2)}, u32[]{:S(2)}) collective-permute-start(f32[8,4096]{1,0:T(8,128)S(1)} %add.35.own_ref), channel_id=1, source_target_pairs={{0,1},{1,0},{2,3},{3,2},{4,5},{5,4},{6,7},{7,6},{8,9},{9,8},{10,11... | collective-permute-start | bytes 393224 | tf_op jit(solution)/shard_map/ppermute | solution.py:203
  24.8 1.4 %collective-permute-start.4 = (f32[8,4096]{1,0:T(8,128)S(1)}, f32[8,4096]{1,0:T(8,128)S(1)}, u32[]{:S(2)}, u32[]{:S(2)}) collective-permute-start(f32[8,4096]{1,0:T(8,128)S(1)} %get-tuple-element.18), channel_id=1, source_target_pairs={{0,1},{1,0},{2,3},{3,2},{4,5},{5,4},{6,7},{7,6},{8,9},{9,8},{10,11... | collective-permute-start | bytes 393224 | tf_op jit(solution)/shard_map/ppermute | solution.py:203
  26.2 6.2 %collective-permute-start.5 = (f32[8,4096]{1,0:T(8,128)S(1)}, f32[8,4096]{1,0:T(8,128)S(1)}, u32[]{:S(2)}, u32[]{:S(2)}) collective-permute-start(f32[8,4096]{1,0:T(8,128)S(1)} %add.36), channel_id=1, source_target_pairs={{0,2},{1,3},{2,0},{3,1},{4,6},{5,7},{6,4},{7,5},{8,10},{9,11},{10,... | collective-permute-start | bytes 393224 | tf_op jit(solution)/shard_map/ppermute | solution.py:203
  32.5 6.9 %collective-permute-start.6 = (f32[8,4096]{1,0:T(8,128)S(1)}, f32[8,4096]{1,0:T(8,128)S(1)}, u32[]{:S(2)}, u32[]{:S(2)}) collective-permute-start(f32[8,4096]{1,0:T(8,128)S(1)} %add.37), channel_id=1, source_target_pairs={{0,6},{1,7},{2,4},{3,5},{4,2},{5,3},{6,0},{7,1},{8,14},{9,15},{10,... | collective-permute-start | bytes 393224 | tf_op jit(solution)/shard_map/ppermute | solution.py:203
  39.4 1.4 %collective-permute-start.7 = (f32[8,4096]{1,0:T(8,128)S(1)}, f32[8,4096]{1,0:T(8,128)S(1)}, u32[]{:S(2)}, u32[]{:S(2)}) collective-permute-start(f32[8,4096]{1,0:T(8,128)S(1)} %add_add_fusion.own_ref), channel_id=1, source_target_pairs={{0,1},{1,0},{2,3},{3,2},{4,5},{5,4},{6,7},{7,6},{8,9},{9,8},{10,11... | collective-permute-start | bytes 393224 | tf_op jit(solution)/shard_map/ppermute | solution.py:203
  42.0 1.2 %collective-permute-start.8 = (f32[1,128]{1,0:T(1,128)S(1)}, f32[1,128]{1,0:T(1,128)S(1)}, u32[]{:S(2)}, u32[]{:S(2)}) collective-permute-start(f32[1,128]{1,0:T(1,128)S(1)} %get-tuple-element.22), channel_id=1, source_target_pairs={{0,1},{1,0},{2,3},{3,2},{4,5},{5,4},{6,7},{7,6},{8,9},{9,8},{10,11... | collective-permute-start | bytes 1544 | tf_op jit(solution)/shard_map/ppermute | solution.py:203
  43.2 4.0 %collective-permute-start.9 = (f32[1,128]{1,0:T(1,128)S(1)}, f32[1,128]{1,0:T(1,128)S(1)}, u32[]{:S(2)}, u32[]{:S(2)}) collective-permute-start(f32[1,128]{1,0:T(1,128)S(1)} %add.40), channel_id=1, source_target_pairs={{0,2},{1,3},{2,0},{3,1},{4,6},{5,7},{6,4},{7,5},{8,10},{9,11},{10,... | collective-permute-start | bytes 1544 | tf_op jit(solution)/shard_map/ppermute | solution.py:203
  47.2 4.7 %collective-permute-start.10 = (f32[1,128]{1,0:T(1,128)S(1)}, f32[1,128]{1,0:T(1,128)S(1)}, u32[]{:S(2)}, u32[]{:S(2)}) collective-permute-start(f32[1,128]{1,0:T(1,128)S(1)} %add.41), channel_id=1, source_target_pairs={{0,4},{1,5},{2,6},{3,7},{4,0},{5,1},{6,2},{7,3},{8,12},{9,13},{10,... | collective-permute-start | bytes 1544 | tf_op jit(solution)/shard_map/ppermute | solution.py:203

commit v4 on v0

v4 whole, which is shorter than its diff:
```python
import functools
import math

import jax
import jax.numpy as jnp
from jax import lax
from jax.experimental import pallas as pl
from jax.experimental.pallas import tpu as pltpu
from jax.sharding import PartitionSpec as P

ROUNDS = 2
BLOCKS = 4
SEGMENTS = 8
LANES = 128
WIDTH = 1024
VMEM_LIMIT = 12 * 1024 * 1024

F32 = jnp.float32
BF16 = jnp.bfloat16
NT = (((1,), (1,)), ((), ()))
NN = (((1,), (0,)), ((), ()))

STRENGTH, TOTAL, SIGNS = 0, 1, 2
SQUARED, DUAL = SIGNS + BLOCKS, SIGNS + 2 * BLOCKS
PLACES = SIGNS + 3 * BLOCKS

def lane_iota(rows):
    return lax.broadcasted_iota(jnp.int32, (rows, LANES), 1)


def row_iota(rows):
    return lax.broadcasted_iota(jnp.int32, (rows, LANES), 0)


def stacked_block(x_ref, block, begin, width):
    size = LANES // (2 * SEGMENTS)
    length = x_ref.shape[1] // (2 * SEGMENTS)
    rows = pl.ds(pl.multiple_of(block * size, size), size)
    return jnp.concatenate(
        [x_ref[rows, g * length + begin : g * length + begin + width] for g in range(2 * SEGMENTS)],
        axis=0,
    )


def block_left(coefficient):
    size = coefficient.shape[0]
    line = jnp.sum(
        jnp.where(lane_iota(size) % size == row_iota(size), coefficient, 0.0), axis=0, keepdims=True
    )
    height = 2 * SEGMENTS
    return jnp.where(lane_iota(height) // size == row_iota(height), line, 0.0).astype(BF16)


def block_scores(product, size):
    height = product.shape[0]
    line = jnp.sum(
        jnp.where(lane_iota(height) // size == row_iota(height), product, 0.0), axis=0, keepdims=True
    )
    return jnp.sum(
        jnp.where(lane_iota(size) % size == row_iota(size), line, 0.0), axis=1, keepdims=True
    )


def block_step(signs, dual, squared, score, total, sigma):
    updated = jnp.clip(dual + total * (1.0 - signs * score) / (sigma * squared), 0.0, 1.0)
    return updated - dual


def advance(x_ref, local_ref, sum_ref, block, following, coefficient, rate, fresh):
    left = block_left(coefficient)
    length = local_ref.shape[1]
    width = min(length, WIDTH)
    product = jnp.zeros((2 * SEGMENTS, LANES), F32)
    for begin in range(0, length, width):
        columns = slice(begin, begin + width)
        update = lax.dot_general(
            left, stacked_block(x_ref, block, begin, width), NN, preferred_element_type=F32
        )
        sum_ref[:, columns] = update if fresh else sum_ref[:, columns] + update
        if following is not None:
            local = rate * update if local_ref is None else local_ref[:, columns] + rate * update
            local_ref[:, columns] = local
            product = product + lax.dot_general(
                local.astype(BF16),
                stacked_block(x_ref, following, begin, width),
                NT,
                preferred_element_type=F32,
            )
    return product


def scores(x_ref, weights, half):
    rows, features = x_ref.shape
    length = features // 2 // SEGMENTS
    base = half * (features // 2)
    weights = weights.astype(BF16)
    total = jnp.zeros((SEGMENTS, rows), F32)
    row = lax.broadcasted_iota(jnp.int32, (SEGMENTS, rows), 0)
    for g in range(SEGMENTS):
        part = lax.dot_general(
            weights,
            x_ref[:, pl.ds(pl.multiple_of(base + g * length, LANES), length)],
            NT,
            preferred_element_type=F32,
        )
        total = total + jnp.where(row == g, part, 0.0)
    return jnp.sum(total, axis=0, keepdims=True)


def core_index():
    return lax.rem(lax.axis_index("blk"), 2)


def split_halves(sum_ref, keep_ref, send_ref, scale):
    low = scale * sum_ref[0:SEGMENTS]
    high = scale * sum_ref[SEGMENTS : 2 * SEGMENTS]
    first = core_index() == 0
    keep_ref[...] = jnp.where(first, low, high)
    send_ref[...] = jnp.where(first, high, low)


def first_kernel(samples, sigma, reg_ref, order_hbm, label_hbm, data_hbm,
                 keep_ref, send_ref, state_ref, x_ref,
                 order_ref, label_ref, local_ref, sum_ref, arrived, small):
    rows, features = x_ref.shape
    blocks = order_ref.shape[1]
    size = rows // blocks
    fetch = pltpu.make_async_copy(order_hbm, order_ref, small.at[0])
    fetch.start()
    labels = pltpu.make_async_copy(label_hbm, label_ref, small.at[1])
    labels.start()
    fetch.wait()
    order = [order_ref[0, position] for position in range(blocks)]

    def load(position):
        place = pl.ds(pl.multiple_of(order[position] * size, size), size)
        return pltpu.make_async_copy(data_hbm.at[place], x_ref.at[place], arrived.at[position])

    for position in range(blocks):
        load(position).start()
    index = jnp.full((size, LANES), reg_ref[0], jnp.int32).astype(F32)
    strength = 0.04 * jnp.exp(0.5 * math.log(2.0) * index)
    total = strength * samples
    scale = 1.0 / math.sqrt(features)
    state_ref[STRENGTH] = strength
    state_ref[TOTAL] = total
    labels.wait()
    label_row = label_ref[...].astype(F32)
    spot = lax.broadcasted_iota(jnp.int32, (size, rows), 0)
    lane = lax.broadcasted_iota(jnp.int32, (size, rows), 1)
    for block in range(blocks):
        column = jnp.sum(
            jnp.where(lane == spot + block * size, label_row, 0.0), axis=1, keepdims=True
        )
        state_ref[SIGNS + block] = jnp.broadcast_to(column, (size, LANES))
    local_ref[...] = jnp.zeros_like(local_ref)
    score = jnp.zeros((size, LANES), F32)
    product = None
    for position in range(blocks):
        block = order[position]
        if position == 0:
            load(0).wait()
        place = pl.ds(pl.multiple_of(block * size, size), size)
        square = jnp.zeros((size, LANES), F32)
        for begin in range(0, features, LANES * 8):
            values = x_ref[place, begin : begin + LANES * 8].astype(F32)
            values = values * values
            for k in range(8):
                square = square + values[:, k * LANES : (k + 1) * LANES]
        squared = jnp.sum(square, axis=1, keepdims=True) / features + 1e-06
        squared = jnp.broadcast_to(squared, (size, LANES))
        state_ref[SQUARED + block] = squared
        if position > 0:
            score = jnp.broadcast_to(scale * block_scores(product, size), (size, LANES))
        signs = state_ref[SIGNS + block]
        step = block_step(signs, jnp.zeros_like(signs), squared, score, total, sigma)
        state_ref[DUAL + block] = step
        if position < blocks - 1:
            load(position + 1).wait()
        following = order[position + 1] if position < blocks - 1 else None
        product = advance(
            x_ref, local_ref, sum_ref, block, following, signs * step,
            (sigma * scale / total)[0:1, 0:1], position == 0,
        )
    split_halves(sum_ref, keep_ref, send_ref, (scale / total)[0:1, 0:1])


def score_norm_kernel(own_ref, x_ref, part_ref, norm_ref):
    own = own_ref[...]
    part_ref[...] = scores(x_ref, own, core_index())
    norm = jnp.sum(jnp.sum(own * own, axis=0, keepdims=True), axis=1, keepdims=True)
    norm_ref[...] = jnp.broadcast_to(norm, norm_ref.shape)


def next_kernel(samples, sigma, order_ref, own_ref, other_ref, state_ref, x_ref,
                keep_ref, send_ref, new_ref, local_ref, sum_ref):
    rows, features = x_ref.shape
    blocks = order_ref.shape[1]
    size = rows // blocks
    scale = 1.0 / math.sqrt(features)
    order = [order_ref[0, position] for position in range(blocks)]
    total = state_ref[TOTAL]
    new_ref[...] = state_ref[...]
    first = core_index() == 0
    local_ref[0:SEGMENTS] = jnp.where(first, own_ref[...], other_ref[...])
    local_ref[SEGMENTS : 2 * SEGMENTS] = jnp.where(first, other_ref[...], own_ref[...])
    length = local_ref.shape[1]
    width = min(length, WIDTH)
    product = jnp.zeros((2 * SEGMENTS, LANES), F32)
    for begin in range(0, length, width):
        product = product + lax.dot_general(
            local_ref[:, begin : begin + width].astype(BF16),
            stacked_block(x_ref, order[0], begin, width),
            NT,
            preferred_element_type=F32,
        )
    for position in range(blocks):
        block = order[position]
        score = jnp.broadcast_to(scale * block_scores(product, size), (size, LANES))
        signs = state_ref[SIGNS + block]
        dual = state_ref[DUAL + block]
        step = block_step(signs, dual, state_ref[SQUARED + block], score, total, sigma)
        new_ref[DUAL + block] = dual + step
        following = order[position + 1] if position < blocks - 1 else None
        product = advance(
            x_ref, local_ref, sum_ref, block, following, signs * step,
            (sigma * scale / total)[0:1, 0:1], position == 0,
        )
    split_halves(sum_ref, keep_ref, send_ref, (scale / total)[0:1, 0:1])


def rows_of(state_ref, start, blocks, size):
    rows = blocks * size
    lane = lax.broadcasted_iota(jnp.int32, (size, rows), 1)
    spot = lax.broadcasted_iota(jnp.int32, (size, rows), 0)
    line = jnp.zeros((1, rows), F32)
    for block in range(blocks):
        line = line + jnp.sum(
            jnp.where(lane == spot + block * size, state_ref[start + block][:, 0:rows], 0.0),
            axis=0, keepdims=True,
        )
    return line


def last_kernel(samples, chips, blocks, part_ref, norm_ref, other_ref, state_ref, x_ref,
                dual_ref, margin_ref, share_ref):
    rows, features = x_ref.shape
    size = rows // blocks
    signs = rows_of(state_ref, SIGNS, blocks, size)
    dual = rows_of(state_ref, DUAL, blocks, size)
    margins = part_ref[...] + scores(x_ref, other_ref[...], 1 - core_index())
    margins = 1.0 / math.sqrt(features) * margins
    hinge = jnp.maximum(0.0, 1.0 - signs * margins)
    share = jnp.sum(hinge - dual, axis=1, keepdims=True) / samples
    norm = state_ref[STRENGTH][0:1, 0:1] * norm_ref[:, 0:1] / chips
    share_ref[...] = jnp.broadcast_to(norm + share, share_ref.shape)
    dual_ref[...] = dual
    margin_ref[...] = margins


def swap(value, peers, mask):
    return lax.ppermute(value, "blk", [(i, i ^ mask) for i in range(peers)])


def reduce_half(keep, arrived, peers):
    own = keep + arrived
    mask = 1
    while mask < peers // 2:
        own = own + swap(own, peers, 2 * mask)
        mask = 2 * mask + 1
    return own


def sum_over_chips(value, peers):
    terms = [value] + [swap(value, peers, 2 * mask) for mask in range(1, peers // 2)]
    while len(terms) > 1:
        terms = [terms[k] + terms[k + 1] for k in range(0, len(terms), 2)]
    return terms[0]


def call(body, outs, spaces, scratch=(), work=0):
    return pl.pallas_call(
        body,
        out_shape=[jax.ShapeDtypeStruct(shape, dtype) for shape, dtype in outs],
        in_specs=[pl.BlockSpec(memory_space=space) for space in spaces],
        out_specs=[pl.BlockSpec(memory_space=pltpu.VMEM) for _ in outs],
        scratch_shapes=list(scratch),
        compiler_params=pltpu.CompilerParams(vmem_limit_bytes=VMEM_LIMIT),
        cost_estimate=pl.CostEstimate(flops=work, bytes_accessed=work // 64, transcendentals=0),
    )


def shards(data, labels, order, reg_index):
    peers = lax.axis_size("blk")
    rows, features = data.shape
    blocks = order.shape[1]
    samples = rows * peers
    work = 32 * rows * features
    length = features // 2 // SEGMENTS
    half = ((SEGMENTS, length), F32)
    line = ((1, rows), F32)
    scalar = ((1, LANES), F32)
    state_shape = ((PLACES, rows // blocks, LANES), F32)
    whole = pltpu.VMEM((2 * SEGMENTS, length), F32)
    S, V, H = pltpu.SMEM, pltpu.VMEM, pltpu.HBM
    pinned = [
        pltpu.with_memory_space_constraint(a, H) for a in (order, labels.reshape(1, rows), data)
    ]
    keep, send, state, x = call(
        functools.partial(first_kernel, samples, float(peers)),
        [half, half, state_shape, ((rows, features), BF16)],
        [S, H, H, H],
        [
            pltpu.SMEM(order.shape, jnp.int32),
            pltpu.VMEM((1, rows), jnp.int32),
            whole,
            whole,
            pltpu.SemaphoreType.DMA((blocks,)),
            pltpu.SemaphoreType.DMA((2,)),
        ],
        work,
    )(reg_index, *pinned)
    own = None
    for index in range(ROUNDS):
        more = reduce_half(keep, swap(send, peers, 1), peers)
        own = more if own is None else own + more
        other = swap(own, peers, 1)
        if index < ROUNDS - 1:
            keep, send, state = call(
                functools.partial(next_kernel, samples, float(peers)),
                [half, half, state_shape],
                [S, V, V, V, V],
                [whole, whole],
                work,
            )(order, own, other, state, x)
    part, norm = call(score_norm_kernel, [line, scalar], [V, V], work=work)(own, x)
    dual, margins, share = call(
        functools.partial(last_kernel, samples, peers // 2, blocks), [line, line, scalar], [V] * 5, work=work
    )(part, norm, other, state, x)
    mask = 1
    while mask < peers:
        share = share + swap(share, peers, mask)
        mask *= 2
    gap = share[0:1, 0:1]
    return dual.reshape(rows), margins.reshape(rows), gap.reshape(1)


def solution(mesh):
    placed = (P("blk", None), P("blk"), P("blk", None), P("grp"))
    return jax.shard_map(
        shards,
        mesh=mesh,
        in_specs=placed,
        out_specs=(P(("grp", "blk")), P(("grp", "blk")), P("grp")),
        check_vma=False,
    )
```

time: 193 us -> 56.2 us (0.29)
  waiting for transfers between devices: 112 us -> 22.9 us
  matrix products: 30.8 us -> 0 us
  between operations: 20.5 us -> 1.34 us
  starting transfers between devices: 0.08 us -> 19.1 us
  blocking collectives: 14.3 us -> 0 us
  Pallas kernels: 0 us -> 12.1 us
  other arithmetic: 11.1 us -> 0.64 us
  local copies, waits for them, and re-layouts: 3.5 us -> 0.01 us
    psum x2 -> x0, waiting for transfers between devices: 112 us -> none  [shards(): weights = weights + lax.psum(delta, 'blk')]
    dot_general x17 -> x0, matrix products: 30.8 us -> none  [the longest x8 13.1 us: local_round(): jnp.dot(block_data, rounded, preferred_element_type=jnp.float32)]
    ppermute x0 -> x11, waiting for transfers between devices: none -> 22.9 us  [swap(): return lax.ppermute(value, 'blk', [(i, i ^ mask) for i in range(peers)])]
    ppermute x0 -> x11, starting transfers between devices: none -> 19.1 us  [swap(): return lax.ppermute(value, 'blk', [(i, i ^ mask) for i in range(peers)])]
    psum x1 -> x0, blocking collectives: 14.3 us -> none  [shards(): hinge_total, dual_total = lax.psum((jnp.sum(hinge), jnp.sum(dual)), 'blk')]
    pallas_call x0 -> x4, Pallas kernels: none -> 12.1 us  [the longest x1 5.72 us: shards(): call(functools.partial(first_kernel, samples, float(peers)), [half, half,...]
    dot_general x1 -> x0, other arithmetic: 3.1 us -> none  [shards(): jnp.einsum('rf,rf->r', data, data, preferred_element_type=jnp.float32)]
    convert_element_type x8 -> x0, other arithmetic: 3.04 us -> none  [the longest x7 2.38 us: local_round(): rounded = local_weights.astype(jnp.bfloat16)]
  transfers between devices with their start and end apart: 2 -> 11, of which waited for: 2 -> 11; matrix products, arithmetic and copies ran while one was open for 1% -> 0% of each run, Pallas kernels for 0% -> 1%
where the time goes in v4:
time: 56.2 us; the launch traced here: 56.1 us
  waiting for transfers between devices  22.9 us (41%)
  starting transfers between devices  19.1 us (34%)
  Pallas kernels  12.1 us (22%)
  between operations  1.34 us (2%)
  other arithmetic  0.64 us (1%)
    ppermute x11, waiting for transfers between devices, swap(): return lax.ppermute(value, 'blk', [(i, i ^ mask) for i in range(peers)])  22.9 us
    ppermute x11, starting transfers between devices, swap(): return lax.ppermute(value, 'blk', [(i, i ^ mask) for i in range(peers)])  19.1 us
    pallas_call x1, Pallas kernels, shards(): call(functools.partial(first_kernel, samples, float(peers)), [half, half,...  5.72 us
    pallas_call x1, Pallas kernels, shards(): call(functools.partial(next_kernel, samples, float(peers)), [half, half,...  4.54 us
    pallas_call x1, Pallas kernels, shards(): call(functools.partial(last_kernel, samples, peers // 2, blocks), [line,...  1.19 us
  transfers between devices with their start and end apart: 11, of which 11 were waited for; matrix products, arithmetic and copies ran while one was open for 0% of the time, Pallas kernels for 1%

profile of v4, /device:TPU:0, one launch (start us, length us, event | category | flops | bytes accessed | tf_op | source)
XLA Modules:
  0.0 56.1 jit_solution(16528418462814603655)
XLA Ops:
  0.6 0.0 copy-start
  1.3 5.7 %shard_map.67 = (f32[8,4096]{1,0:T(8,128)S(1)}, f32[8,4096]{1,0:T(8,128)S(1)}, f32[14,8,128]{2,1,0:T(8,128)S(1)}, bf16[32,65536]{1,0:T(8,128)(2,1)S(1)}) custom-call(s32[1]{0:T(128)S(6)} %copy.7.reg_ref, s32[1,4]{1,0:T(1,128)} %order_ref.1, s32[1,32]{1,0:T(1,128)} %bitcast.5, bf16[32,65536]{1,0:T(8,128)(2,1)} %data_hbm.1), custom_call_target="tpu_custom_call" | custom-call | flops 67108864 | bytes 1048576 | tf_op jit(solution)/shard_map/pallas_call | solution.py:309
  7.0 0.6 collective-permute-start
  7.6 1.0 %collective-permute-done = f32[8,4096]{1,0:T(8,128)S(1)} collective-permute-done((f32[8,4096]{1,0:T(8,128)S(1)}, f32[8,4096]{1,0:T(8,128)S(1)}, u32[]{:S(2)}, u32[]{:S(2)}) %collective-permute-start) | collective-permute-done | bytes 131104 | tf_op jit(solution)/shard_map/ppermute | solution.py:262
  8.6 3.0 %collective-permute-start.1 = (f32[8,4096]{1,0:T(8,128)S(1)}, f32[8,4096]{1,0:T(8,128)S(1)}, u32[]{:S(2)}, u32[]{:S(2)}) collective-permute-start(f32[8,4096]{1,0:T(8,128)S(1)} %add.30), channel_id=1, source_target_pairs={{0,2},{1,3},{2,0},{3,1},{4,6},{5,7},{6,4},{7,5},{8,10},{9,11},{10,... | collective-permute-start | bytes 393224 | tf_op jit(solution)/shard_map/ppermute | solution.py:262
  11.6 3.8 %collective-permute-done.1 = f32[8,4096]{1,0:T(8,128)S(1)} collective-permute-done((f32[8,4096]{1,0:T(8,128)S(1)}, f32[8,4096]{1,0:T(8,128)S(1)}, u32[]{:S(2)}, u32[]{:S(2)}) %collective-permute-start.1) | collective-permute-done | bytes 131104 | tf_op jit(solution)/shard_map/ppermute | solution.py:262
  15.4 3.8 %collective-permute-start.2 = (f32[8,4096]{1,0:T(8,128)S(1)}, f32[8,4096]{1,0:T(8,128)S(1)}, u32[]{:S(2)}, u32[]{:S(2)}) collective-permute-start(f32[8,4096]{1,0:T(8,128)S(1)} %add.31), channel_id=1, source_target_pairs={{0,6},{1,7},{2,4},{3,5},{4,2},{5,3},{6,0},{7,1},{8,14},{9,15},{10,... | collective-permute-start | bytes 393224 | tf_op jit(solution)/shard_map/ppermute | solution.py:262
  19.2 3.1 %collective-permute-done.2 = f32[8,4096]{1,0:T(8,128)S(1)} collective-permute-done((f32[8,4096]{1,0:T(8,128)S(1)}, f32[8,4096]{1,0:T(8,128)S(1)}, u32[]{:S(2)}, u32[]{:S(2)}) %collective-permute-start.2) | collective-permute-done | bytes 131104 | tf_op jit(solution)/shard_map/ppermute | solution.py:262
  22.4 0.1 collective-permute-start.3
  22.5 1.3 %collective-permute-done.3.other_ref = f32[8,4096]{1,0:T(8,128)S(1)} collective-permute-done((f32[8,4096]{1,0:T(8,128)S(1)}, f32[8,4096]{1,0:T(8,128)S(1)}, u32[]{:S(2)}, u32[]{:S(2)}) %collective-permute-start.3) | collective-permute-done | bytes 131104 | tf_op jit(solution)/shard_map/ppermute | solution.py:262
  23.8 0.0 copy-done
  23.8 4.5 %shard_map.68 = (f32[8,4096]{1,0:T(8,128)S(1)}, f32[8,4096]{1,0:T(8,128)S(1)}, f32[14,8,128]{2,1,0:T(8,128)S(1)}) custom-call(s32[1,4]{1,0:T(1,128)S(1)} %copy-done, f32[8,4096]{1,0:T(8,128)S(1)} %add.32.own_ref, f32[8,4096]{1,0:T(8,128)S(1)} %collective-permute-done.3.other_ref, f32[14,8,128]{2,1,0:T(8,128)S(1)} %get-tuple-element.17.state_ref, ...), custom_call_target="tpu_custom_call" | custom-call | flops 67108864 | bytes 1048576 | tf_op jit(solution)/shard_map/pallas_call | solution.py:329
  28.3 0.2 collective-permute-start.4
  28.5 1.2 %collective-permute-done.4 = f32[8,4096]{1,0:T(8,128)S(1)} collective-permute-done((f32[8,4096]{1,0:T(8,128)S(1)}, f32[8,4096]{1,0:T(8,128)S(1)}, u32[]{:S(2)}, u32[]{:S(2)}) %collective-permute-start.4) | collective-permute-done | bytes 131104 | tf_op jit(solution)/shard_map/ppermute | solution.py:262
  29.8 2.4 %collective-permute-start.5 = (f32[8,4096]{1,0:T(8,128)S(1)}, f32[8,4096]{1,0:T(8,128)S(1)}, u32[]{:S(2)}, u32[]{:S(2)}) collective-permute-start(f32[8,4096]{1,0:T(8,128)S(1)} %add.33), channel_id=1, source_target_pairs={{0,2},{1,3},{2,0},{3,1},{4,6},{5,7},{6,4},{7,5},{8,10},{9,11},{10,... | collective-permute-start | bytes 393224 | tf_op jit(solution)/shard_map/ppermute | solution.py:262
  32.2 3.8 %collective-permute-done.5 = f32[8,4096]{1,0:T(8,128)S(1)} collective-permute-done((f32[8,4096]{1,0:T(8,128)S(1)}, f32[8,4096]{1,0:T(8,128)S(1)}, u32[]{:S(2)}, u32[]{:S(2)}) %collective-permute-start.5) | collective-permute-done | bytes 131104 | tf_op jit(solution)/shard_map/ppermute | solution.py:262
  36.0 3.1 %collective-permute-start.6 = (f32[8,4096]{1,0:T(8,128)S(1)}, f32[8,4096]{1,0:T(8,128)S(1)}, u32[]{:S(2)}, u32[]{:S(2)}) collective-permute-start(f32[8,4096]{1,0:T(8,128)S(1)} %add.34), channel_id=1, source_target_pairs={{0,6},{1,7},{2,4},{3,5},{4,2},{5,3},{6,0},{7,1},{8,14},{9,15},{10,... | collective-permute-start | bytes 393224 | tf_op jit(solution)/shard_map/ppermute | solution.py:262
  39.1 3.8 %collective-permute-done.6 = f32[8,4096]{1,0:T(8,128)S(1)} collective-permute-done((f32[8,4096]{1,0:T(8,128)S(1)}, f32[8,4096]{1,0:T(8,128)S(1)}, u32[]{:S(2)}, u32[]{:S(2)}) %collective-permute-start.6) | collective-permute-done | bytes 131104 | tf_op jit(solution)/shard_map/ppermute | solution.py:262
  43.0 0.1 collective-permute-start.7
  43.1 0.7 %shard_map.69 = (f32[1,32]{1,0:T(1,128)S(1)}, f32[1,128]{1,0:T(1,128)S(1)}) custom-call(f32[8,4096]{1,0:T(8,128)S(1)} %add_add_fusion.own_ref, bf16[32,65536]{1,0:T(8,128)(2,1)S(1)} %get-tuple-element.18.x_ref), custom_call_target="tpu_custom_call" | custom-call | flops 67108864 | bytes 1048576 | tf_op jit(solution)/shard_map/pallas_call | solution.py:336
  43.8 0.7 %collective-permute-done.7.other_ref = f32[8,4096]{1,0:T(8,128)S(1)} collective-permute-done((f32[8,4096]{1,0:T(8,128)S(1)}, f32[8,4096]{1,0:T(8,128)S(1)}, u32[]{:S(2)}, u32[]{:S(2)}) %collective-permute-start.7) | collective-permute-done | bytes 131104 | tf_op jit(solution)/shard_map/ppermute | solution.py:262
  44.4 1.2 %shard_map.70 = (f32[1,32]{1,0:T(1,128)}, f32[1,32]{1,0:T(1,128)}, f32[1,128]{1,0:T(1,128)S(1)}) custom-call(f32[1,32]{1,0:T(1,128)S(1)} %get-tuple-element.21.part_ref, f32[1,128]{1,0:T(1,128)S(1)} %get-tuple-element.22.norm_ref, f32[8,4096]{1,0:T(8,128)S(1)} %collective-permute-done.7.other_ref, f32[14,8,128]{2,1,0:T(8,128)S(1)} %get-tuple-element.23.state_ref, ...), custom_call_target="tpu_custom_call" | custom-call | flops 67108864 | bytes 1048576 | tf_op jit(solution)/shard_map/pallas_call | solution.py:337
  45.6 0.1 collective-permute-start.8
  45.8 1.0 %collective-permute-done.8 = f32[1,128]{1,0:T(1,128)S(1)} collective-permute-done((f32[1,128]{1,0:T(1,128)S(1)}, f32[1,128]{1,0:T(1,128)S(1)}, u32[]{:S(2)}, u32[]{:S(2)}) %collective-permute-start.8) | collective-permute-done | bytes 544 | tf_op jit(solution)/shard_map/ppermute | solution.py:262
  46.8 2.5 %collective-permute-start.9 = (f32[1,128]{1,0:T(1,128)S(1)}, f32[1,128]{1,0:T(1,128)S(1)}, u32[]{:S(2)}, u32[]{:S(2)}) collective-permute-start(f32[1,128]{1,0:T(1,128)S(1)} %add.37), channel_id=1, source_target_pairs={{0,2},{1,3},{2,0},{3,1},{4,6},{5,7},{6,4},{7,5},{8,10},{9,11},{10,... | collective-permute-start | bytes 1544 | tf_op jit(solution)/shard_map/ppermute | solution.py:262
  49.2 1.5 %collective-permute-done.9 = f32[1,128]{1,0:T(1,128)S(1)} collective-permute-done((f32[1,128]{1,0:T(1,128)S(1)}, f32[1,128]{1,0:T(1,128)S(1)}, u32[]{:S(2)}, u32[]{:S(2)}) %collective-permute-start.9) | collective-permute-done | bytes 544 | tf_op jit(solution)/shard_map/ppermute | solution.py:262
  50.8 3.2 %collective-permute-start.10 = (f32[1,128]{1,0:T(1,128)S(1)}, f32[1,128]{1,0:T(1,128)S(1)}, u32[]{:S(2)}, u32[]{:S(2)}) collective-permute-start(f32[1,128]{1,0:T(1,128)S(1)} %add.38), channel_id=1, source_target_pairs={{0,4},{1,5},{2,6},{3,7},{4,0},{5,1},{6,2},{7,3},{8,12},{9,13},{10,... | collective-permute-start | bytes 1544 | tf_op jit(solution)/shard_map/ppermute | solution.py:262
  54.0 1.5 %collective-permute-done.10 = f32[1,128]{1,0:T(1,128)S(1)} collective-permute-done((f32[1,128]{1,0:T(1,128)S(1)}, f32[1,128]{1,0:T(1,128)S(1)}, u32[]{:S(2)}, u32[]{:S(2)}) %collective-permute-start.10) | collective-permute-done | bytes 544 | tf_op jit(solution)/shard_map/ppermute | solution.py:262
  55.5 0.5 add.39
  (8 shorter events, 0.1 us)
Async XLA Ops:
  0.6 23.2 %copy-start = (s32[1,4]{1,0:T(1,128)S(1)}, s32[1,4]{1,0:T(1,128)}, u32[]{:S(2)}) copy-start(s32[1,4]{1,0:T(1,128)} %order_ref.1) | copy-start | bytes 52
  7.0 1.5 %collective-permute-start = (f32[8,4096]{1,0:T(8,128)S(1)}, f32[8,4096]{1,0:T(8,128)S(1)}, u32[]{:S(2)}, u32[]{:S(2)}) collective-permute-start(f32[8,4096]{1,0:T(8,128)S(1)} %get-tuple-element.16), channel_id=1, source_target_pairs={{0,1},{1,0},{2,3},{3,2},{4,5},{5,4},{6,7},{7,6},{8,9},{9,8},{10,11... | collective-permute-start | bytes 393224 | tf_op jit(solution)/shard_map/ppermute | solution.py:262
  8.6 6.8 %collective-permute-start.1 = (f32[8,4096]{1,0:T(8,128)S(1)}, f32[8,4096]{1,0:T(8,128)S(1)}, u32[]{:S(2)}, u32[]{:S(2)}) collective-permute-start(f32[8,4096]{1,0:T(8,128)S(1)} %add.30), channel_id=1, source_target_pairs={{0,2},{1,3},{2,0},{3,1},{4,6},{5,7},{6,4},{7,5},{8,10},{9,11},{10,... | collective-permute-start | bytes 393224 | tf_op jit(solution)/shard_map/ppermute | solution.py:262
  15.4 6.9 %collective-permute-start.2 = (f32[8,4096]{1,0:T(8,128)S(1)}, f32[8,4096]{1,0:T(8,128)S(1)}, u32[]{:S(2)}, u32[]{:S(2)}) collective-permute-start(f32[8,4096]{1,0:T(8,128)S(1)} %add.31), channel_id=1, source_target_pairs={{0,6},{1,7},{2,4},{3,5},{4,2},{5,3},{6,0},{7,1},{8,14},{9,15},{10,... | collective-permute-start | bytes 393224 | tf_op jit(solution)/shard_map/ppermute | solution.py:262
  22.4 1.4 %collective-permute-start.3 = (f32[8,4096]{1,0:T(8,128)S(1)}, f32[8,4096]{1,0:T(8,128)S(1)}, u32[]{:S(2)}, u32[]{:S(2)}) collective-permute-start(f32[8,4096]{1,0:T(8,128)S(1)} %add.32.own_ref), channel_id=1, source_target_pairs={{0,1},{1,0},{2,3},{3,2},{4,5},{5,4},{6,7},{7,6},{8,9},{9,8},{10,11... | collective-permute-start | bytes 393224 | tf_op jit(solution)/shard_map/ppermute | solution.py:262
  28.3 1.4 %collective-permute-start.4 = (f32[8,4096]{1,0:T(8,128)S(1)}, f32[8,4096]{1,0:T(8,128)S(1)}, u32[]{:S(2)}, u32[]{:S(2)}) collective-permute-start(f32[8,4096]{1,0:T(8,128)S(1)} %get-tuple-element.20), channel_id=1, source_target_pairs={{0,1},{1,0},{2,3},{3,2},{4,5},{5,4},{6,7},{7,6},{8,9},{9,8},{10,11... | collective-permute-start | bytes 393224 | tf_op jit(solution)/shard_map/ppermute | solution.py:262
  29.8 6.2 %collective-permute-start.5 = (f32[8,4096]{1,0:T(8,128)S(1)}, f32[8,4096]{1,0:T(8,128)S(1)}, u32[]{:S(2)}, u32[]{:S(2)}) collective-permute-start(f32[8,4096]{1,0:T(8,128)S(1)} %add.33), channel_id=1, source_target_pairs={{0,2},{1,3},{2,0},{3,1},{4,6},{5,7},{6,4},{7,5},{8,10},{9,11},{10,... | collective-permute-start | bytes 393224 | tf_op jit(solution)/shard_map/ppermute | solution.py:262
  36.0 6.9 %collective-permute-start.6 = (f32[8,4096]{1,0:T(8,128)S(1)}, f32[8,4096]{1,0:T(8,128)S(1)}, u32[]{:S(2)}, u32[]{:S(2)}) collective-permute-start(f32[8,4096]{1,0:T(8,128)S(1)} %add.34), channel_id=1, source_target_pairs={{0,6},{1,7},{2,4},{3,5},{4,2},{5,3},{6,0},{7,1},{8,14},{9,15},{10,... | collective-permute-start | bytes 393224 | tf_op jit(solution)/shard_map/ppermute | solution.py:262
  43.0 1.4 %collective-permute-start.7 = (f32[8,4096]{1,0:T(8,128)S(1)}, f32[8,4096]{1,0:T(8,128)S(1)}, u32[]{:S(2)}, u32[]{:S(2)}) collective-permute-start(f32[8,4096]{1,0:T(8,128)S(1)} %add_add_fusion.own_ref), channel_id=1, source_target_pairs={{0,1},{1,0},{2,3},{3,2},{4,5},{5,4},{6,7},{7,6},{8,9},{9,8},{10,11... | collective-permute-start | bytes 393224 | tf_op jit(solution)/shard_map/ppermute | solution.py:262
  45.6 1.2 %collective-permute-start.8 = (f32[1,128]{1,0:T(1,128)S(1)}, f32[1,128]{1,0:T(1,128)S(1)}, u32[]{:S(2)}, u32[]{:S(2)}) collective-permute-start(f32[1,128]{1,0:T(1,128)S(1)} %get-tuple-element.26), channel_id=1, source_target_pairs={{0,1},{1,0},{2,3},{3,2},{4,5},{5,4},{6,7},{7,6},{8,9},{9,8},{10,11... | collective-permute-start | bytes 1544 | tf_op jit(solution)/shard_map/ppermute | solution.py:262
  46.8 4.0 %collective-permute-start.9 = (f32[1,128]{1,0:T(1,128)S(1)}, f32[1,128]{1,0:T(1,128)S(1)}, u32[]{:S(2)}, u32[]{:S(2)}) collective-permute-start(f32[1,128]{1,0:T(1,128)S(1)} %add.37), channel_id=1, source_target_pairs={{0,2},{1,3},{2,0},{3,1},{4,6},{5,7},{6,4},{7,5},{8,10},{9,11},{10,... | collective-permute-start | bytes 1544 | tf_op jit(solution)/shard_map/ppermute | solution.py:262
  50.8 4.7 %collective-permute-start.10 = (f32[1,128]{1,0:T(1,128)S(1)}, f32[1,128]{1,0:T(1,128)S(1)}, u32[]{:S(2)}, u32[]{:S(2)}) collective-permute-start(f32[1,128]{1,0:T(1,128)S(1)} %add.38), channel_id=1, source_target_pairs={{0,4},{1,5},{2,6},{3,7},{4,0},{5,1},{6,2},{7,3},{8,12},{9,13},{10,... | collective-permute-start | bytes 1544 | tf_op jit(solution)/shard_map/ppermute | solution.py:262

commit v5 on v4

v5 whole, which is shorter than its diff:
```python
import functools
import math

import jax
import jax.numpy as jnp
from jax import lax
from jax.experimental import pallas as pl
from jax.experimental.pallas import tpu as pltpu
from jax.sharding import PartitionSpec as P

ROUNDS = 2
BLOCKS = 4
LANES = 128
GROUP = 32
VMEM_LIMIT = 12 * 1024 * 1024

F32 = jnp.float32
BF16 = jnp.bfloat16
NT = (((1,), (1,)), ((), ()))
NN = (((1,), (0,)), ((), ()))

STRENGTH, TOTAL, SIGNS = 0, 1, 2
SQUARED, DUAL = SIGNS + BLOCKS, SIGNS + 2 * BLOCKS
PLACE, PIECES = SIGNS + 3 * BLOCKS, SIGNS + 4 * BLOCKS


def iota(shape, axis):
    return lax.broadcasted_iota(jnp.int32, shape, axis)


def block_left(coefficient):
    size = coefficient.shape[0]
    line = jnp.sum(
        jnp.where(iota((size, LANES), 1) % size == iota((size, LANES), 0), coefficient, 0.0),
        axis=0, keepdims=True,
    )
    shape = (GROUP, GROUP * size)
    wide = jnp.concatenate([line] * (GROUP * size // LANES), axis=1)
    return jnp.where(iota(shape, 1) // size == iota(shape, 0), wide, 0.0).astype(BF16)


def products(x_ref, block, weights, first, size):
    groups = weights.shape[0] // GROUP
    left = jnp.concatenate(
        [weights[g * GROUP : (g + 1) * GROUP] for g in range(groups)], axis=1
    ).astype(BF16)
    begin = first * size
    right = jnp.concatenate(
        [
            x_ref[block, pl.ds(begin + g * GROUP * size, GROUP * size), :]
            for g in range(groups)
        ],
        axis=1,
    )
    return lax.dot_general(left, right, NT, preferred_element_type=F32)


def same_tile(product, size):
    shape = product.shape
    line = jnp.sum(
        jnp.where(iota(shape, 1) // size == iota(shape, 0), product, 0.0), axis=0, keepdims=True
    )
    total = line[:, 0:LANES]
    for begin in range(LANES, shape[1], LANES):
        total = total + line[:, begin : begin + LANES]
    return total


def per_sample(line, size):
    column = jnp.sum(
        jnp.where(iota((size, LANES), 1) % size == iota((size, LANES), 0), line, 0.0),
        axis=1, keepdims=True,
    )
    return jnp.broadcast_to(column, (size, LANES))


def block_step(signs, dual, squared, score, total, sigma):
    updated = jnp.clip(dual + total * (1.0 - signs * score) / (sigma * squared), 0.0, 1.0)
    return updated - dual


def add_products(totals, x_ref, position, weights, round_ref, begin):
    size = totals[0].shape[0]
    rows = slice(begin, begin + GROUP)
    round_ref[rows] = weights.astype(BF16).astype(F32)
    values = x_ref[position, begin * size : (begin + GROUP) * size, :].astype(F32)
    totals = list(totals)
    for tile in range(GROUP):
        term = values[tile * size : (tile + 1) * size] * round_ref[begin + tile : begin + tile + 1]
        totals[tile % len(totals)] = totals[tile % len(totals)] + term
    return totals


def total_score(totals, scale):
    while len(totals) > 1:
        totals = [totals[k] + totals[k + 1] for k in range(0, len(totals), 2)]
    return jnp.broadcast_to(scale * jnp.sum(totals[0], axis=1, keepdims=True), totals[0].shape)


def no_totals(size):
    return [jnp.zeros((size, LANES), F32) for _ in range(4)]


def advance(x_ref, local_ref, sum_ref, round_ref, position, coefficient, rate, fresh, empty, onward):
    size = coefficient.shape[0]
    left = block_left(coefficient)
    totals = no_totals(size)
    for begin in range(0, sum_ref.shape[0], GROUP):
        rows = slice(begin, begin + GROUP)
        update = lax.dot_general(
            left,
            x_ref[position, begin * size : (begin + GROUP) * size, :],
            NN,
            preferred_element_type=F32,
        )
        sum_ref[rows] = update if fresh else sum_ref[rows] + update
        if onward:
            local = rate * update if empty else local_ref[rows] + rate * update
            local_ref[rows] = local
            totals = add_products(totals, x_ref, position + 1, local, round_ref, begin)
    return totals


def core_index():
    return lax.rem(lax.axis_index("blk"), 2)


def split_halves(sum_ref, keep_ref, send_ref, scale):
    half = keep_ref.shape[0]
    low = scale * sum_ref[0:half]
    high = scale * sum_ref[half : 2 * half]
    first = core_index() == 0
    keep_ref[...] = jnp.where(first, low, high)
    send_ref[...] = jnp.where(first, high, low)


def first_kernel(samples, sigma, reg_ref, order_hbm, label_hbm, data_hbm,
                 keep_ref, send_ref, state_ref, x_ref,
                 order_ref, label_ref, local_ref, sum_ref, round_ref, arrived, small):
    blocks = order_ref.shape[1]
    size = x_ref.shape[1] // sum_ref.shape[0]
    rows, features = blocks * size, sum_ref.shape[0] * LANES
    fetch = pltpu.make_async_copy(order_hbm, order_ref, small.at[0])
    fetch.start()
    labels = pltpu.make_async_copy(label_hbm, label_ref, small.at[1])
    labels.start()
    fetch.wait()
    order = [order_ref[0, position] for position in range(blocks)]

    def load(position):
        block = order[position]
        return pltpu.make_async_copy(data_hbm.at[block], x_ref.at[position], arrived.at[position])

    for position in range(blocks):
        load(position).start()
    index = jnp.full((size, LANES), reg_ref[0], jnp.int32).astype(F32)
    strength = 0.04 * jnp.exp(0.5 * math.log(2.0) * index)
    total = strength * samples
    scale = 1.0 / math.sqrt(features)
    state_ref[STRENGTH] = strength
    state_ref[TOTAL] = total
    labels.wait()
    label_row = label_ref[...].astype(F32)
    spot = lax.broadcasted_iota(jnp.int32, (size, rows), 0)
    lane = lax.broadcasted_iota(jnp.int32, (size, rows), 1)
    for position in range(blocks):
        begin = order[position] * size
        column = jnp.sum(jnp.where(lane == spot + begin, label_row, 0.0), axis=1, keepdims=True)
        state_ref[SIGNS + position] = jnp.broadcast_to(column, (size, LANES))
        state_ref[PLACE + position] = jnp.full((size, LANES), begin, jnp.int32).astype(F32)
    score = jnp.zeros((size, LANES), F32)
    for position in range(blocks):
        if position == 0:
            load(0).wait()
        square = no_totals(size)
        for begin in range(0, size * sum_ref.shape[0], 16 * size):
            values = x_ref[position, begin : begin + 16 * size, :].astype(F32)
            values = values * values
            for k in range(16):
                square[k % 4] = square[k % 4] + values[k * size : (k + 1) * size]
        squared = total_score(square, 1.0) / features + 1e-06
        state_ref[SQUARED + position] = squared
        if position > 0:
            score = total_score(totals, scale)
        signs = state_ref[SIGNS + position]
        step = block_step(signs, jnp.zeros_like(signs), squared, score, total, sigma)
        state_ref[DUAL + position] = step
        if position < blocks - 1:
            load(position + 1).wait()
        totals = advance(
            x_ref, local_ref, sum_ref, round_ref, position, signs * step,
            (sigma * scale / total)[0:1, 0:1], position == 0, position == 0, position < blocks - 1,
        )
    split_halves(sum_ref, keep_ref, send_ref, (scale / total)[0:1, 0:1])


def half_lines(x_ref, weights, core):
    blocks = x_ref.shape[0]
    half = weights.shape[0]
    size = x_ref.shape[1] // (2 * half)
    return [
        same_tile(products(x_ref, block, weights, core * half, size), size) for block in range(blocks)
    ]


def score_norm_kernel(own_ref, x_ref, part_ref, norm_ref):
    own = own_ref[...]
    lines = half_lines(x_ref, own, core_index())
    for block in range(len(lines)):
        part_ref[block : block + 1] = lines[block]
    norm = jnp.sum(jnp.sum(own * own, axis=0, keepdims=True), axis=1, keepdims=True)
    norm_ref[...] = jnp.broadcast_to(norm, norm_ref.shape)


def next_kernel(sigma, own_ref, other_ref, state_ref, x_ref,
                keep_ref, send_ref, new_ref, local_ref, sum_ref, round_ref):
    blocks = x_ref.shape[0]
    size = x_ref.shape[1] // sum_ref.shape[0]
    half = own_ref.shape[0]
    scale = 1.0 / math.sqrt(sum_ref.shape[0] * LANES)
    total = state_ref[TOTAL]
    new_ref[...] = state_ref[...]
    first = core_index() == 0
    totals = no_totals(size)
    for begin in range(0, 2 * half, GROUP):
        rows = slice(begin % half, begin % half + GROUP)
        own, other = own_ref[rows], other_ref[rows]
        if begin < half:
            local = jnp.where(first, own, other)
        else:
            local = jnp.where(first, other, own)
        local_ref[begin : begin + GROUP] = local
        totals = add_products(totals, x_ref, 0, local, round_ref, begin)
    for position in range(blocks):
        score = total_score(totals, scale)
        signs = state_ref[SIGNS + position]
        dual = state_ref[DUAL + position]
        step = block_step(signs, dual, state_ref[SQUARED + position], score, total, sigma)
        new_ref[DUAL + position] = dual + step
        totals = advance(
            x_ref, local_ref, sum_ref, round_ref, position, signs * step,
            (sigma * scale / total)[0:1, 0:1], position == 0, False, position < blocks - 1,
        )
    split_halves(sum_ref, keep_ref, send_ref, (scale / total)[0:1, 0:1])


def in_line(pieces, places):
    size = pieces[0].shape[0]
    shape = (size, len(pieces) * size)
    target = iota(shape, 1).astype(F32)
    spot = iota(shape, 0).astype(F32)
    line = jnp.zeros((1, shape[1]), F32)
    for piece, place in zip(pieces, places):
        here = target == spot + place[:, 0 : shape[1]]
        line = line + jnp.sum(jnp.where(here, piece[:, 0 : shape[1]], 0.0), axis=0, keepdims=True)
    return line


def last_kernel(samples, chips, part_ref, norm_ref, other_ref, state_ref, x_ref,
                dual_ref, margin_ref, share_ref):
    blocks = x_ref.shape[0]
    half = other_ref.shape[0]
    size = x_ref.shape[1] // (2 * half)
    scale = 1.0 / math.sqrt(2 * half * LANES)
    lines = half_lines(x_ref, other_ref[...], 1 - core_index())
    margins, spread = [], jnp.zeros((size, LANES), F32)
    for block in range(blocks):
        margins.append(scale * per_sample(part_ref[block : block + 1] + lines[block], size))
        hinge = jnp.maximum(0.0, 1.0 - state_ref[SIGNS + block] * margins[block])
        spread = spread + (hinge - state_ref[DUAL + block])
    share = jnp.sum(spread, axis=0, keepdims=True) / samples
    norm = state_ref[STRENGTH][0:1] * norm_ref[...] / chips
    share_ref[...] = norm + share
    places = [state_ref[PLACE + block] for block in range(blocks)]
    dual_ref[...] = in_line([state_ref[DUAL + block] for block in range(blocks)], places)
    margin_ref[...] = in_line(margins, places)


def swap(value, peers, mask):
    return lax.ppermute(value, "blk", [(i, i ^ mask) for i in range(peers)])


def reduce_half(keep, arrived, peers):
    own = keep + arrived
    mask = 1
    while mask < peers // 2:
        own = own + swap(own, peers, 2 * mask)
        mask = 2 * mask + 1
    return own


def sum_over_chips(value, peers):
    terms = [value] + [swap(value, peers, 2 * mask) for mask in range(1, peers // 2)]
    while len(terms) > 1:
        terms = [terms[k] + terms[k + 1] for k in range(0, len(terms), 2)]
    return terms[0]


def call(body, outs, spaces, scratch=(), work=0):
    return pl.pallas_call(
        body,
        out_shape=[jax.ShapeDtypeStruct(shape, dtype) for shape, dtype in outs],
        in_specs=[pl.BlockSpec(memory_space=space) for space in spaces],
        out_specs=[pl.BlockSpec(memory_space=pltpu.VMEM) for _ in outs],
        scratch_shapes=list(scratch),
        compiler_params=pltpu.CompilerParams(vmem_limit_bytes=VMEM_LIMIT),
        cost_estimate=pl.CostEstimate(flops=work, bytes_accessed=work // 64, transcendentals=0),
    )


def shards(data, labels, order, reg_index):
    peers = lax.axis_size("blk")
    rows, features = data.shape
    blocks = order.shape[1]
    samples = rows * peers
    work = 32 * rows * features
    size = rows // blocks
    tiles = features // LANES
    half = ((tiles // 2, LANES), F32)
    tiled = data.reshape(blocks, size, tiles, LANES).transpose(0, 2, 1, 3)
    tiled = tiled.reshape(blocks, tiles * size, LANES)
    line = ((1, rows), F32)
    scalar = ((1, LANES), F32)
    state_shape = ((PIECES, size, LANES), F32)
    whole = pltpu.VMEM((tiles, LANES), F32)
    S, V, H = pltpu.SMEM, pltpu.VMEM, pltpu.HBM
    pinned = [
        pltpu.with_memory_space_constraint(a, H) for a in (order, labels.reshape(1, rows), tiled)
    ]
    keep, send, state, x = call(
        functools.partial(first_kernel, samples, float(peers)),
        [half, half, state_shape, (tiled.shape, BF16)],
        [S, H, H, H],
        [
            pltpu.SMEM(order.shape, jnp.int32),
            pltpu.VMEM((1, rows), jnp.int32),
            whole,
            whole,
            whole,
            pltpu.SemaphoreType.DMA((blocks,)),
            pltpu.SemaphoreType.DMA((2,)),
        ],
        work,
    )(reg_index, *pinned)
    own = None
    for index in range(ROUNDS):
        more = reduce_half(keep, swap(send, peers, 1), peers)
        own = more if own is None else own + more
        other = swap(own, peers, 1)
        if index < ROUNDS - 1:
            keep, send, state = call(
                functools.partial(next_kernel, float(peers)),
                [half, half, state_shape],
                [V] * 4,
                [whole] * 3,
                work,
            )(own, other, state, x)
    part, norm = call(score_norm_kernel, [((blocks, LANES), F32), scalar], [V, V], work=work)(own, x)
    dual, margins, share = call(
        functools.partial(last_kernel, samples, peers // 2), [line, line, scalar], [V] * 5, work=work
    )(part, norm, other, state, x)
    mask = 1
    while mask < peers:
        share = share + swap(share, peers, mask)
        mask *= 2
    gap = share[0:1, 0:1]
    return dual.reshape(rows), margins.reshape(rows), gap.reshape(1)


def solution(mesh):
    placed = (P("blk", None), P("blk"), P("blk", None), P("grp"))
    return jax.shard_map(
        shards,
        mesh=mesh,
        in_specs=placed,
        out_specs=(P(("grp", "blk")), P(("grp", "blk")), P("grp")),
        check_vma=False,
    )
```

time: 56.2 us -> 52.5 us (0.934)
  Pallas kernels: 12.1 us -> 8.44 us
    pallas_call x3, Pallas kernels: 6.41 us -> 4.19 us  [the longest x1 2.12 us: shards(): call(functools.partial(next_kernel, float(peers)), [half, half, state_sha...]
    pallas_call x1, Pallas kernels: 5.72 us -> 4.26 us  [shards(): call(functools.partial(first_kernel, samples, float(peers)), [half, half,...]
where the time goes in v5:
time: 52.5 us; the launch traced here: 52.3 us
  waiting for transfers between devices  22.8 us (43%)
  starting transfers between devices  19.1 us (36%)
  Pallas kernels  8.44 us (16%)
  between operations  1.34 us (3%)
  other arithmetic  0.63 us (1%)
    ppermute x11, waiting for transfers between devices, swap(): return lax.ppermute(value, 'blk', [(i, i ^ mask) for i in range(peers)])  22.8 us
    ppermute x11, starting transfers between devices, swap(): return lax.ppermute(value, 'blk', [(i, i ^ mask) for i in range(peers)])  19.1 us
    pallas_call x1, Pallas kernels, shards(): call(functools.partial(first_kernel, samples, float(peers)), [half, half,...  4.26 us
    pallas_call x1, Pallas kernels, shards(): call(functools.partial(next_kernel, float(peers)), [half, half, state_sha...  2.12 us
    pallas_call x1, Pallas kernels, shards(): call(functools.partial(last_kernel, samples, peers // 2), [line, line, sc...  1.33 us
  transfers between devices with their start and end apart: 11, of which 11 were waited for; matrix products, arithmetic and copies ran while one was open for 0% of the time, Pallas kernels for 1%

profile of v5, /device:TPU:0, one launch (start us, length us, event | category | flops | bytes accessed | tf_op | source)
XLA Modules:
  0.0 52.3 jit_solution(17052242705324408648)
XLA Ops:
  1.3 4.3 %shard_map.67 = (f32[256,128]{1,0:T(8,128)S(1)}, f32[256,128]{1,0:T(8,128)S(1)}, f32[18,8,128]{2,1,0:T(8,128)S(1)}, bf16[4,4096,128]{2,1,0:T(8,128)(2,1)S(1)}) custom-call(s32[1]{0:T(128)S(6)} %copy.7.reg_ref, s32[1,4]{1,0:T(1,128)} %order_hbm.1, s32[1,32]{1,0:T(1,128)} %bitcast.11, bf16[4,4096,128]{2,1,0:T(8,128)(2,1)} %bitcast.10), custom_call_target="tpu_custom_call" | custom-call | flops 67108864 | bytes 1048576 | tf_op jit(solution)/shard_map/pallas_call | solution.py:330
  5.5 0.6 %collective-permute-start = (f32[256,128]{1,0:T(8,128)S(1)}, f32[256,128]{1,0:T(8,128)S(1)}, u32[]{:S(2)}, u32[]{:S(2)}) collective-permute-start(f32[256,128]{1,0:T(8,128)S(1)} %get-tuple-element.16), channel_id=1, source_target_pairs={{0,1},{1,0},{2,3},{3,2},{4,5},{5,4},{6,7},{7,6},{8,9},{9,8},{10,11... | collective-permute-start | bytes 393224 | tf_op jit(solution)/shard_map/ppermute | solution.py:280
  6.1 1.0 %collective-permute-done = f32[256,128]{1,0:T(8,128)S(1)} collective-permute-done((f32[256,128]{1,0:T(8,128)S(1)}, f32[256,128]{1,0:T(8,128)S(1)}, u32[]{:S(2)}, u32[]{:S(2)}) %collective-permute-start) | collective-permute-done | bytes 131104 | tf_op jit(solution)/shard_map/ppermute | solution.py:280
  7.1 3.0 %collective-permute-start.1 = (f32[256,128]{1,0:T(8,128)S(1)}, f32[256,128]{1,0:T(8,128)S(1)}, u32[]{:S(2)}, u32[]{:S(2)}) collective-permute-start(f32[256,128]{1,0:T(8,128)S(1)} %add.30), channel_id=1, source_target_pairs={{0,2},{1,3},{2,0},{3,1},{4,6},{5,7},{6,4},{7,5},{8,10},{9,11},{10,... | collective-permute-start | bytes 393224 | tf_op jit(solution)/shard_map/ppermute | solution.py:280
  10.1 3.8 %collective-permute-done.1 = f32[256,128]{1,0:T(8,128)S(1)} collective-permute-done((f32[256,128]{1,0:T(8,128)S(1)}, f32[256,128]{1,0:T(8,128)S(1)}, u32[]{:S(2)}, u32[]{:S(2)}) %collective-permute-start.1) | collective-permute-done | bytes 131104 | tf_op jit(solution)/shard_map/ppermute | solution.py:280
  13.9 3.8 %collective-permute-start.2 = (f32[256,128]{1,0:T(8,128)S(1)}, f32[256,128]{1,0:T(8,128)S(1)}, u32[]{:S(2)}, u32[]{:S(2)}) collective-permute-start(f32[256,128]{1,0:T(8,128)S(1)} %add.31), channel_id=1, source_target_pairs={{0,6},{1,7},{2,4},{3,5},{4,2},{5,3},{6,0},{7,1},{8,14},{9,15},{10,... | collective-permute-start | bytes 393224 | tf_op jit(solution)/shard_map/ppermute | solution.py:280
  17.8 3.1 %collective-permute-done.2 = f32[256,128]{1,0:T(8,128)S(1)} collective-permute-done((f32[256,128]{1,0:T(8,128)S(1)}, f32[256,128]{1,0:T(8,128)S(1)}, u32[]{:S(2)}, u32[]{:S(2)}) %collective-permute-start.2) | collective-permute-done | bytes 131104 | tf_op jit(solution)/shard_map/ppermute | solution.py:280
  20.9 0.1 collective-permute-start.3
  21.0 1.3 %collective-permute-done.3.other_ref = f32[256,128]{1,0:T(8,128)S(1)} collective-permute-done((f32[256,128]{1,0:T(8,128)S(1)}, f32[256,128]{1,0:T(8,128)S(1)}, u32[]{:S(2)}, u32[]{:S(2)}) %collective-permute-start.3) | collective-permute-done | bytes 131104 | tf_op jit(solution)/shard_map/ppermute | solution.py:280
  22.3 2.1 %shard_map.68 = (f32[256,128]{1,0:T(8,128)S(1)}, f32[256,128]{1,0:T(8,128)S(1)}, f32[18,8,128]{2,1,0:T(8,128)S(1)}) custom-call(f32[256,128]{1,0:T(8,128)S(1)} %add.32.own_ref, f32[256,128]{1,0:T(8,128)S(1)} %collective-permute-done.3.other_ref, f32[18,8,128]{2,1,0:T(8,128)S(1)} %get-tuple-element.17.state_ref, bf16[4,4096,128]{2,1,0:T(8,128)(2,1)S(1)} %get-tuple-element.18.x_ref), custom_call_target="tpu_custom_call" | custom-call | flops 67108864 | bytes 1048576 | tf_op jit(solution)/shard_map/pallas_call | solution.py:351
  24.4 0.2 collective-permute-start.4
  24.6 1.2 %collective-permute-done.4 = f32[256,128]{1,0:T(8,128)S(1)} collective-permute-done((f32[256,128]{1,0:T(8,128)S(1)}, f32[256,128]{1,0:T(8,128)S(1)}, u32[]{:S(2)}, u32[]{:S(2)}) %collective-permute-start.4) | collective-permute-done | bytes 131104 | tf_op jit(solution)/shard_map/ppermute | solution.py:280
  25.9 2.4 %collective-permute-start.5 = (f32[256,128]{1,0:T(8,128)S(1)}, f32[256,128]{1,0:T(8,128)S(1)}, u32[]{:S(2)}, u32[]{:S(2)}) collective-permute-start(f32[256,128]{1,0:T(8,128)S(1)} %add.33), channel_id=1, source_target_pairs={{0,2},{1,3},{2,0},{3,1},{4,6},{5,7},{6,4},{7,5},{8,10},{9,11},{10,... | collective-permute-start | bytes 393224 | tf_op jit(solution)/shard_map/ppermute | solution.py:280
  28.3 3.8 %collective-permute-done.5 = f32[256,128]{1,0:T(8,128)S(1)} collective-permute-done((f32[256,128]{1,0:T(8,128)S(1)}, f32[256,128]{1,0:T(8,128)S(1)}, u32[]{:S(2)}, u32[]{:S(2)}) %collective-permute-start.5) | collective-permute-done | bytes 131104 | tf_op jit(solution)/shard_map/ppermute | solution.py:280
  32.1 3.1 %collective-permute-start.6 = (f32[256,128]{1,0:T(8,128)S(1)}, f32[256,128]{1,0:T(8,128)S(1)}, u32[]{:S(2)}, u32[]{:S(2)}) collective-permute-start(f32[256,128]{1,0:T(8,128)S(1)} %add.34), channel_id=1, source_target_pairs={{0,6},{1,7},{2,4},{3,5},{4,2},{5,3},{6,0},{7,1},{8,14},{9,15},{10,... | collective-permute-start | bytes 393224 | tf_op jit(solution)/shard_map/ppermute | solution.py:280
  35.2 3.8 %collective-permute-done.6 = f32[256,128]{1,0:T(8,128)S(1)} collective-permute-done((f32[256,128]{1,0:T(8,128)S(1)}, f32[256,128]{1,0:T(8,128)S(1)}, u32[]{:S(2)}, u32[]{:S(2)}) %collective-permute-start.6) | collective-permute-done | bytes 131104 | tf_op jit(solution)/shard_map/ppermute | solution.py:280
  39.1 0.1 collective-permute-start.7
  39.2 0.7 %shard_map.69 = (f32[4,128]{1,0:T(4,128)S(1)}, f32[1,128]{1,0:T(1,128)S(1)}) custom-call(f32[256,128]{1,0:T(8,128)S(1)} %add_add_fusion.own_ref, bf16[4,4096,128]{2,1,0:T(8,128)(2,1)S(1)} %get-tuple-element.18.x_ref), custom_call_target="tpu_custom_call" | custom-call | flops 67108864 | bytes 1048576 | tf_op jit(solution)/shard_map/pallas_call | solution.py:358
  39.9 0.6 %collective-permute-done.7.other_ref = f32[256,128]{1,0:T(8,128)S(1)} collective-permute-done((f32[256,128]{1,0:T(8,128)S(1)}, f32[256,128]{1,0:T(8,128)S(1)}, u32[]{:S(2)}, u32[]{:S(2)}) %collective-permute-start.7) | collective-permute-done | bytes 131104 | tf_op jit(solution)/shard_map/ppermute | solution.py:280
  40.5 1.3 %shard_map.70 = (f32[1,32]{1,0:T(1,128)}, f32[1,32]{1,0:T(1,128)}, f32[1,128]{1,0:T(1,128)S(1)}) custom-call(f32[4,128]{1,0:T(4,128)S(1)} %get-tuple-element.21.part_ref, f32[1,128]{1,0:T(1,128)S(1)} %get-tuple-element.22.norm_ref, f32[256,128]{1,0:T(8,128)S(1)} %collective-permute-done.7.other_ref, f32[18,8,128]{2,1,0:T(8,128)S(1)} %get-tuple-element.23.state_ref, ...), custom_call_target="tpu_custom_call" | custom-call | flops 67108864 | bytes 1048576 | tf_op jit(solution)/shard_map/pallas_call | solution.py:359
  41.8 0.1 collective-permute-start.8
  42.0 1.0 %collective-permute-done.8 = f32[1,128]{1,0:T(1,128)S(1)} collective-permute-done((f32[1,128]{1,0:T(1,128)S(1)}, f32[1,128]{1,0:T(1,128)S(1)}, u32[]{:S(2)}, u32[]{:S(2)}) %collective-permute-start.8) | collective-permute-done | bytes 544 | tf_op jit(solution)/shard_map/ppermute | solution.py:280
  43.0 2.5 %collective-permute-start.9 = (f32[1,128]{1,0:T(1,128)S(1)}, f32[1,128]{1,0:T(1,128)S(1)}, u32[]{:S(2)}, u32[]{:S(2)}) collective-permute-start(f32[1,128]{1,0:T(1,128)S(1)} %add.37), channel_id=1, source_target_pairs={{0,2},{1,3},{2,0},{3,1},{4,6},{5,7},{6,4},{7,5},{8,10},{9,11},{10,... | collective-permute-start | bytes 1544 | tf_op jit(solution)/shard_map/ppermute | solution.py:280
  45.5 1.5 %collective-permute-done.9 = f32[1,128]{1,0:T(1,128)S(1)} collective-permute-done((f32[1,128]{1,0:T(1,128)S(1)}, f32[1,128]{1,0:T(1,128)S(1)}, u32[]{:S(2)}, u32[]{:S(2)}) %collective-permute-start.9) | collective-permute-done | bytes 544 | tf_op jit(solution)/shard_map/ppermute | solution.py:280
  47.0 3.2 %collective-permute-start.10 = (f32[1,128]{1,0:T(1,128)S(1)}, f32[1,128]{1,0:T(1,128)S(1)}, u32[]{:S(2)}, u32[]{:S(2)}) collective-permute-start(f32[1,128]{1,0:T(1,128)S(1)} %add.38), channel_id=1, source_target_pairs={{0,4},{1,5},{2,6},{3,7},{4,0},{5,1},{6,2},{7,3},{8,12},{9,13},{10,... | collective-permute-start | bytes 1544 | tf_op jit(solution)/shard_map/ppermute | solution.py:280
  50.2 1.5 %collective-permute-done.10 = f32[1,128]{1,0:T(1,128)S(1)} collective-permute-done((f32[1,128]{1,0:T(1,128)S(1)}, f32[1,128]{1,0:T(1,128)S(1)}, u32[]{:S(2)}, u32[]{:S(2)}) %collective-permute-start.10) | collective-permute-done | bytes 544 | tf_op jit(solution)/shard_map/ppermute | solution.py:280
  51.8 0.5 add.39
  (8 shorter events, 0.1 us)
Async XLA Ops:
  5.5 1.5 %collective-permute-start = (f32[256,128]{1,0:T(8,128)S(1)}, f32[256,128]{1,0:T(8,128)S(1)}, u32[]{:S(2)}, u32[]{:S(2)}) collective-permute-start(f32[256,128]{1,0:T(8,128)S(1)} %get-tuple-element.16), channel_id=1, source_target_pairs={{0,1},{1,0},{2,3},{3,2},{4,5},{5,4},{6,7},{7,6},{8,9},{9,8},{10,11... | collective-permute-start | bytes 393224 | tf_op jit(solution)/shard_map/ppermute | solution.py:280
  7.1 6.8 %collective-permute-start.1 = (f32[256,128]{1,0:T(8,128)S(1)}, f32[256,128]{1,0:T(8,128)S(1)}, u32[]{:S(2)}, u32[]{:S(2)}) collective-permute-start(f32[256,128]{1,0:T(8,128)S(1)} %add.30), channel_id=1, source_target_pairs={{0,2},{1,3},{2,0},{3,1},{4,6},{5,7},{6,4},{7,5},{8,10},{9,11},{10,... | collective-permute-start | bytes 393224 | tf_op jit(solution)/shard_map/ppermute | solution.py:280
  13.9 6.9 %collective-permute-start.2 = (f32[256,128]{1,0:T(8,128)S(1)}, f32[256,128]{1,0:T(8,128)S(1)}, u32[]{:S(2)}, u32[]{:S(2)}) collective-permute-start(f32[256,128]{1,0:T(8,128)S(1)} %add.31), channel_id=1, source_target_pairs={{0,6},{1,7},{2,4},{3,5},{4,2},{5,3},{6,0},{7,1},{8,14},{9,15},{10,... | collective-permute-start | bytes 393224 | tf_op jit(solution)/shard_map/ppermute | solution.py:280
  20.9 1.4 %collective-permute-start.3 = (f32[256,128]{1,0:T(8,128)S(1)}, f32[256,128]{1,0:T(8,128)S(1)}, u32[]{:S(2)}, u32[]{:S(2)}) collective-permute-start(f32[256,128]{1,0:T(8,128)S(1)} %add.32.own_ref), channel_id=1, source_target_pairs={{0,1},{1,0},{2,3},{3,2},{4,5},{5,4},{6,7},{7,6},{8,9},{9,8},{10,11... | collective-permute-start | bytes 393224 | tf_op jit(solution)/shard_map/ppermute | solution.py:280
  24.4 1.4 %collective-permute-start.4 = (f32[256,128]{1,0:T(8,128)S(1)}, f32[256,128]{1,0:T(8,128)S(1)}, u32[]{:S(2)}, u32[]{:S(2)}) collective-permute-start(f32[256,128]{1,0:T(8,128)S(1)} %get-tuple-element.20), channel_id=1, source_target_pairs={{0,1},{1,0},{2,3},{3,2},{4,5},{5,4},{6,7},{7,6},{8,9},{9,8},{10,11... | collective-permute-start | bytes 393224 | tf_op jit(solution)/shard_map/ppermute | solution.py:280
  25.9 6.2 %collective-permute-start.5 = (f32[256,128]{1,0:T(8,128)S(1)}, f32[256,128]{1,0:T(8,128)S(1)}, u32[]{:S(2)}, u32[]{:S(2)}) collective-permute-start(f32[256,128]{1,0:T(8,128)S(1)} %add.33), channel_id=1, source_target_pairs={{0,2},{1,3},{2,0},{3,1},{4,6},{5,7},{6,4},{7,5},{8,10},{9,11},{10,... | collective-permute-start | bytes 393224 | tf_op jit(solution)/shard_map/ppermute | solution.py:280
  32.1 6.9 %collective-permute-start.6 = (f32[256,128]{1,0:T(8,128)S(1)}, f32[256,128]{1,0:T(8,128)S(1)}, u32[]{:S(2)}, u32[]{:S(2)}) collective-permute-start(f32[256,128]{1,0:T(8,128)S(1)} %add.34), channel_id=1, source_target_pairs={{0,6},{1,7},{2,4},{3,5},{4,2},{5,3},{6,0},{7,1},{8,14},{9,15},{10,... | collective-permute-start | bytes 393224 | tf_op jit(solution)/shard_map/ppermute | solution.py:280
  39.1 1.4 %collective-permute-start.7 = (f32[256,128]{1,0:T(8,128)S(1)}, f32[256,128]{1,0:T(8,128)S(1)}, u32[]{:S(2)}, u32[]{:S(2)}) collective-permute-start(f32[256,128]{1,0:T(8,128)S(1)} %add_add_fusion.own_ref), channel_id=1, source_target_pairs={{0,1},{1,0},{2,3},{3,2},{4,5},{5,4},{6,7},{7,6},{8,9},{9,8},{10,11... | collective-permute-start | bytes 393224 | tf_op jit(solution)/shard_map/ppermute | solution.py:280
  41.8 1.2 %collective-permute-start.8 = (f32[1,128]{1,0:T(1,128)S(1)}, f32[1,128]{1,0:T(1,128)S(1)}, u32[]{:S(2)}, u32[]{:S(2)}) collective-permute-start(f32[1,128]{1,0:T(1,128)S(1)} %get-tuple-element.26), channel_id=1, source_target_pairs={{0,1},{1,0},{2,3},{3,2},{4,5},{5,4},{6,7},{7,6},{8,9},{9,8},{10,11... | collective-permute-start | bytes 1544 | tf_op jit(solution)/shard_map/ppermute | solution.py:280
  43.0 4.0 %collective-permute-start.9 = (f32[1,128]{1,0:T(1,128)S(1)}, f32[1,128]{1,0:T(1,128)S(1)}, u32[]{:S(2)}, u32[]{:S(2)}) collective-permute-start(f32[1,128]{1,0:T(1,128)S(1)} %add.37), channel_id=1, source_target_pairs={{0,2},{1,3},{2,0},{3,1},{4,6},{5,7},{6,4},{7,5},{8,10},{9,11},{10,... | collective-permute-start | bytes 1544 | tf_op jit(solution)/shard_map/ppermute | solution.py:280
  47.0 4.7 %collective-permute-start.10 = (f32[1,128]{1,0:T(1,128)S(1)}, f32[1,128]{1,0:T(1,128)S(1)}, u32[]{:S(2)}, u32[]{:S(2)}) collective-permute-start(f32[1,128]{1,0:T(1,128)S(1)} %add.38), channel_id=1, source_target_pairs={{0,4},{1,5},{2,6},{3,7},{4,0},{5,1},{6,2},{7,3},{8,12},{9,13},{10,... | collective-permute-start | bytes 1544 | tf_op jit(solution)/shard_map/ppermute | solution.py:280

commit v6 on v5

--- a/solution.py
+++ b/solution.py
@@ -16,7 +16,6 @@
 
 F32 = jnp.float32
 BF16 = jnp.bfloat16
-NT = (((1,), (1,)), ((), ()))
 NN = (((1,), (0,)), ((), ()))
 
 STRENGTH, TOTAL, SIGNS = 0, 1, 2
@@ -37,41 +36,6 @@
     shape = (GROUP, GROUP * size)
     wide = jnp.concatenate([line] * (GROUP * size // LANES), axis=1)
     return jnp.where(iota(shape, 1) // size == iota(shape, 0), wide, 0.0).astype(BF16)
-
-
-def products(x_ref, block, weights, first, size):
-    groups = weights.shape[0] // GROUP
-    left = jnp.concatenate(
-        [weights[g * GROUP : (g + 1) * GROUP] for g in range(groups)], axis=1
-    ).astype(BF16)
-    begin = first * size
-    right = jnp.concatenate(
-        [
-            x_ref[block, pl.ds(begin + g * GROUP * size, GROUP * size), :]
-            for g in range(groups)
-        ],
-        axis=1,
-    )
-    return lax.dot_general(left, right, NT, preferred_element_type=F32)
-
-
-def same_tile(product, size):
-    shape = product.shape
-    line = jnp.sum(
-        jnp.where(iota(shape, 1) // size == iota(shape, 0), product, 0.0), axis=0, keepdims=True
-    )
-    total = line[:, 0:LANES]
-    for begin in range(LANES, shape[1], LANES):
-        total = total + line[:, begin : begin + LANES]
-    return total
-
-
-def per_sample(line, size):
-    column = jnp.sum(
-        jnp.where(iota((size, LANES), 1) % size == iota((size, LANES), 0), line, 0.0),
-        axis=1, keepdims=True,
-    )
-    return jnp.broadcast_to(column, (size, LANES))
 
 
 def block_step(signs, dual, squared, score, total, sigma):
@@ -194,20 +158,27 @@
     split_halves(sum_ref, keep_ref, send_ref, (scale / total)[0:1, 0:1])
 
 
-def half_lines(x_ref, weights, core):
+def half_products(x_ref, weights_ref, round_ref, core):
     blocks = x_ref.shape[0]
-    half = weights.shape[0]
+    half = weights_ref.shape[0]
     size = x_ref.shape[1] // (2 * half)
-    return [
-        same_tile(products(x_ref, block, weights, core * half, size), size) for block in range(blocks)
-    ]
-
-
-def score_norm_kernel(own_ref, x_ref, part_ref, norm_ref):
+    totals = [no_totals(size)[:2] for _ in range(blocks)]
+    round_ref[...] = weights_ref[...].astype(BF16).astype(F32)
+    for begin in range(0, half, GROUP):
+        rows = pl.ds(pl.multiple_of((core * half + begin) * size, GROUP * size), GROUP * size)
+        for block in range(blocks):
+            values = x_ref[block, rows, :].astype(F32)
+            for tile in range(GROUP):
+                term = values[tile * size : (tile + 1) * size] * round_ref[begin + tile : begin + tile + 1]
+                totals[block][tile % 2] = totals[block][tile % 2] + term
+    return [first + second for first, second in totals]
+
+
+def score_norm_kernel(own_ref, x_ref, part_ref, norm_ref, round_ref):
     own = own_ref[...]
-    lines = half_lines(x_ref, own, core_index())
-    for block in range(len(lines)):
-        part_ref[block : block + 1] = lines[block]
+    parts = half_products(x_ref, own_ref, round_ref, core_index())
+    for block, part in enumerate(parts):
+        part_ref[block] = part
     norm = jnp.sum(jnp.sum(own * own, axis=0, keepdims=True), axis=1, keepdims=True)
     norm_ref[...] = jnp.broadcast_to(norm, norm_ref.shape)
 
@@ -257,23 +228,27 @@
 
 
 def last_kernel(samples, chips, part_ref, norm_ref, other_ref, state_ref, x_ref,
-                dual_ref, margin_ref, share_ref):
+                share_ref, margin_ref, round_ref):
     blocks = x_ref.shape[0]
     half = other_ref.shape[0]
     size = x_ref.shape[1] // (2 * half)
     scale = 1.0 / math.sqrt(2 * half * LANES)
-    lines = half_lines(x_ref, other_ref[...], 1 - core_index())
-    margins, spread = [], jnp.zeros((size, LANES), F32)
+    parts = half_products(x_ref, other_ref, round_ref, 1 - core_index())
+    spread = jnp.zeros((size, LANES), F32)
     for block in range(blocks):
-        margins.append(scale * per_sample(part_ref[block : block + 1] + lines[block], size))
-        hinge = jnp.maximum(0.0, 1.0 - state_ref[SIGNS + block] * margins[block])
+        margins = total_score([part_ref[block] + parts[block]], scale)
+        margin_ref[block] = margins
+        hinge = jnp.maximum(0.0, 1.0 - state_ref[SIGNS + block] * margins)
         spread = spread + (hinge - state_ref[DUAL + block])
     share = jnp.sum(spread, axis=0, keepdims=True) / samples
-    norm = state_ref[STRENGTH][0:1] * norm_ref[...] / chips
-    share_ref[...] = norm + share
+    share_ref[...] = state_ref[STRENGTH][0:1] * norm_ref[...] / chips + share
+
+
+def line_kernel(state_ref, margin_ref, dual_ref, out_ref):
+    blocks = margin_ref.shape[0]
     places = [state_ref[PLACE + block] for block in range(blocks)]
     dual_ref[...] = in_line([state_ref[DUAL + block] for block in range(blocks)], places)
-    margin_ref[...] = in_line(margins, places)
+    out_ref[...] = in_line([margin_ref[block] for block in range(blocks)], places)
 
 
 def swap(value, peers, mask):
@@ -355,10 +330,13 @@
                 [whole] * 3,
                 work,
             )(own, other, state, x)
-    part, norm = call(score_norm_kernel, [((blocks, LANES), F32), scalar], [V, V], work=work)(own, x)
-    dual, margins, share = call(
-        functools.partial(last_kernel, samples, peers // 2), [line, line, scalar], [V] * 5, work=work
+    pieces = ((blocks, size, LANES), F32)
+    rounded = [pltpu.VMEM((tiles // 2, LANES), F32)]
+    part, norm = call(score_norm_kernel, [pieces, scalar], [V, V], rounded, work)(own, x)
+    share, spread = call(
+        functools.partial(last_kernel, samples, peers // 2), [scalar, pieces], [V] * 5, rounded, work
     )(part, norm, other, state, x)
+    dual, margins = call(line_kernel, [line, line], [V] * 2, work=work)(state, spread)
     mask = 1
     while mask < peers:
         share = share + swap(share, peers, mask)

time: 52.5 us -> 51.7 us (0.985)
    pallas_call x2 -> x3, Pallas kernels: 2.07 us -> 1.63 us  [the longest x1 0.57 us: shards(): call(functools.partial(last_kernel, samples, peers // 2), [scalar, pieces...]
  transfers between devices with their start and end apart: 11 -> 11, of which waited for: 11 -> 11; matrix products, arithmetic and copies ran while one was open for 0% -> 0% of each run, Pallas kernels for 1% -> 2%
where the time goes in v6:
time: 51.7 us; the launch traced here: 51.5 us
  waiting for transfers between devices  22.5 us (44%)
  starting transfers between devices  19.1 us (37%)
  Pallas kernels  8 us (15%)
  between operations  1.33 us (3%)
  other arithmetic  0.64 us (1%)
    ppermute x11, waiting for transfers between devices, swap(): return lax.ppermute(value, 'blk', [(i, i ^ mask) for i in range(peers)])  22.5 us
    ppermute x11, starting transfers between devices, swap(): return lax.ppermute(value, 'blk', [(i, i ^ mask) for i in range(peers)])  19.1 us
    pallas_call x1, Pallas kernels, shards(): call(functools.partial(first_kernel, samples, float(peers)), [half, half,...  4.25 us
    pallas_call x1, Pallas kernels, shards(): call(functools.partial(next_kernel, float(peers)), [half, half, state_sha...  2.12 us
  transfers between devices with their start and end apart: 11, of which 11 were waited for; matrix products, arithmetic and copies ran while one was open for 0% of the time, Pallas kernels for 2%

profile of v6, /device:TPU:0, one launch (start us, length us, event | category | flops | bytes accessed | tf_op | source)
XLA Modules:
  0.0 51.5 jit_solution(13968199034390616504)
XLA Ops:
  1.3 4.3 %shard_map.67 = (f32[256,128]{1,0:T(8,128)S(1)}, f32[256,128]{1,0:T(8,128)S(1)}, f32[18,8,128]{2,1,0:T(8,128)S(1)}, bf16[4,4096,128]{2,1,0:T(8,128)(2,1)S(1)}) custom-call(s32[1]{0:T(128)S(6)} %copy.7.reg_ref, s32[1,4]{1,0:T(1,128)} %order_hbm.1, s32[1,32]{1,0:T(1,128)} %bitcast.11, bf16[4,4096,128]{2,1,0:T(8,128)(2,1)} %bitcast.10), custom_call_target="tpu_custom_call" | custom-call | flops 67108864 | bytes 1048576 | tf_op jit(solution)/shard_map/pallas_call | solution.py:305
  5.5 0.6 %collective-permute-start = (f32[256,128]{1,0:T(8,128)S(1)}, f32[256,128]{1,0:T(8,128)S(1)}, u32[]{:S(2)}, u32[]{:S(2)}) collective-permute-start(f32[256,128]{1,0:T(8,128)S(1)} %get-tuple-element.17), channel_id=1, source_target_pairs={{0,1},{1,0},{2,3},{3,2},{4,5},{5,4},{6,7},{7,6},{8,9},{9,8},{10,11... | collective-permute-start | bytes 393224 | tf_op jit(solution)/shard_map/ppermute | solution.py:255
  6.1 1.0 %collective-permute-done = f32[256,128]{1,0:T(8,128)S(1)} collective-permute-done((f32[256,128]{1,0:T(8,128)S(1)}, f32[256,128]{1,0:T(8,128)S(1)}, u32[]{:S(2)}, u32[]{:S(2)}) %collective-permute-start) | collective-permute-done | bytes 131104 | tf_op jit(solution)/shard_map/ppermute | solution.py:255
  7.1 3.0 %collective-permute-start.1 = (f32[256,128]{1,0:T(8,128)S(1)}, f32[256,128]{1,0:T(8,128)S(1)}, u32[]{:S(2)}, u32[]{:S(2)}) collective-permute-start(f32[256,128]{1,0:T(8,128)S(1)} %add.30), channel_id=1, source_target_pairs={{0,2},{1,3},{2,0},{3,1},{4,6},{5,7},{6,4},{7,5},{8,10},{9,11},{10,... | collective-permute-start | bytes 393224 | tf_op jit(solution)/shard_map/ppermute | solution.py:255
  10.1 3.8 %collective-permute-done.1 = f32[256,128]{1,0:T(8,128)S(1)} collective-permute-done((f32[256,128]{1,0:T(8,128)S(1)}, f32[256,128]{1,0:T(8,128)S(1)}, u32[]{:S(2)}, u32[]{:S(2)}) %collective-permute-start.1) | collective-permute-done | bytes 131104 | tf_op jit(solution)/shard_map/ppermute | solution.py:255
  13.9 3.8 %collective-permute-start.2 = (f32[256,128]{1,0:T(8,128)S(1)}, f32[256,128]{1,0:T(8,128)S(1)}, u32[]{:S(2)}, u32[]{:S(2)}) collective-permute-start(f32[256,128]{1,0:T(8,128)S(1)} %add.31), channel_id=1, source_target_pairs={{0,6},{1,7},{2,4},{3,5},{4,2},{5,3},{6,0},{7,1},{8,14},{9,15},{10,... | collective-permute-start | bytes 393224 | tf_op jit(solution)/shard_map/ppermute | solution.py:255
  17.8 3.1 %collective-permute-done.2 = f32[256,128]{1,0:T(8,128)S(1)} collective-permute-done((f32[256,128]{1,0:T(8,128)S(1)}, f32[256,128]{1,0:T(8,128)S(1)}, u32[]{:S(2)}, u32[]{:S(2)}) %collective-permute-start.2) | collective-permute-done | bytes 131104 | tf_op jit(solution)/shard_map/ppermute | solution.py:255
  20.9 0.1 collective-permute-start.3
  21.0 1.3 %collective-permute-done.3.other_ref = f32[256,128]{1,0:T(8,128)S(1)} collective-permute-done((f32[256,128]{1,0:T(8,128)S(1)}, f32[256,128]{1,0:T(8,128)S(1)}, u32[]{:S(2)}, u32[]{:S(2)}) %collective-permute-start.3) | collective-permute-done | bytes 131104 | tf_op jit(solution)/shard_map/ppermute | solution.py:255
  22.3 2.1 %shard_map.68 = (f32[256,128]{1,0:T(8,128)S(1)}, f32[256,128]{1,0:T(8,128)S(1)}, f32[18,8,128]{2,1,0:T(8,128)S(1)}) custom-call(f32[256,128]{1,0:T(8,128)S(1)} %add.32.own_ref, f32[256,128]{1,0:T(8,128)S(1)} %collective-permute-done.3.other_ref, f32[18,8,128]{2,1,0:T(8,128)S(1)} %get-tuple-element.18.state_ref, bf16[4,4096,128]{2,1,0:T(8,128)(2,1)S(1)} %get-tuple-element.19.x_ref), custom_call_target="tpu_custom_call" | custom-call | flops 67108864 | bytes 1048576 | tf_op jit(solution)/shard_map/pallas_call | solution.py:326
  24.4 0.2 collective-permute-start.4
  24.6 1.2 %collective-permute-done.4 = f32[256,128]{1,0:T(8,128)S(1)} collective-permute-done((f32[256,128]{1,0:T(8,128)S(1)}, f32[256,128]{1,0:T(8,128)S(1)}, u32[]{:S(2)}, u32[]{:S(2)}) %collective-permute-start.4) | collective-permute-done | bytes 131104 | tf_op jit(solution)/shard_map/ppermute | solution.py:255
  25.9 2.4 %collective-permute-start.5 = (f32[256,128]{1,0:T(8,128)S(1)}, f32[256,128]{1,0:T(8,128)S(1)}, u32[]{:S(2)}, u32[]{:S(2)}) collective-permute-start(f32[256,128]{1,0:T(8,128)S(1)} %add.33), channel_id=1, source_target_pairs={{0,2},{1,3},{2,0},{3,1},{4,6},{5,7},{6,4},{7,5},{8,10},{9,11},{10,... | collective-permute-start | bytes 393224 | tf_op jit(solution)/shard_map/ppermute | solution.py:255
  28.3 3.8 %collective-permute-done.5 = f32[256,128]{1,0:T(8,128)S(1)} collective-permute-done((f32[256,128]{1,0:T(8,128)S(1)}, f32[256,128]{1,0:T(8,128)S(1)}, u32[]{:S(2)}, u32[]{:S(2)}) %collective-permute-start.5) | collective-permute-done | bytes 131104 | tf_op jit(solution)/shard_map/ppermute | solution.py:255
  32.1 3.1 %collective-permute-start.6 = (f32[256,128]{1,0:T(8,128)S(1)}, f32[256,128]{1,0:T(8,128)S(1)}, u32[]{:S(2)}, u32[]{:S(2)}) collective-permute-start(f32[256,128]{1,0:T(8,128)S(1)} %add.34), channel_id=1, source_target_pairs={{0,6},{1,7},{2,4},{3,5},{4,2},{5,3},{6,0},{7,1},{8,14},{9,15},{10,... | collective-permute-start | bytes 393224 | tf_op jit(solution)/shard_map/ppermute | solution.py:255
  35.2 3.8 %collective-permute-done.6 = f32[256,128]{1,0:T(8,128)S(1)} collective-permute-done((f32[256,128]{1,0:T(8,128)S(1)}, f32[256,128]{1,0:T(8,128)S(1)}, u32[]{:S(2)}, u32[]{:S(2)}) %collective-permute-start.6) | collective-permute-done | bytes 131104 | tf_op jit(solution)/shard_map/ppermute | solution.py:255
  39.1 0.1 collective-permute-start.7
  39.2 0.5 %shard_map.69 = (f32[4,8,128]{2,1,0:T(8,128)S(1)}, f32[1,128]{1,0:T(1,128)S(1)}) custom-call(f32[256,128]{1,0:T(8,128)S(1)} %add_add_fusion.own_ref, bf16[4,4096,128]{2,1,0:T(8,128)(2,1)S(1)} %get-tuple-element.19.x_ref), custom_call_target="tpu_custom_call" | custom-call | flops 67108864 | bytes 1048576 | tf_op jit(solution)/shard_map/pallas_call | solution.py:335
  39.7 0.8 %collective-permute-done.7.other_ref = f32[256,128]{1,0:T(8,128)S(1)} collective-permute-done((f32[256,128]{1,0:T(8,128)S(1)}, f32[256,128]{1,0:T(8,128)S(1)}, u32[]{:S(2)}, u32[]{:S(2)}) %collective-permute-start.7) | collective-permute-done | bytes 131104 | tf_op jit(solution)/shard_map/ppermute | solution.py:255
  40.5 0.6 %shard_map.70 = (f32[1,128]{1,0:T(1,128)S(1)}, f32[4,8,128]{2,1,0:T(8,128)S(1)}) custom-call(f32[4,8,128]{2,1,0:T(8,128)S(1)} %get-tuple-element.23.part_ref, f32[1,128]{1,0:T(1,128)S(1)} %get-tuple-element.24.norm_ref, f32[256,128]{1,0:T(8,128)S(1)} %collective-permute-done.7.other_ref, f32[18,8,128]{2,1,0:T(8,128)S(1)} %get-tuple-element.20.state_ref, ...), custom_call_target="tpu_custom_call" | custom-call | flops 67108864 | bytes 1048576 | tf_op jit(solution)/shard_map/pallas_call | solution.py:336
  41.1 0.2 collective-permute-start.8
  41.2 1.0 %collective-permute-done.8 = f32[1,128]{1,0:T(1,128)S(1)} collective-permute-done((f32[1,128]{1,0:T(1,128)S(1)}, f32[1,128]{1,0:T(1,128)S(1)}, u32[]{:S(2)}, u32[]{:S(2)}) %collective-permute-start.8) | collective-permute-done | bytes 544 | tf_op jit(solution)/shard_map/ppermute | solution.py:255
  42.2 2.5 %collective-permute-start.9 = (f32[1,128]{1,0:T(1,128)S(1)}, f32[1,128]{1,0:T(1,128)S(1)}, u32[]{:S(2)}, u32[]{:S(2)}) collective-permute-start(f32[1,128]{1,0:T(1,128)S(1)} %add.37), channel_id=1, source_target_pairs={{0,2},{1,3},{2,0},{3,1},{4,6},{5,7},{6,4},{7,5},{8,10},{9,11},{10,... | collective-permute-start | bytes 1544 | tf_op jit(solution)/shard_map/ppermute | solution.py:255
  44.7 1.5 %collective-permute-done.9 = f32[1,128]{1,0:T(1,128)S(1)} collective-permute-done((f32[1,128]{1,0:T(1,128)S(1)}, f32[1,128]{1,0:T(1,128)S(1)}, u32[]{:S(2)}, u32[]{:S(2)}) %collective-permute-start.9) | collective-permute-done | bytes 544 | tf_op jit(solution)/shard_map/ppermute | solution.py:255
  46.3 3.2 %collective-permute-start.10 = (f32[1,128]{1,0:T(1,128)S(1)}, f32[1,128]{1,0:T(1,128)S(1)}, u32[]{:S(2)}, u32[]{:S(2)}) collective-permute-start(f32[1,128]{1,0:T(1,128)S(1)} %add.38), channel_id=1, source_target_pairs={{0,4},{1,5},{2,6},{3,7},{4,0},{5,1},{6,2},{7,3},{8,12},{9,13},{10,... | collective-permute-start | bytes 1544 | tf_op jit(solution)/shard_map/ppermute | solution.py:255
  49.5 0.5 %shard_map.71 = (f32[1,32]{1,0:T(1,128)}, f32[1,32]{1,0:T(1,128)}) custom-call(f32[18,8,128]{2,1,0:T(8,128)S(1)} %get-tuple-element.20.state_ref, f32[4,8,128]{2,1,0:T(8,128)S(1)} %get-tuple-element.25.margin_ref), custom_call_target="tpu_custom_call" | custom-call | flops 67108864 | bytes 1048576 | tf_op jit(solution)/shard_map/pallas_call | solution.py:339
  50.0 1.0 %collective-permute-done.10 = f32[1,128]{1,0:T(1,128)S(1)} collective-permute-done((f32[1,128]{1,0:T(1,128)S(1)}, f32[1,128]{1,0:T(1,128)S(1)}, u32[]{:S(2)}, u32[]{:S(2)}) %collective-permute-start.10) | collective-permute-done | bytes 544 | tf_op jit(solution)/shard_map/ppermute | solution.py:255
  51.0 0.5 add.39
  (8 shorter events, 0.1 us)
Async XLA Ops:
  5.5 1.5 %collective-permute-start = (f32[256,128]{1,0:T(8,128)S(1)}, f32[256,128]{1,0:T(8,128)S(1)}, u32[]{:S(2)}, u32[]{:S(2)}) collective-permute-start(f32[256,128]{1,0:T(8,128)S(1)} %get-tuple-element.17), channel_id=1, source_target_pairs={{0,1},{1,0},{2,3},{3,2},{4,5},{5,4},{6,7},{7,6},{8,9},{9,8},{10,11... | collective-permute-start | bytes 393224 | tf_op jit(solution)/shard_map/ppermute | solution.py:255
  7.1 6.8 %collective-permute-start.1 = (f32[256,128]{1,0:T(8,128)S(1)}, f32[256,128]{1,0:T(8,128)S(1)}, u32[]{:S(2)}, u32[]{:S(2)}) collective-permute-start(f32[256,128]{1,0:T(8,128)S(1)} %add.30), channel_id=1, source_target_pairs={{0,2},{1,3},{2,0},{3,1},{4,6},{5,7},{6,4},{7,5},{8,10},{9,11},{10,... | collective-permute-start | bytes 393224 | tf_op jit(solution)/shard_map/ppermute | solution.py:255
  13.9 6.9 %collective-permute-start.2 = (f32[256,128]{1,0:T(8,128)S(1)}, f32[256,128]{1,0:T(8,128)S(1)}, u32[]{:S(2)}, u32[]{:S(2)}) collective-permute-start(f32[256,128]{1,0:T(8,128)S(1)} %add.31), channel_id=1, source_target_pairs={{0,6},{1,7},{2,4},{3,5},{4,2},{5,3},{6,0},{7,1},{8,14},{9,15},{10,... | collective-permute-start | bytes 393224 | tf_op jit(solution)/shard_map/ppermute | solution.py:255
  20.9 1.4 %collective-permute-start.3 = (f32[256,128]{1,0:T(8,128)S(1)}, f32[256,128]{1,0:T(8,128)S(1)}, u32[]{:S(2)}, u32[]{:S(2)}) collective-permute-start(f32[256,128]{1,0:T(8,128)S(1)} %add.32.own_ref), channel_id=1, source_target_pairs={{0,1},{1,0},{2,3},{3,2},{4,5},{5,4},{6,7},{7,6},{8,9},{9,8},{10,11... | collective-permute-start | bytes 393224 | tf_op jit(solution)/shard_map/ppermute | solution.py:255
  24.4 1.4 %collective-permute-start.4 = (f32[256,128]{1,0:T(8,128)S(1)}, f32[256,128]{1,0:T(8,128)S(1)}, u32[]{:S(2)}, u32[]{:S(2)}) collective-permute-start(f32[256,128]{1,0:T(8,128)S(1)} %get-tuple-element.22), channel_id=1, source_target_pairs={{0,1},{1,0},{2,3},{3,2},{4,5},{5,4},{6,7},{7,6},{8,9},{9,8},{10,11... | collective-permute-start | bytes 393224 | tf_op jit(solution)/shard_map/ppermute | solution.py:255
  25.9 6.2 %collective-permute-start.5 = (f32[256,128]{1,0:T(8,128)S(1)}, f32[256,128]{1,0:T(8,128)S(1)}, u32[]{:S(2)}, u32[]{:S(2)}) collective-permute-start(f32[256,128]{1,0:T(8,128)S(1)} %add.33), channel_id=1, source_target_pairs={{0,2},{1,3},{2,0},{3,1},{4,6},{5,7},{6,4},{7,5},{8,10},{9,11},{10,... | collective-permute-start | bytes 393224 | tf_op jit(solution)/shard_map/ppermute | solution.py:255
  32.1 6.9 %collective-permute-start.6 = (f32[256,128]{1,0:T(8,128)S(1)}, f32[256,128]{1,0:T(8,128)S(1)}, u32[]{:S(2)}, u32[]{:S(2)}) collective-permute-start(f32[256,128]{1,0:T(8,128)S(1)} %add.34), channel_id=1, source_target_pairs={{0,6},{1,7},{2,4},{3,5},{4,2},{5,3},{6,0},{7,1},{8,14},{9,15},{10,... | collective-permute-start | bytes 393224 | tf_op jit(solution)/shard_map/ppermute | solution.py:255
  39.1 1.4 %collective-permute-start.7 = (f32[256,128]{1,0:T(8,128)S(1)}, f32[256,128]{1,0:T(8,128)S(1)}, u32[]{:S(2)}, u32[]{:S(2)}) collective-permute-start(f32[256,128]{1,0:T(8,128)S(1)} %add_add_fusion.own_ref), channel_id=1, source_target_pairs={{0,1},{1,0},{2,3},{3,2},{4,5},{5,4},{6,7},{7,6},{8,9},{9,8},{10,11... | collective-permute-start | bytes 393224 | tf_op jit(solution)/shard_map/ppermute | solution.py:255
  41.1 1.2 %collective-permute-start.8 = (f32[1,128]{1,0:T(1,128)S(1)}, f32[1,128]{1,0:T(1,128)S(1)}, u32[]{:S(2)}, u32[]{:S(2)}) collective-permute-start(f32[1,128]{1,0:T(1,128)S(1)} %get-tuple-element.28), channel_id=1, source_target_pairs={{0,1},{1,0},{2,3},{3,2},{4,5},{5,4},{6,7},{7,6},{8,9},{9,8},{10,11... | collective-permute-start | bytes 1544 | tf_op jit(solution)/shard_map/ppermute | solution.py:255
  42.2 4.0 %collective-permute-start.9 = (f32[1,128]{1,0:T(1,128)S(1)}, f32[1,128]{1,0:T(1,128)S(1)}, u32[]{:S(2)}, u32[]{:S(2)}) collective-permute-start(f32[1,128]{1,0:T(1,128)S(1)} %add.37), channel_id=1, source_target_pairs={{0,2},{1,3},{2,0},{3,1},{4,6},{5,7},{6,4},{7,5},{8,10},{9,11},{10,... | collective-permute-start | bytes 1544 | tf_op jit(solution)/shard_map/ppermute | solution.py:255
  46.3 4.7 %collective-permute-start.10 = (f32[1,128]{1,0:T(1,128)S(1)}, f32[1,128]{1,0:T(1,128)S(1)}, u32[]{:S(2)}, u32[]{:S(2)}) collective-permute-start(f32[1,128]{1,0:T(1,128)S(1)} %add.38), channel_id=1, source_target_pairs={{0,4},{1,5},{2,6},{3,7},{4,0},{5,1},{6,2},{7,3},{8,12},{9,13},{10,... | collective-permute-start | bytes 1544 | tf_op jit(solution)/shard_map/ppermute | solution.py:255

commit v7 on v6

--- a/solution.py
+++ b/solution.py
@@ -11,7 +11,7 @@
 ROUNDS = 2
 BLOCKS = 4
 LANES = 128
-GROUP = 32
+GROUP = 16
 VMEM_LIMIT = 12 * 1024 * 1024
 
 F32 = jnp.float32

time: 51.7 us -> 51.8 us (level)
  no operation moved by 1% of the time
where the time goes in v7:
time: 51.8 us; the launch traced here: 51.7 us
  waiting for transfers between devices  22.5 us (43%)
  starting transfers between devices  19.1 us (37%)
  Pallas kernels  8.13 us (16%)
  between operations  1.33 us (3%)
  other arithmetic  0.64 us (1%)
    ppermute x11, waiting for transfers between devices, swap(): return lax.ppermute(value, 'blk', [(i, i ^ mask) for i in range(peers)])  22.5 us
    ppermute x11, starting transfers between devices, swap(): return lax.ppermute(value, 'blk', [(i, i ^ mask) for i in range(peers)])  19.1 us
    pallas_call x1, Pallas kernels, shards(): call(functools.partial(first_kernel, samples, float(peers)), [half, half,...  4.27 us
    pallas_call x1, Pallas kernels, shards(): call(functools.partial(next_kernel, float(peers)), [half, half, state_sha...  2.25 us
  transfers between devices with their start and end apart: 11, of which 11 were waited for; matrix products, arithmetic and copies ran while one was open for 0% of the time, Pallas kernels for 2%

profile of v7, /device:TPU:0, one launch (start us, length us, event | category | flops | bytes accessed | tf_op | source)
XLA Modules:
  0.0 51.7 jit_solution(16301888725529756846)
XLA Ops:
  1.3 4.3 %shard_map.67 = (f32[256,128]{1,0:T(8,128)S(1)}, f32[256,128]{1,0:T(8,128)S(1)}, f32[18,8,128]{2,1,0:T(8,128)S(1)}, bf16[4,4096,128]{2,1,0:T(8,128)(2,1)S(1)}) custom-call(s32[1]{0:T(128)S(6)} %copy.7.reg_ref, s32[1,4]{1,0:T(1,128)} %order_hbm.1, s32[1,32]{1,0:T(1,128)} %bitcast.11, bf16[4,4096,128]{2,1,0:T(8,128)(2,1)} %bitcast.10), custom_call_target="tpu_custom_call" | custom-call | flops 67108864 | bytes 1048576 | tf_op jit(solution)/shard_map/pallas_call | solution.py:305
  5.6 0.6 %collective-permute-start = (f32[256,128]{1,0:T(8,128)S(1)}, f32[256,128]{1,0:T(8,128)S(1)}, u32[]{:S(2)}, u32[]{:S(2)}) collective-permute-start(f32[256,128]{1,0:T(8,128)S(1)} %get-tuple-element.17), channel_id=1, source_target_pairs={{0,1},{1,0},{2,3},{3,2},{4,5},{5,4},{6,7},{7,6},{8,9},{9,8},{10,11... | collective-permute-start | bytes 393224 | tf_op jit(solution)/shard_map/ppermute | solution.py:255
  6.1 1.0 %collective-permute-done = f32[256,128]{1,0:T(8,128)S(1)} collective-permute-done((f32[256,128]{1,0:T(8,128)S(1)}, f32[256,128]{1,0:T(8,128)S(1)}, u32[]{:S(2)}, u32[]{:S(2)}) %collective-permute-start) | collective-permute-done | bytes 131104 | tf_op jit(solution)/shard_map/ppermute | solution.py:255
  7.1 3.0 %collective-permute-start.1 = (f32[256,128]{1,0:T(8,128)S(1)}, f32[256,128]{1,0:T(8,128)S(1)}, u32[]{:S(2)}, u32[]{:S(2)}) collective-permute-start(f32[256,128]{1,0:T(8,128)S(1)} %add.30), channel_id=1, source_target_pairs={{0,2},{1,3},{2,0},{3,1},{4,6},{5,7},{6,4},{7,5},{8,10},{9,11},{10,... | collective-permute-start | bytes 393224 | tf_op jit(solution)/shard_map/ppermute | solution.py:255
  10.1 3.8 %collective-permute-done.1 = f32[256,128]{1,0:T(8,128)S(1)} collective-permute-done((f32[256,128]{1,0:T(8,128)S(1)}, f32[256,128]{1,0:T(8,128)S(1)}, u32[]{:S(2)}, u32[]{:S(2)}) %collective-permute-start.1) | collective-permute-done | bytes 131104 | tf_op jit(solution)/shard_map/ppermute | solution.py:255
  13.9 3.8 %collective-permute-start.2 = (f32[256,128]{1,0:T(8,128)S(1)}, f32[256,128]{1,0:T(8,128)S(1)}, u32[]{:S(2)}, u32[]{:S(2)}) collective-permute-start(f32[256,128]{1,0:T(8,128)S(1)} %add.31), channel_id=1, source_target_pairs={{0,6},{1,7},{2,4},{3,5},{4,2},{5,3},{6,0},{7,1},{8,14},{9,15},{10,... | collective-permute-start | bytes 393224 | tf_op jit(solution)/shard_map/ppermute | solution.py:255
  17.8 3.1 %collective-permute-done.2 = f32[256,128]{1,0:T(8,128)S(1)} collective-permute-done((f32[256,128]{1,0:T(8,128)S(1)}, f32[256,128]{1,0:T(8,128)S(1)}, u32[]{:S(2)}, u32[]{:S(2)}) %collective-permute-start.2) | collective-permute-done | bytes 131104 | tf_op jit(solution)/shard_map/ppermute | solution.py:255
  20.9 0.1 collective-permute-start.3
  21.0 1.3 %collective-permute-done.3.other_ref = f32[256,128]{1,0:T(8,128)S(1)} collective-permute-done((f32[256,128]{1,0:T(8,128)S(1)}, f32[256,128]{1,0:T(8,128)S(1)}, u32[]{:S(2)}, u32[]{:S(2)}) %collective-permute-start.3) | collective-permute-done | bytes 131104 | tf_op jit(solution)/shard_map/ppermute | solution.py:255
  22.3 2.3 %shard_map.68 = (f32[256,128]{1,0:T(8,128)S(1)}, f32[256,128]{1,0:T(8,128)S(1)}, f32[18,8,128]{2,1,0:T(8,128)S(1)}) custom-call(f32[256,128]{1,0:T(8,128)S(1)} %add.32.own_ref, f32[256,128]{1,0:T(8,128)S(1)} %collective-permute-done.3.other_ref, f32[18,8,128]{2,1,0:T(8,128)S(1)} %get-tuple-element.18.state_ref, bf16[4,4096,128]{2,1,0:T(8,128)(2,1)S(1)} %get-tuple-element.19.x_ref), custom_call_target="tpu_custom_call" | custom-call | flops 67108864 | bytes 1048576 | tf_op jit(solution)/shard_map/pallas_call | solution.py:326
  24.6 0.2 collective-permute-start.4
  24.8 1.2 %collective-permute-done.4 = f32[256,128]{1,0:T(8,128)S(1)} collective-permute-done((f32[256,128]{1,0:T(8,128)S(1)}, f32[256,128]{1,0:T(8,128)S(1)}, u32[]{:S(2)}, u32[]{:S(2)}) %collective-permute-start.4) | collective-permute-done | bytes 131104 | tf_op jit(solution)/shard_map/ppermute | solution.py:255
  26.0 2.4 %collective-permute-start.5 = (f32[256,128]{1,0:T(8,128)S(1)}, f32[256,128]{1,0:T(8,128)S(1)}, u32[]{:S(2)}, u32[]{:S(2)}) collective-permute-start(f32[256,128]{1,0:T(8,128)S(1)} %add.33), channel_id=1, source_target_pairs={{0,2},{1,3},{2,0},{3,1},{4,6},{5,7},{6,4},{7,5},{8,10},{9,11},{10,... | collective-permute-start | bytes 393224 | tf_op jit(solution)/shard_map/ppermute | solution.py:255
  28.4 3.8 %collective-permute-done.5 = f32[256,128]{1,0:T(8,128)S(1)} collective-permute-done((f32[256,128]{1,0:T(8,128)S(1)}, f32[256,128]{1,0:T(8,128)S(1)}, u32[]{:S(2)}, u32[]{:S(2)}) %collective-permute-start.5) | collective-permute-done | bytes 131104 | tf_op jit(solution)/shard_map/ppermute | solution.py:255
  32.3 3.1 %collective-permute-start.6 = (f32[256,128]{1,0:T(8,128)S(1)}, f32[256,128]{1,0:T(8,128)S(1)}, u32[]{:S(2)}, u32[]{:S(2)}) collective-permute-start(f32[256,128]{1,0:T(8,128)S(1)} %add.34), channel_id=1, source_target_pairs={{0,6},{1,7},{2,4},{3,5},{4,2},{5,3},{6,0},{7,1},{8,14},{9,15},{10,... | collective-permute-start | bytes 393224 | tf_op jit(solution)/shard_map/ppermute | solution.py:255
  35.4 3.8 %collective-permute-done.6 = f32[256,128]{1,0:T(8,128)S(1)} collective-permute-done((f32[256,128]{1,0:T(8,128)S(1)}, f32[256,128]{1,0:T(8,128)S(1)}, u32[]{:S(2)}, u32[]{:S(2)}) %collective-permute-start.6) | collective-permute-done | bytes 131104 | tf_op jit(solution)/shard_map/ppermute | solution.py:255
  39.2 0.1 collective-permute-start.7
  39.3 0.5 %shard_map.69 = (f32[4,8,128]{2,1,0:T(8,128)S(1)}, f32[1,128]{1,0:T(1,128)S(1)}) custom-call(f32[256,128]{1,0:T(8,128)S(1)} %add_add_fusion.own_ref, bf16[4,4096,128]{2,1,0:T(8,128)(2,1)S(1)} %get-tuple-element.19.x_ref), custom_call_target="tpu_custom_call" | custom-call | flops 67108864 | bytes 1048576 | tf_op jit(solution)/shard_map/pallas_call | solution.py:335
  39.8 0.8 %collective-permute-done.7.other_ref = f32[256,128]{1,0:T(8,128)S(1)} collective-permute-done((f32[256,128]{1,0:T(8,128)S(1)}, f32[256,128]{1,0:T(8,128)S(1)}, u32[]{:S(2)}, u32[]{:S(2)}) %collective-permute-start.7) | collective-permute-done | bytes 131104 | tf_op jit(solution)/shard_map/ppermute | solution.py:255
  40.6 0.6 %shard_map.70 = (f32[1,128]{1,0:T(1,128)S(1)}, f32[4,8,128]{2,1,0:T(8,128)S(1)}) custom-call(f32[4,8,128]{2,1,0:T(8,128)S(1)} %get-tuple-element.23.part_ref, f32[1,128]{1,0:T(1,128)S(1)} %get-tuple-element.24.norm_ref, f32[256,128]{1,0:T(8,128)S(1)} %collective-permute-done.7.other_ref, f32[18,8,128]{2,1,0:T(8,128)S(1)} %get-tuple-element.20.state_ref, ...), custom_call_target="tpu_custom_call" | custom-call | flops 67108864 | bytes 1048576 | tf_op jit(solution)/shard_map/pallas_call | solution.py:336
  41.2 0.2 collective-permute-start.8
  41.4 1.0 %collective-permute-done.8 = f32[1,128]{1,0:T(1,128)S(1)} collective-permute-done((f32[1,128]{1,0:T(1,128)S(1)}, f32[1,128]{1,0:T(1,128)S(1)}, u32[]{:S(2)}, u32[]{:S(2)}) %collective-permute-start.8) | collective-permute-done | bytes 544 | tf_op jit(solution)/shard_map/ppermute | solution.py:255
  42.4 2.5 %collective-permute-start.9 = (f32[1,128]{1,0:T(1,128)S(1)}, f32[1,128]{1,0:T(1,128)S(1)}, u32[]{:S(2)}, u32[]{:S(2)}) collective-permute-start(f32[1,128]{1,0:T(1,128)S(1)} %add.37), channel_id=1, source_target_pairs={{0,2},{1,3},{2,0},{3,1},{4,6},{5,7},{6,4},{7,5},{8,10},{9,11},{10,... | collective-permute-start | bytes 1544 | tf_op jit(solution)/shard_map/ppermute | solution.py:255
  44.9 1.5 %collective-permute-done.9 = f32[1,128]{1,0:T(1,128)S(1)} collective-permute-done((f32[1,128]{1,0:T(1,128)S(1)}, f32[1,128]{1,0:T(1,128)S(1)}, u32[]{:S(2)}, u32[]{:S(2)}) %collective-permute-start.9) | collective-permute-done | bytes 544 | tf_op jit(solution)/shard_map/ppermute | solution.py:255
  46.4 3.2 %collective-permute-start.10 = (f32[1,128]{1,0:T(1,128)S(1)}, f32[1,128]{1,0:T(1,128)S(1)}, u32[]{:S(2)}, u32[]{:S(2)}) collective-permute-start(f32[1,128]{1,0:T(1,128)S(1)} %add.38), channel_id=1, source_target_pairs={{0,4},{1,5},{2,6},{3,7},{4,0},{5,1},{6,2},{7,3},{8,12},{9,13},{10,... | collective-permute-start | bytes 1544 | tf_op jit(solution)/shard_map/ppermute | solution.py:255
  49.6 0.5 %shard_map.71 = (f32[1,32]{1,0:T(1,128)}, f32[1,32]{1,0:T(1,128)}) custom-call(f32[18,8,128]{2,1,0:T(8,128)S(1)} %get-tuple-element.20.state_ref, f32[4,8,128]{2,1,0:T(8,128)S(1)} %get-tuple-element.25.margin_ref), custom_call_target="tpu_custom_call" | custom-call | flops 67108864 | bytes 1048576 | tf_op jit(solution)/shard_map/pallas_call | solution.py:339
  50.1 1.0 %collective-permute-done.10 = f32[1,128]{1,0:T(1,128)S(1)} collective-permute-done((f32[1,128]{1,0:T(1,128)S(1)}, f32[1,128]{1,0:T(1,128)S(1)}, u32[]{:S(2)}, u32[]{:S(2)}) %collective-permute-start.10) | collective-permute-done | bytes 544 | tf_op jit(solution)/shard_map/ppermute | solution.py:255
  51.2 0.5 add.39
  (8 shorter events, 0.1 us)
Async XLA Ops:
  5.6 1.5 %collective-permute-start = (f32[256,128]{1,0:T(8,128)S(1)}, f32[256,128]{1,0:T(8,128)S(1)}, u32[]{:S(2)}, u32[]{:S(2)}) collective-permute-start(f32[256,128]{1,0:T(8,128)S(1)} %get-tuple-element.17), channel_id=1, source_target_pairs={{0,1},{1,0},{2,3},{3,2},{4,5},{5,4},{6,7},{7,6},{8,9},{9,8},{10,11... | collective-permute-start | bytes 393224 | tf_op jit(solution)/shard_map/ppermute | solution.py:255
  7.1 6.8 %collective-permute-start.1 = (f32[256,128]{1,0:T(8,128)S(1)}, f32[256,128]{1,0:T(8,128)S(1)}, u32[]{:S(2)}, u32[]{:S(2)}) collective-permute-start(f32[256,128]{1,0:T(8,128)S(1)} %add.30), channel_id=1, source_target_pairs={{0,2},{1,3},{2,0},{3,1},{4,6},{5,7},{6,4},{7,5},{8,10},{9,11},{10,... | collective-permute-start | bytes 393224 | tf_op jit(solution)/shard_map/ppermute | solution.py:255
  13.9 6.9 %collective-permute-start.2 = (f32[256,128]{1,0:T(8,128)S(1)}, f32[256,128]{1,0:T(8,128)S(1)}, u32[]{:S(2)}, u32[]{:S(2)}) collective-permute-start(f32[256,128]{1,0:T(8,128)S(1)} %add.31), channel_id=1, source_target_pairs={{0,6},{1,7},{2,4},{3,5},{4,2},{5,3},{6,0},{7,1},{8,14},{9,15},{10,... | collective-permute-start | bytes 393224 | tf_op jit(solution)/shard_map/ppermute | solution.py:255
  20.9 1.4 %collective-permute-start.3 = (f32[256,128]{1,0:T(8,128)S(1)}, f32[256,128]{1,0:T(8,128)S(1)}, u32[]{:S(2)}, u32[]{:S(2)}) collective-permute-start(f32[256,128]{1,0:T(8,128)S(1)} %add.32.own_ref), channel_id=1, source_target_pairs={{0,1},{1,0},{2,3},{3,2},{4,5},{5,4},{6,7},{7,6},{8,9},{9,8},{10,11... | collective-permute-start | bytes 393224 | tf_op jit(solution)/shard_map/ppermute | solution.py:255
  24.6 1.4 %collective-permute-start.4 = (f32[256,128]{1,0:T(8,128)S(1)}, f32[256,128]{1,0:T(8,128)S(1)}, u32[]{:S(2)}, u32[]{:S(2)}) collective-permute-start(f32[256,128]{1,0:T(8,128)S(1)} %get-tuple-element.22), channel_id=1, source_target_pairs={{0,1},{1,0},{2,3},{3,2},{4,5},{5,4},{6,7},{7,6},{8,9},{9,8},{10,11... | collective-permute-start | bytes 393224 | tf_op jit(solution)/shard_map/ppermute | solution.py:255
  26.0 6.2 %collective-permute-start.5 = (f32[256,128]{1,0:T(8,128)S(1)}, f32[256,128]{1,0:T(8,128)S(1)}, u32[]{:S(2)}, u32[]{:S(2)}) collective-permute-start(f32[256,128]{1,0:T(8,128)S(1)} %add.33), channel_id=1, source_target_pairs={{0,2},{1,3},{2,0},{3,1},{4,6},{5,7},{6,4},{7,5},{8,10},{9,11},{10,... | collective-permute-start | bytes 393224 | tf_op jit(solution)/shard_map/ppermute | solution.py:255
  32.3 6.9 %collective-permute-start.6 = (f32[256,128]{1,0:T(8,128)S(1)}, f32[256,128]{1,0:T(8,128)S(1)}, u32[]{:S(2)}, u32[]{:S(2)}) collective-permute-start(f32[256,128]{1,0:T(8,128)S(1)} %add.34), channel_id=1, source_target_pairs={{0,6},{1,7},{2,4},{3,5},{4,2},{5,3},{6,0},{7,1},{8,14},{9,15},{10,... | collective-permute-start | bytes 393224 | tf_op jit(solution)/shard_map/ppermute | solution.py:255
  39.2 1.4 %collective-permute-start.7 = (f32[256,128]{1,0:T(8,128)S(1)}, f32[256,128]{1,0:T(8,128)S(1)}, u32[]{:S(2)}, u32[]{:S(2)}) collective-permute-start(f32[256,128]{1,0:T(8,128)S(1)} %add_add_fusion.own_ref), channel_id=1, source_target_pairs={{0,1},{1,0},{2,3},{3,2},{4,5},{5,4},{6,7},{7,6},{8,9},{9,8},{10,11... | collective-permute-start | bytes 393224 | tf_op jit(solution)/shard_map/ppermute | solution.py:255
  41.2 1.2 %collective-permute-start.8 = (f32[1,128]{1,0:T(1,128)S(1)}, f32[1,128]{1,0:T(1,128)S(1)}, u32[]{:S(2)}, u32[]{:S(2)}) collective-permute-start(f32[1,128]{1,0:T(1,128)S(1)} %get-tuple-element.28), channel_id=1, source_target_pairs={{0,1},{1,0},{2,3},{3,2},{4,5},{5,4},{6,7},{7,6},{8,9},{9,8},{10,11... | collective-permute-start | bytes 1544 | tf_op jit(solution)/shard_map/ppermute | solution.py:255
  42.4 4.0 %collective-permute-start.9 = (f32[1,128]{1,0:T(1,128)S(1)}, f32[1,128]{1,0:T(1,128)S(1)}, u32[]{:S(2)}, u32[]{:S(2)}) collective-permute-start(f32[1,128]{1,0:T(1,128)S(1)} %add.37), channel_id=1, source_target_pairs={{0,2},{1,3},{2,0},{3,1},{4,6},{5,7},{6,4},{7,5},{8,10},{9,11},{10,... | collective-permute-start | bytes 1544 | tf_op jit(solution)/shard_map/ppermute | solution.py:255
  46.4 4.7 %collective-permute-start.10 = (f32[1,128]{1,0:T(1,128)S(1)}, f32[1,128]{1,0:T(1,128)S(1)}, u32[]{:S(2)}, u32[]{:S(2)}) collective-permute-start(f32[1,128]{1,0:T(1,128)S(1)} %add.38), channel_id=1, source_target_pairs={{0,4},{1,5},{2,6},{3,7},{4,0},{5,1},{6,2},{7,3},{8,12},{9,13},{10,... | collective-permute-start | bytes 1544 | tf_op jit(solution)/shard_map/ppermute | solution.py:255
